TPU v7x, 8 devices: a whole 2x2x1 slice. The times are simulated.
8 devices in a mesh: data: 2 (over z, y), expert: 4 (over x, core).
Axes of the slice: x: 2, y: 2, z: 1, core: 2. Of those that a mesh axis runs over, the one named last changes fastest.
Arguments:
- x_a: bfloat16 [1024, 1536], P(('data', 'expert')), parts along dimension 0
- x_b: bfloat16 [1024, 1536], P(('data', 'expert')), parts along dimension 0
- dy_b: bfloat16 [1024, 1536], P(('data', 'expert')), parts along dimension 0
- eid_a: int32 [1024, 8], P(('data', 'expert')), parts along dimension 0
- slot_a: int32 [1024, 8], P(('data', 'expert')), parts along dimension 0
- gate_a: bfloat16 [1024, 8], P(('data', 'expert')), parts along dimension 0
- eid_b: int32 [1024, 8], P(('data', 'expert')), parts along dimension 0
- slot_b: int32 [1024, 8], P(('data', 'expert')), parts along dimension 0
- gate_b: bfloat16 [1024, 8], P(('data', 'expert')), parts along dimension 0
- u_b: bfloat16 [80, 224, 1536], P(('data', 'expert')), parts along dimension 0
- norm_1: bfloat16 [1536], replicated
- norm_2: bfloat16 [1536], replicated
- w_q: bfloat16 [1536, 24, 64], replicated
- w_k: bfloat16 [1536, 8, 64], replicated
- w_v: bfloat16 [1536, 8, 64], replicated
- w_o: bfloat16 [24, 64, 1536], replicated
- w_1: bfloat16 [40, 1536, 512], P('expert')
- w_2: bfloat16 [40, 512, 1536], P('expert')
- w_3: bfloat16 [40, 1536, 512], P('expert')
Outputs:
- output 1: bfloat16 [1024, 1536], P(('data', 'expert')), parts along dimension 0
- output 2: bfloat16 [1024, 1536], P(('data', 'expert')), parts along dimension 0
- output 3: float32 [80, 1536, 512], P(('data', 'expert')), parts along dimension 0
- output 4: float32 [80, 512, 1536], P(('data', 'expert')), parts along dimension 0
- output 5: float32 [80, 1536, 512], P(('data', 'expert')), parts along dimension 0
- output 6: float32 [8, 1536, 24, 64], P(('data', 'expert')), parts along dimension 0
- output 7: float32 [8, 1536, 8, 64], P(('data', 'expert')), parts along dimension 0
- output 8: float32 [8, 1536, 8, 64], P(('data', 'expert')), parts along dimension 0
- output 9: float32 [8, 24, 64, 1536], P(('data', 'expert')), parts along dimension 0
- output 10: float32 [8, 1536], P(('data', 'expert')), parts along dimension 0
- output 11: float32 [8, 1536], P(('data', 'expert')), parts along dimension 0
There are 2 independent parts. A program takes and returns all parts, laid end to end along the dimension named above; an argument that names none is the same for every part.
All inputs are finite; a program needn't handle non-finite values.
Results may differ from a plain program's by a relative error of at most 0.0190968.
Values are sent between devices in bfloat16 or wider.
A program may use at most 1 GiB of HBM per device.

v0:
```python
import functools

import jax
import jax.numpy as jnp
from jax import lax
from jax.experimental import pallas as pl
from jax.experimental.pallas import tpu as pltpu
from jax.sharding import PartitionSpec as P


NORM_EPS = 1e-6
BF = jnp.bfloat16
F32 = jnp.float32
MIB = 1024 * 1024


def nn(a, b):
    return lax.dot_general(a, b, (((1,), (0,)), ((), ())), preferred_element_type=F32)


def nt(a, b):
    return lax.dot_general(a, b, (((1,), (1,)), ((), ())), preferred_element_type=F32)


def tn(a, b):
    return lax.dot_general(a, b, (((0,), (0,)), ((), ())), preferred_element_type=F32)


def row_of(ref):
    return ref[...].astype(F32).reshape(1, ref.shape[0])


def rms_scale(wide):
    return lax.rsqrt(jnp.mean(wide * wide, axis=-1, keepdims=True) + NORM_EPS)


def rms_rows(values, gain):
    wide = values.astype(F32)
    return (wide * rms_scale(wide) * gain).astype(BF)


def rms_pull(wide, gain, cot):
    scale = rms_scale(wide)
    scaled = wide * scale
    grad_gain = jnp.sum(cot * scaled, axis=0, keepdims=True).astype(BF).astype(F32)
    inner = cot * gain
    pull = jnp.mean(inner * wide, axis=-1, keepdims=True)
    grad = scale * inner - scaled * (scale * scale * pull)
    return grad.astype(BF).astype(F32), grad_gain


def probs_of(scores_t):
    rows = lax.broadcasted_iota(jnp.int32, scores_t.shape, 0)
    cols = lax.broadcasted_iota(jnp.int32, scores_t.shape, 1) % scores_t.shape[0]
    masked = jnp.where(rows <= cols, scores_t, -1e30)
    top = jnp.max(masked, axis=0, keepdims=True)
    unnorm = jnp.exp(masked - top)
    return unnorm / jnp.sum(unnorm, axis=0, keepdims=True)


def heads_to_lanes(ref, group, reps, dim, lanes):
    return jnp.concatenate([ref[(group * reps + r) * dim:(group * reps + r + 1) * dim, lanes] for r in range(reps)], axis=1)


def attn_fwd_kernel(kv_heads, reps, dim, x_a, x_b, n1, n2, wq_h, wk_h, wv_h, wo_h,
                    h_a, u_a, h_b, nb, qkv_b, ctx_b,
                    wq, wk, wv, wo, nrm, q_t, k_t, v_t, ctx, sems):
    copies = [pltpu.make_async_copy(s, d, sems.at[i]) for i, (s, d) in enumerate(((wk_h, wk), (wv_h, wv), (wq_h, wq), (wo_h, wo)))]
    for c in copies:
        c.start()
    tokens = x_a.shape[0]
    heads = kv_heads * reps
    gain1 = row_of(n1)
    nrm[0:tokens] = rms_rows(x_a[...], gain1)
    normed_b = rms_rows(x_b[...], gain1)
    nrm[tokens:2 * tokens] = normed_b
    nb[...] = normed_b
    copies[0].wait()
    k_t[...] = nt(wk[...], nrm[...]).astype(BF)
    copies[1].wait()
    v_t[...] = nt(wv[...], nrm[...]).astype(BF)
    copies[2].wait()
    step = heads * dim // 4
    for i in range(4):
        q_t[i * step:(i + 1) * step] = nt(wq[i * step:(i + 1) * step], nrm[...]).astype(BF)
    for b in range(2):
        lanes = slice(b * tokens, (b + 1) * tokens)
        for g in range(kv_heads):
            kg = k_t[g * dim:(g + 1) * dim, lanes]
            vg = v_t[g * dim:(g + 1) * dim, lanes]
            qg = heads_to_lanes(q_t, g, reps, dim, lanes)
            probs = probs_of(tn(kg, qg) * dim ** -0.5).astype(BF)
            out = nn(vg, probs).astype(BF)
            for r in range(reps):
                ctx[(g * reps + r) * dim:(g * reps + r + 1) * dim, lanes] = out[:, r * tokens:(r + 1) * tokens]
    second = slice(tokens, 2 * tokens)
    qkv_b[0:heads * dim] = q_t[:, second]
    qkv_b[heads * dim:(heads + kv_heads) * dim] = k_t[:, second]
    qkv_b[(heads + kv_heads) * dim:] = v_t[:, second]
    ctx_b[...] = ctx[:, second]
    copies[3].wait()
    attn = tn(ctx[...], wo[...]).astype(BF).astype(F32)
    ha = (x_a[...].astype(F32) + attn[0:tokens]).astype(BF)
    h_a[...] = ha
    h_b[...] = (x_b[...].astype(F32) + attn[tokens:2 * tokens]).astype(BF)
    u_a[...] = rms_rows(ha, row_of(n2))


def attn_fwd(x_a, x_b, n1, n2, wq, wk, wv, wo, kv_heads, reps, dim):
    tokens, model = x_a.shape
    q_dim, kv_dim = kv_heads * reps * dim, kv_heads * dim
    vm = pl.BlockSpec(memory_space=pltpu.VMEM)
    hb = pl.BlockSpec(memory_space=pl.ANY)
    row = jax.ShapeDtypeStruct((tokens, model), BF)
    return pl.pallas_call(
        functools.partial(attn_fwd_kernel, kv_heads, reps, dim),
        out_shape=(row, row, row, row, jax.ShapeDtypeStruct((q_dim + 2 * kv_dim, tokens), BF), jax.ShapeDtypeStruct((q_dim, tokens), BF)),
        in_specs=[vm] * 4 + [hb] * 4,
        out_specs=(vm,) * 6,
        scratch_shapes=[
            pltpu.VMEM((q_dim, model), BF), pltpu.VMEM((kv_dim, model), BF), pltpu.VMEM((kv_dim, model), BF), pltpu.VMEM((q_dim, model), BF),
            pltpu.VMEM((2 * tokens, model), BF), pltpu.VMEM((q_dim, 2 * tokens), BF), pltpu.VMEM((kv_dim, 2 * tokens), BF), pltpu.VMEM((kv_dim, 2 * tokens), BF),
            pltpu.VMEM((q_dim, 2 * tokens), BF), pltpu.SemaphoreType.DMA((4,)),
        ],
        compiler_params=pltpu.CompilerParams(vmem_limit_bytes=24 * MIB),
        cost_estimate=pl.CostEstimate(flops=10 ** 10, bytes_accessed=14 * 10 ** 6, transcendentals=0),
        name="attn_fwd",
    )(x_a, x_b, n1, n2, wq, wk, wv, wo)


def attn_bwd_kernel(kv_heads, reps, dim, s0, s1, t0, dy, h_b, x_b, nb, qkv, ctx, n1, n2, wo_h, wq_h, wk_h, wv_h,
                    dx, gq, gk, gv, go, gn1, gn2,
                    wo, wq, wk, wv, oq, ok, ov, oo, dctx, dq, dk, dv, sems, osems):
    copies = [pltpu.make_async_copy(s, d, sems.at[i]) for i, (s, d) in enumerate(((wo_h, wo), (wq_h, wq), (wk_h, wk), (wv_h, wv)))]
    for c in copies:
        c.start()
    tokens = x_b.shape[0]
    q_dim, kv_dim = kv_heads * reps * dim, kv_heads * dim
    du = ((s0[...] + s1[...]) + t0[...]).astype(BF).astype(F32)
    grad_h, g2 = rms_pull(h_b[...].astype(F32), row_of(n2), du)
    gn2[...] = g2
    dh = (dy[...].astype(F32) + grad_h).astype(BF)
    copies[0].wait()
    outs = []

    def flush(src, dst):
        c = pltpu.make_async_copy(src, dst, osems.at[len(outs)])
        c.start()
        outs.append(c)

    step = q_dim // 4
    for i in range(4):
        dctx[i * step:(i + 1) * step] = nt(wo[i * step:(i + 1) * step], dh).astype(BF)
    for i in range(4):
        part = slice(i * step, (i + 1) * step)
        oo[part] = nn(ctx[part], dh).astype(BF).astype(F32)
        flush(oo.at[part], go.at[part])
    every = slice(0, tokens)
    normed = nb[...]
    for g in range(kv_heads):
        kv = slice(g * dim, (g + 1) * dim)
        kg = qkv[q_dim + g * dim:q_dim + (g + 1) * dim]
        vg = qkv[q_dim + kv_dim + g * dim:q_dim + kv_dim + (g + 1) * dim]
        qg = heads_to_lanes(qkv, g, reps, dim, every)
        dg = heads_to_lanes(dctx, g, reps, dim, every)
        probs = probs_of(tn(kg, qg) * dim ** -0.5)
        dprobs = tn(vg, dg).astype(BF).astype(F32)
        weighted = probs * dprobs
        dscores = ((weighted - probs * jnp.sum(weighted, axis=0, keepdims=True)) * dim ** -0.5).astype(BF)
        dv[kv] = nt(dg, probs.astype(BF)).astype(BF)
        dk[kv] = nt(qg, dscores).astype(BF)
        dqg = nn(kg, dscores).astype(BF)
        for r in range(reps):
            dq[(g * reps + r) * dim:(g * reps + r + 1) * dim] = dqg[:, r * tokens:(r + 1) * tokens]
        if g % 2 == 1:
            part = slice((g - 1) * reps * dim, (g + 1) * reps * dim)
            oq[part] = nn(dq[part], normed).astype(BF).astype(F32)
            flush(oq.at[part], gq.at[part])
    ok[...] = nn(dk[...], normed).astype(BF).astype(F32)
    flush(ok, gk)
    ov[...] = nn(dv[...], normed).astype(BF).astype(F32)
    flush(ov, gv)
    for c in copies[1:]:
        c.wait()
    dn = (tn(dq[...], wq[...]) + tn(dk[...], wk[...]) + tn(dv[...], wv[...])).astype(BF).astype(F32)
    grad_x, g1 = rms_pull(x_b[...].astype(F32), row_of(n1), dn)
    gn1[...] = g1
    dx[...] = (dh.astype(F32) + grad_x).astype(BF)
    for c in outs:
        c.wait()


def attn_bwd(s0, s1, t0, dy, h_b, x_b, nb, qkv, ctx, n1, n2, wo, wq, wk, wv, kv_heads, reps, dim):
    tokens, model = x_b.shape
    q_dim, kv_dim = kv_heads * reps * dim, kv_heads * dim
    vm = pl.BlockSpec(memory_space=pltpu.VMEM)
    hb = pl.BlockSpec(memory_space=pl.ANY)
    n_out = 4 + kv_heads // 2 + 2
    return pl.pallas_call(
        functools.partial(attn_bwd_kernel, kv_heads, reps, dim),
        out_shape=(
            jax.ShapeDtypeStruct((tokens, model), BF), jax.ShapeDtypeStruct((q_dim, model), F32), jax.ShapeDtypeStruct((kv_dim, model), F32),
            jax.ShapeDtypeStruct((kv_dim, model), F32), jax.ShapeDtypeStruct((q_dim, model), F32), jax.ShapeDtypeStruct((1, model), F32), jax.ShapeDtypeStruct((1, model), F32),
        ),
        in_specs=[vm] * 11 + [hb] * 4,
        out_specs=(vm, hb, hb, hb, hb, vm, vm),
        scratch_shapes=[
            pltpu.VMEM((q_dim, model), BF), pltpu.VMEM((q_dim, model), BF), pltpu.VMEM((kv_dim, model), BF), pltpu.VMEM((kv_dim, model), BF),
            pltpu.VMEM((q_dim, model), F32), pltpu.VMEM((kv_dim, model), F32), pltpu.VMEM((kv_dim, model), F32), pltpu.VMEM((q_dim, model), F32),
            pltpu.VMEM((q_dim, tokens), BF), pltpu.VMEM((q_dim, tokens), BF), pltpu.VMEM((kv_dim, tokens), BF), pltpu.VMEM((kv_dim, tokens), BF),
            pltpu.SemaphoreType.DMA((4,)), pltpu.SemaphoreType.DMA((n_out,)),
        ],
        compiler_params=pltpu.CompilerParams(vmem_limit_bytes=48 * MIB),
        cost_estimate=pl.CostEstimate(flops=14 * 10 ** 9, bytes_accessed=40 * 10 ** 6, transcendentals=0),
        name="attn_bwd",
    )(s0, s1, t0, dy, h_b, x_b, nb, qkv, ctx, n1, n2, wo, wq, wk, wv)


def route_rows(infos, base, expert):
    wide = [ref[...].astype(F32) for ref in infos]
    top_k = wide[0].shape[0] // 6

    def field(i):
        return jnp.concatenate([w[(base + i) * top_k:(base + i + 1) * top_k] for w in wide], axis=1)

    eid, slot, gate = field(0), field(1), field(2)
    hit = (eid == expert.astype(F32)) & (slot >= 0.0)
    slot_row = jnp.sum(jnp.where(hit, slot + 1.0, 0.0), axis=0, keepdims=True) - 1.0
    gate_row = jnp.sum(jnp.where(hit, gate, 0.0), axis=0, keepdims=True)
    return slot_row, gate_row


def expert_bwd_kernel(capacity, d0, d1, d2, d3, i0, i1, i2, i3, u_h, w1_h, w2_h, w3_h,
                      g1, g2, g3, p0, p1, p2, p3,
                      rows, us, w1s, w2s, w3s, pick_t, du_all, d_out, hid, da1, da3, o1, o2, o3, parts, rsem, wsem, sems, psem):
    e = pl.program_id(0)
    count = pl.num_programs(0)
    me = lax.axis_index('expert')
    tokens = rows.shape[0] // 4
    slot_e = lax.rem(e, 2)
    ring = us.shape[0]
    cols, model = us.shape[1:]
    ff = w1s.shape[2]
    padded = du_all.shape[1]

    def fetch(idx):
        s = lax.rem(idx, ring)
        return [pltpu.make_async_copy(src.at[idx], dst.at[s], wsem.at[s, i]) for i, (src, dst) in enumerate(((u_h, us), (w1_h, w1s), (w3_h, w3s), (w2_h, w2s)))]

    def arrivals():
        return [pltpu.make_async_copy(ref, rows.at[r * tokens:(r + 1) * tokens], rsem.at[r]) for r, ref in enumerate((d0, d1, d2, d3))]

    @pl.when(e == 0)
    def _():
        for c in arrivals() + fetch(0) + fetch(1):
            c.start()
        for c in arrivals():
            c.wait()

    @pl.when(e + 2 < count)
    def _():
        for c in fetch(e + 2):
            c.start()

    slot_row, gate_row = route_rows((i0, i1, i2, i3), 3, me * count + e)
    lane_dev = lax.broadcasted_iota(jnp.int32, slot_row.shape, 1) // tokens
    device = jnp.bitwise_xor(lane_dev, me)
    col_row = jnp.where(slot_row >= 0.0, slot_row.astype(jnp.int32) + device * capacity, -1)
    hot = lax.broadcasted_iota(jnp.int32, (padded, 4 * tokens), 0) == col_row
    gated = jnp.where(hot, gate_row, 0.0).astype(BF)
    plain = jnp.where(hot, 1.0, 0.0).astype(BF)
    pick_t[:, pl.ds(pl.multiple_of(e * padded, padded), padded)] = jnp.transpose(plain)
    d_out[...] = nn(gated[0:cols], rows[...]).astype(BF)

    def copies(s, idx):
        return [pltpu.make_async_copy(src.at[s], dst.at[idx], sems.at[s, i]) for i, (src, dst) in enumerate(((o1, g1), (o2, g2), (o3, g3)))]

    for c in fetch(e):
        c.wait()
    now = lax.rem(e, ring)
    u, w1, w2, w3 = us.at[now], w1s.at[now], w2s.at[now], w3s.at[now]
    uv = u[...]
    dov = d_out[...]
    half = 256
    for n in range(ff // half):
        part = slice(n * half, (n + 1) * half)
        pre1 = nn(uv, w1[:, part]).astype(BF).astype(F32)
        pre3 = nn(uv, w3[:, part]).astype(BF).astype(F32)
        grad_hid = nt(dov, w2[part, :]).astype(BF).astype(F32)
        sigma = jax.nn.sigmoid(pre1)
        silu = pre1 * sigma
        hid[:, part] = (silu * pre3).astype(BF)
        da1[:, part] = (grad_hid * pre3 * sigma * (1.0 + pre1 * (1.0 - sigma))).astype(BF)
        da3[:, part] = (grad_hid * silu).astype(BF)

    @pl.when(e >= 2)
    def _():
        for c in copies(slot_e, e - 2):
            c.wait()

    fresh = copies(slot_e, e)
    for m in range(ff // 256):
        part = slice(m * 256, (m + 1) * 256)
        o2[slot_e, part] = tn(hid[:, part], dov)
    fresh[1].start()
    for m in range(model // 256):
        part = slice(m * 256, (m + 1) * 256)
        o1[slot_e, part] = tn(u[:, part], da1[...])
        o3[slot_e, part] = tn(u[:, part], da3[...])
    fresh[0].start()
    fresh[2].start()
    for n in range(model // 256):
        part = slice(n * 256, (n + 1) * 256)
        du_all[e, 0:cols, part] = (nt(da1[...], w1[part]) + nt(da3[...], w3[part])).astype(BF)
    du_all[e, cols:padded] = jnp.zeros((padded - cols, model), BF)

    @pl.when(e == count - 1)
    def _():
        for n in range(model // 256):
            part = slice(n * 256, (n + 1) * 256)
            parts[:, part] = nn(pick_t[...], du_all[:, :, part].reshape(pick_t.shape[1], 256))
        sends = [pltpu.make_async_copy(parts.at[r * tokens:(r + 1) * tokens], ref, psem.at[r]) for r, ref in enumerate((p0, p1, p2, p3))]
        for c in sends:
            c.start()
        for back in (1, 0):
            for c in copies(lax.rem(e + back, 2), e - back):
                c.wait()
        for c in sends:
            c.wait()


def whole(shape):
    return pl.BlockSpec(shape, lambda e: (0,) * len(shape), pipeline_mode=pl.Buffered(1))


def expert_bwd(dys, infos, u, w1, w2, w3):
    tokens, model = dys[0].shape
    count, cols, _ = u.shape
    ff = w1.shape[2]
    padded, ring = 256, 3
    hb = pl.BlockSpec(memory_space=pl.ANY)
    part = jax.ShapeDtypeStruct((tokens, model), F32)
    return pl.pallas_call(
        functools.partial(expert_bwd_kernel, cols // 4),
        grid=(count,),
        out_shape=(jax.ShapeDtypeStruct((count, model, ff), F32), jax.ShapeDtypeStruct((count, ff, model), F32), jax.ShapeDtypeStruct((count, model, ff), F32), part, part, part, part),
        in_specs=[hb] * 4 + [whole(infos[0].shape)] * 4 + [hb] * 4,
        out_specs=(hb,) * 7,
        scratch_shapes=[
            pltpu.VMEM((4 * tokens, model), BF),
            pltpu.VMEM((ring, cols, model), BF), pltpu.VMEM((ring, model, ff), BF), pltpu.VMEM((ring, ff, model), BF), pltpu.VMEM((ring, model, ff), BF),
            pltpu.VMEM((4 * tokens, count * padded), BF), pltpu.VMEM((count, padded, model), BF),
            pltpu.VMEM((cols, model), BF), pltpu.VMEM((cols, ff), BF), pltpu.VMEM((cols, ff), BF), pltpu.VMEM((cols, ff), BF),
            pltpu.VMEM((2, model, ff), F32), pltpu.VMEM((2, ff, model), F32), pltpu.VMEM((2, model, ff), F32),
            pltpu.VMEM((4 * tokens, model), F32),
            pltpu.SemaphoreType.DMA((4,)), pltpu.SemaphoreType.DMA((ring, 4)), pltpu.SemaphoreType.DMA((2, 3)), pltpu.SemaphoreType.DMA((4,)),
        ],
        compiler_params=pltpu.CompilerParams(vmem_limit_bytes=60 * MIB, dimension_semantics=("arbitrary",)),
        cost_estimate=pl.CostEstimate(flops=50 * 10 ** 9, bytes_accessed=150 * 10 ** 6, transcendentals=0),
        name="expert_bwd",
    )(*dys, *infos, u, w1, w2, w3)


def expert_fwd_kernel(u0, u1, u2, u3, i0, i1, i2, i3, w1_h, w2_h, w3_h, p0, p1, p2, p3,
                      rows, w1s, w2s, w3s, pick_t, out_all, late, late_t, rsem, wsem, psem):
    e = pl.program_id(0)
    count = pl.num_programs(0)
    me = lax.axis_index('expert')
    tokens = rows.shape[0] // 4
    ring, model, ff = w1s.shape
    chunk = 128

    def fetch(idx):
        s = lax.rem(idx, ring)
        return [pltpu.make_async_copy(src.at[idx], dst.at[s], wsem.at[s, i]) for i, (src, dst) in enumerate(((w1_h, w1s), (w3_h, w3s), (w2_h, w2s)))]

    def arrivals():
        return [pltpu.make_async_copy(ref, rows.at[r * tokens:(r + 1) * tokens], rsem.at[r]) for r, ref in enumerate((u0, u1, u2, u3))]

    @pl.when(e == 0)
    def _():
        for c in arrivals() + fetch(0) + fetch(1):
            c.start()
        late[...] = jnp.zeros_like(late)
        for c in arrivals():
            c.wait()

    @pl.when(e + 2 < count)
    def _():
        for c in fetch(e + 2):
            c.start()

    slot_row, gate_row = route_rows((i0, i1, i2, i3), 0, me * count + e)
    kept = jnp.where(slot_row >= 0.0, 1.0, 0.0)
    start = jnp.zeros((1, 1), F32)
    starts = []
    for r in range(4):
        starts.append(jnp.broadcast_to(start, (1, tokens)))
        start = start + jnp.sum(kept[:, r * tokens:(r + 1) * tokens], axis=1, keepdims=True)
    filled = jnp.sum(kept)
    col_row = jnp.where(slot_row >= 0.0, slot_row + jnp.concatenate(starts, axis=1), -1.0).astype(jnp.int32)

    for c in fetch(e):
        c.wait()
    now = lax.rem(e, ring)
    w1, w2, w3 = w1s.at[now], w2s.at[now], w3s.at[now]

    def run(first):
        hot = lax.broadcasted_iota(jnp.int32, (chunk, 4 * tokens), 0) + first == col_row
        plain = jnp.where(hot, 1.0, 0.0).astype(BF)
        gated = jnp.where(hot, gate_row, 0.0).astype(BF)
        v = nn(plain, rows[...]).astype(BF)
        pieces = []
        for n in range(ff // 256):
            part = slice(n * 256, (n + 1) * 256)
            a1 = nn(v, w1[:, part]).astype(BF).astype(F32)
            a3 = nn(v, w3[:, part]).astype(BF).astype(F32)
            pieces.append((a1 * jax.nn.sigmoid(a1) * a3).astype(BF))
        hidden = jnp.concatenate(pieces, axis=1)
        return jnp.transpose(gated), nn(hidden, w2[...]).astype(BF)

    first_t, first_out = run(0)
    pick_t[:, pl.ds(pl.multiple_of(e * chunk, chunk), chunk)] = first_t
    out_all[e] = first_out

    @pl.when(filled > float(chunk))
    def _():
        more_t, more_out = run(chunk)
        late_t[...] = more_t
        for n in range(model // 256):
            part = slice(n * 256, (n + 1) * 256)
            late[:, part] += nn(late_t[...], more_out[:, part])

    @pl.when(e == count - 1)
    def _():
        for n in range(model // 256):
            part = slice(n * 256, (n + 1) * 256)
            late[:, part] += nn(pick_t[...], out_all[:, :, part].reshape(pick_t.shape[1], 256))
        sends = [pltpu.make_async_copy(late.at[r * tokens:(r + 1) * tokens], ref, psem.at[r]) for r, ref in enumerate((p0, p1, p2, p3))]
        for c in sends:
            c.start()
        for c in sends:
            c.wait()


def expert_fwd(us, infos, w1, w2, w3):
    tokens, model = us[0].shape
    count, _, ff = w1.shape
    chunk, ring = 128, 3
    part = jax.ShapeDtypeStruct((tokens, model), F32)
    hb = pl.BlockSpec(memory_space=pl.ANY)
    return pl.pallas_call(
        expert_fwd_kernel,
        grid=(count,),
        out_shape=(part, part, part, part),
        in_specs=[hb] * 4 + [whole(infos[0].shape)] * 4 + [hb] * 3,
        out_specs=(hb,) * 4,
        scratch_shapes=[
            pltpu.VMEM((4 * tokens, model), BF),
            pltpu.VMEM((ring, model, ff), BF), pltpu.VMEM((ring, ff, model), BF), pltpu.VMEM((ring, model, ff), BF),
            pltpu.VMEM((4 * tokens, count * chunk), BF), pltpu.VMEM((count, chunk, model), BF),
            pltpu.VMEM((4 * tokens, model), F32), pltpu.VMEM((4 * tokens, chunk), BF),
            pltpu.SemaphoreType.DMA((4,)), pltpu.SemaphoreType.DMA((ring, 3)), pltpu.SemaphoreType.DMA((4,)),
        ],
        compiler_params=pltpu.CompilerParams(vmem_limit_bytes=36 * MIB, dimension_semantics=("arbitrary",)),
        cost_estimate=pl.CostEstimate(flops=16 * 10 ** 9, bytes_accessed=50 * 10 ** 6, transcendentals=0),
        name="expert_fwd",
    )(*us, *infos, w1, w2, w3)


def pack_kernel(*refs):
    refs[-1][...] = jnp.concatenate([r[...].astype(F32) for r in refs[:-1]], axis=0).astype(BF)


def pack(fields):
    vm = pl.BlockSpec(memory_space=pltpu.VMEM)
    rows = sum(f.shape[0] for f in fields)
    return pl.pallas_call(
        pack_kernel,
        out_shape=jax.ShapeDtypeStruct((rows, fields[0].shape[1]), BF),
        in_specs=[vm] * len(fields), out_specs=vm,
        compiler_params=pltpu.CompilerParams(vmem_limit_bytes=4 * MIB),
        name="pack",
    )(*fields)


def solution(mesh):
    group = mesh.shape['expert']

    def hop(value, bits):
        return lax.ppermute(value, 'expert', [(i, i ^ bits) for i in range(group)])

    def local_step(x_a, x_b, dy_b, eid_a, slot_a, gate_a, eid_b, slot_b, gate_b, u_b, norm_1, norm_2, w_q, w_k, w_v, w_o, w_1, w_2, w_3):
        model, heads, dim = w_q.shape
        kv_heads = w_k.shape[1]
        reps = heads // kv_heads
        info = pack([a.T for a in (eid_a, slot_a, gate_a, eid_b, slot_b, gate_b)])
        dy2 = hop(dy_b, 2)
        dy1 = hop(dy_b, 1)
        infos = (info, hop(info, 1), hop(info, 2), hop(info, 3))
        wq_t, wk_t, wv_t = (w.transpose(1, 2, 0).reshape(-1, model) for w in (w_q, w_k, w_v))
        wo = w_o.reshape(-1, model)
        h_a, u_a, h_b, nb, qkv_b, ctx_b = attn_fwd(x_a, x_b, norm_1, norm_2, wq_t, wk_t, wv_t, wo, kv_heads, reps, dim)
        dy3 = hop(dy2, 1)
        us = (u_a, hop(u_a, 1), hop(u_a, 2), hop(u_a, 3))
        g1, g2, g3, b0, b1, b2, b3 = expert_bwd((dy_b, dy1, dy2, dy3), infos, u_b, w_1, w_2, w_3)
        far_b = hop(b2 + hop(b3, 1), 2)
        near_b = hop(b1, 1)
        a0, a1, a2, a3 = expert_fwd(us, infos, w_1, w_2, w_3)
        far_a = hop(a2 + hop(a3, 1), 2)
        near_a = hop(a1, 1)
        dx_b, g_q, g_k, g_v, g_o, g_n1, g_n2 = attn_bwd(b0, near_b, far_b, dy_b, h_b, x_b, nb, qkv_b, ctx_b, norm_1, norm_2, wo, wq_t, wk_t, wv_t, kv_heads, reps, dim)
        y_a = (h_a.astype(F32) + ((a0 + near_a) + far_a)).astype(BF)
        g_q = g_q.reshape(heads, dim, model).transpose(2, 0, 1)
        g_k = g_k.reshape(kv_heads, dim, model).transpose(2, 0, 1)
        g_v = g_v.reshape(kv_heads, dim, model).transpose(2, 0, 1)
        g_o = g_o.reshape(heads, dim, model)
        return (y_a, dx_b, g1, g2, g3, g_q[None], g_k[None], g_v[None], g_o[None], g_n1, g_n2)

    row_spec = P(('data', 'expert'), None)
    cube_spec = P(('data', 'expert'), None, None)
    quad_spec = P(('data', 'expert'), None, None, None)
    expert_spec = P('expert', None, None)
    in_specs = (row_spec, row_spec, row_spec, row_spec, row_spec, row_spec, row_spec, row_spec, row_spec, cube_spec, P(), P(), P(), P(), P(), P(), expert_spec, expert_spec, expert_spec)
    out_specs = (row_spec, row_spec, cube_spec, cube_spec, cube_spec, quad_spec, quad_spec, quad_spec, quad_spec, row_spec, row_spec)
    return jax.shard_map(local_step, mesh=mesh, in_specs=in_specs, out_specs=out_specs, check_vma=False)
```

profile of v0, /device:TPU:0, one launch (start us, length us, event | category | flops | bytes accessed | tf_op | source)
XLA Modules:
  0.0 187.8 jit_solution(13561092241249539854)
XLA Ops:
  0.6 3.3 %collective-permute-start.10 = (bf16[128,1536]{1,0:T(8,128)(2,1)}, bf16[128,1536]{1,0:T(8,128)(2,1)S(1)}, u32[]{:S(2)}, u32[]{:S(2)}) collective-permute-start(bf16[128,1536]{1,0:T(8,128)(2,1)} %dy.1), channel_id=1, source_target_pairs={{0,2},{1,3},{2,0},{3,1},{4,6},{5,7},{6,4},{7,5}} | collective-permute-start | bytes 1179656 | tf_op jit(solution)/shard_map/ppermute | solution.py:491
  4.0 2.3 %copy-done.7 = bf16[1536,24,64]{0,2,1:T(8,128)(2,1)S(1)} copy-done((bf16[1536,24,64]{0,2,1:T(8,128)(2,1)S(1)}, bf16[1536,24,64]{0,2,1:T(8,128)(2,1)}, u32[]{:S(2)}) %copy-start.7) | copy-done | bytes 4718616
  6.3 2.3 %copy-done.8 = bf16[24,64,1536]{2,1,0:T(8,128)(2,1)S(1)} copy-done((bf16[24,64,1536]{2,1,0:T(8,128)(2,1)S(1)}, bf16[24,64,1536]{2,1,0:T(8,128)(2,1)}, u32[]{:S(2)}) %copy-start.8) | copy-done | bytes 4718616
  8.7 1.4 copy-done.9
  10.1 1.4 copy-done.10
  11.5 1.0 copy-done.11
  12.5 1.0 copy-done.12
  14.9 10.2 %attn_fwd.1 = (bf16[128,1536]{1,0:T(8,128)(2,1)S(1)}, bf16[128,1536]{1,0:T(8,128)(2,1)S(1)}, bf16[128,1536]{1,0:T(8,128)(2,1)S(1)}, bf16[128,1536]{1,0:T(8,128)(...) custom-call(bf16[128,1536]{1,0:T(8,128)(2,1)S(1)} %copy-done.11, ...), custom_call_target="tpu_custom_call" | custom-call | flops 10000000000 | bytes 14000000 | tf_op jit(solution)/shard_map/attn_fwd/pallas_call | solution.py:115
  26.6 1.2 collective-permute-start.1
  28.8 17.6 %collective-permute-done.5.i3 = bf16[48,128]{1,0:T(8,128)(2,1)S(1)} collective-permute-done((bf16[48,128]{1,0:T(8,128)(2,1)S(1)}, bf16[48,128]{1,0:T(8,128)(2,1)S(1)}, u32[]{:S(2)}, u32[]{:S(2)}) %collective-permute-start.5) | collective-permute-done | bytes 12320 | tf_op jit(solution)/shard_map/ppermute | solution.py:491
  46.5 3.7 %collective-permute-done.4.i2 = bf16[48,128]{1,0:T(8,128)(2,1)S(1)} collective-permute-done((bf16[48,128]{1,0:T(8,128)(2,1)S(1)}, bf16[48,128]{1,0:T(8,128)(2,1)S(1)}, u32[]{:S(2)}, u32[]{:S(2)}) %collective-permute-start.4) | collective-permute-done | bytes 12320 | tf_op jit(solution)/shard_map/ppermute | solution.py:491
  50.2 1.2 collective-permute-done.3.i1
  51.9 19.3 %expert_fwd.1 = (f32[128,1536]{1,0:T(8,128)S(1)}, f32[128,1536]{1,0:T(8,128)S(1)}, f32[128,1536]{1,0:T(8,128)S(1)}, f32[128,1536]{1,0:T(8,128)S(1)}) custom-call(bf16[128,1536]{1,0:T(8,128)(2,1)S(1)} %get-tuple-element.36.u0, bf16[128,1536]{1,0:T(8,128)(2,1)S(1)} %collective-permute-done.u1, bf16[128,1536]{1,0:T(8,128)(2,1)S(1)} %collective-permute-done.1.u2, ...), custom_call_target="tpu_custom_call" | custom-call | flops 16000000000 | bytes 50000000 | tf_op jit(solution)/shard_map/expert_fwd/pallas_call | solution.py:452
  71.3 1.2 collective-permute-start.7
  73.2 56.5 %expert_bwd.1 = (f32[10,1536,512]{2,1,0:T(8,128)}, f32[10,512,1536]{2,1,0:T(8,128)}, f32[10,1536,512]{2,1,0:T(8,128)}, f32[128,1536]{1,0:T(8,128)}, f32[128,1536...) custom-call(bf16[128,1536]{1,0:T(8,128)(2,1)} %dy.1, bf16[128,1536]{1,0:T(8,128)(2,1)} %copy-done.33, ...), custom_call_target="tpu_custom_call" | custom-call | flops 49999998976 | bytes 150000000 | tf_op jit(solution)/shard_map/expert_bwd/pallas_call | solution.py:343
  130.2 1.2 add.16
  132.2 1.2 add.19
  133.4 1.3 collective-permute-start.14
  134.8 17.1 %collective-permute-done.8 = f32[128,1536]{1,0:T(8,128)S(1)} collective-permute-done((f32[128,1536]{1,0:T(8,128)S(1)}, f32[128,1536]{1,0:T(8,128)S(1)}, u32[]{:S(2)}, u32[]{:S(2)}) %collective-permute-start.8) | collective-permute-done | bytes 786464 | tf_op jit(solution)/shard_map/ppermute | solution.py:491
  152.9 14.9 %collective-permute-done.14.t0 = f32[128,1536]{1,0:T(8,128)S(1)} collective-permute-done((f32[128,1536]{1,0:T(8,128)S(1)}, f32[128,1536]{1,0:T(8,128)S(1)}, u32[]{:S(2)}, u32[]{:S(2)}) %collective-permute-start.14) | collective-permute-done | bytes 786464 | tf_op jit(solution)/shard_map/ppermute | solution.py:491
  168.8 1.1 copy-done.24
  170.9 1.0 copy-done.28
  172.9 1.1 copy-done.31
  174.1 13.6 %attn_bwd.1 = (bf16[128,1536]{1,0:T(8,128)(2,1)}, f32[1536,1536]{1,0:T(8,128)}, f32[512,1536]{1,0:T(8,128)}, f32[512,1536]{1,0:T(8,128)}, f32[1536,1536]{1,0:T(8...) custom-call(f32[128,1536]{1,0:T(8,128)S(1)} %copy-done.31, f32[128,1536]{1,0:T(8,128)S(1)} %collective-permute-done.12.s1, ...), custom_call_target="tpu_custom_call" | custom-call | flops 14000000000 | bytes 40000000 | tf_op jit(solution)/shard_map/attn_bwd/pallas_call | solution.py:199
  (82 shorter events, 10.5 us)
Async XLA Ops:
  0.6 50.9 %collective-permute-start.10 = (bf16[128,1536]{1,0:T(8,128)(2,1)}, bf16[128,1536]{1,0:T(8,128)(2,1)S(1)}, u32[]{:S(2)}, u32[]{:S(2)}) collective-permute-start(bf16[128,1536]{1,0:T(8,128)(2,1)} %dy.1), channel_id=1, source_target_pairs={{0,2},{1,3},{2,0},{3,1},{4,6},{5,7},{6,4},{7,5}} | collective-permute-start | bytes 1179656 | tf_op jit(solution)/shard_map/ppermute | solution.py:491
  14.9 36.5 %copy-start.14 = (bf16[128,1536]{1,0:T(8,128)(2,1)S(1)}, bf16[128,1536]{1,0:T(8,128)(2,1)}, u32[]{:S(2)}) copy-start(bf16[128,1536]{1,0:T(8,128)(2,1)} %dy.1) | copy-start | bytes 1179652
  26.6 44.6 %copy-start.23 = (bf16[2560,128]{1,0:T(8,128)(2,1)}, bf16[2560,128]{1,0:T(8,128)(2,1)S(1)}, u32[]{:S(2)}) copy-start(bf16[2560,128]{1,0:T(8,128)(2,1)S(1)} %get-tuple-element.47.qkv) | copy-start | bytes 1966084
  26.6 44.6 %copy-start.29 = (bf16[1536,128]{1,0:T(8,128)(2,1)}, bf16[1536,128]{1,0:T(8,128)(2,1)S(1)}, u32[]{:S(2)}) copy-start(bf16[1536,128]{1,0:T(8,128)(2,1)S(1)} %get-tuple-element.48.ctx) | copy-start | bytes 1179652
  26.6 25.2 %collective-permute-start.2 = (bf16[128,1536]{1,0:T(8,128)(2,1)S(1)}, bf16[128,1536]{1,0:T(8,128)(2,1)S(1)}, u32[]{:S(2)}, u32[]{:S(2)}) collective-permute-start(bf16[128,1536]{1,0:T(8,128)(2,1)S(1)} %get-tuple-element.36.u0), channel_id=1, source_target_pairs={{0,3},{1,2},{2,1},{3,0},{4,7},{5,6},{6,5},{7,4}} | collective-permute-start | bytes 1179656 | tf_op jit(solution)/shard_map/ppermute | solution.py:491
  26.6 25.2 %collective-permute-start.1 = (bf16[128,1536]{1,0:T(8,128)(2,1)S(1)}, bf16[128,1536]{1,0:T(8,128)(2,1)S(1)}, u32[]{:S(2)}, u32[]{:S(2)}) collective-permute-start(bf16[128,1536]{1,0:T(8,128)(2,1)S(1)} %get-tuple-element.36.u0), channel_id=1, source_target_pairs={{0,2},{1,3},{2,0},{3,1},{4,6},{5,7},{6,4},{7,5}} | collective-permute-start | bytes 1179656 | tf_op jit(solution)/shard_map/ppermute | solution.py:491
  27.8 24.1 %collective-permute-start = (bf16[128,1536]{1,0:T(8,128)(2,1)S(1)}, bf16[128,1536]{1,0:T(8,128)(2,1)S(1)}, u32[]{:S(2)}, u32[]{:S(2)}) collective-permute-start(bf16[128,1536]{1,0:T(8,128)(2,1)S(1)} %get-tuple-element.36.u0), channel_id=1, source_target_pairs={{0,1},{1,0},{2,3},{3,2},{4,5},{5,4},{6,7},{7,6}} | collective-permute-start | bytes 1179656 | tf_op jit(solution)/shard_map/ppermute | solution.py:491
  28.5 42.7 %copy-start = (bf16[48,128]{1,0:T(8,128)(2,1)}, bf16[48,128]{1,0:T(8,128)(2,1)S(1)}, u32[]{:S(2)}) copy-start(bf16[48,128]{1,0:T(8,128)(2,1)S(1)} %pack.1.i0) | copy-start | bytes 36868
  28.5 17.9 %collective-permute-start.5 = (bf16[48,128]{1,0:T(8,128)(2,1)S(1)}, bf16[48,128]{1,0:T(8,128)(2,1)S(1)}, u32[]{:S(2)}, u32[]{:S(2)}) collective-permute-start(bf16[48,128]{1,0:T(8,128)(2,1)S(1)} %pack.1.i0), channel_id=1, source_target_pairs={{0,3},{1,2},{2,1},{3,0},{4,7},{5,6},{6,5},{7,4}} | collective-permute-start | bytes 36872 | tf_op jit(solution)/shard_map/ppermute | solution.py:491
  46.5 24.7 %copy-start.16 = (bf16[48,128]{1,0:T(8,128)(2,1)}, bf16[48,128]{1,0:T(8,128)(2,1)S(1)}, u32[]{:S(2)}) copy-start(bf16[48,128]{1,0:T(8,128)(2,1)S(1)} %collective-permute-done.5.i3) | copy-start | bytes 36868
  46.5 3.7 %collective-permute-start.4 = (bf16[48,128]{1,0:T(8,128)(2,1)S(1)}, bf16[48,128]{1,0:T(8,128)(2,1)S(1)}, u32[]{:S(2)}, u32[]{:S(2)}) collective-permute-start(bf16[48,128]{1,0:T(8,128)(2,1)S(1)} %pack.1.i0), channel_id=1, source_target_pairs={{0,2},{1,3},{2,0},{3,1},{4,6},{5,7},{6,4},{7,5}} | collective-permute-start | bytes 36872 | tf_op jit(solution)/shard_map/ppermute | solution.py:491
  50.1 21.1 %copy-start.17 = (bf16[48,128]{1,0:T(8,128)(2,1)}, bf16[48,128]{1,0:T(8,128)(2,1)S(1)}, u32[]{:S(2)}) copy-start(bf16[48,128]{1,0:T(8,128)(2,1)S(1)} %collective-permute-done.4.i2) | copy-start | bytes 36868
  50.2 1.2 collective-permute-start.3
  51.3 21.1 %collective-permute-start.9 = (bf16[128,1536]{1,0:T(8,128)(2,1)S(1)}, bf16[128,1536]{1,0:T(8,128)(2,1)S(1)}, u32[]{:S(2)}, u32[]{:S(2)}) collective-permute-start(bf16[128,1536]{1,0:T(8,128)(2,1)S(1)} %copy-done.14), channel_id=1, source_target_pairs={{0,1},{1,0},{2,3},{3,2},{4,5},{5,4},{6,7},{7,6}} | collective-permute-start | bytes 1179656 | tf_op jit(solution)/shard_map/ppermute | solution.py:491
  51.5 21.7 %collective-permute-start.11 = (bf16[128,1536]{1,0:T(8,128)(2,1)S(1)}, bf16[128,1536]{1,0:T(8,128)(2,1)}, u32[]{:S(2)}, u32[]{:S(2)}) collective-permute-start(bf16[128,1536]{1,0:T(8,128)(2,1)S(1)} %collective-permute-done.10.d2), channel_id=1, source_target_pairs={{0,1},{1,0},{2,3},{3,2},{4,5},{5,4},{6,7},{7,6}} | collective-permute-start | bytes 1179656 | tf_op jit(solution)/shard_map/ppermute | solution.py:491
  71.2 96.6 %copy-start.13 = (bf16[128,1536]{1,0:T(8,128)(2,1)S(1)}, bf16[128,1536]{1,0:T(8,128)(2,1)}, u32[]{:S(2)}) copy-start(bf16[128,1536]{1,0:T(8,128)(2,1)} %x_b.3) | copy-start | bytes 1179652
  71.2 96.6 %copy-start.20 = (bf16[1536]{0:T(1024)(128)(2,1)S(1)}, bf16[1536]{0:T(1024)(128)(2,1)}, u32[]{:S(2)}) copy-start(bf16[1536]{0:T(1024)(128)(2,1)} %n1.3) | copy-start | bytes 9220
  71.3 96.6 %copy-start.22 = (bf16[1536]{0:T(1024)(128)(2,1)S(1)}, bf16[1536]{0:T(1024)(128)(2,1)}, u32[]{:S(2)}) copy-start(bf16[1536]{0:T(1024)(128)(2,1)} %n2.3) | copy-start | bytes 9220
  71.3 59.0 %collective-permute-start.7 = (f32[128,1536]{1,0:T(8,128)S(1)}, f32[128,1536]{1,0:T(8,128)}, u32[]{:S(2)}, u32[]{:S(2)}) collective-permute-start(f32[128,1536]{1,0:T(8,128)S(1)} %get-tuple-element.40), channel_id=1, source_target_pairs={{0,1},{1,0},{2,3},{3,2},{4,5},{5,4},{6,7},{7,6}} | collective-permute-start | bytes 2359304 | tf_op jit(solution)/shard_map/ppermute | solution.py:491
  129.7 2.5 %collective-permute-start.13 = (f32[128,1536]{1,0:T(8,128)}, f32[128,1536]{1,0:T(8,128)S(1)}, u32[]{:S(2)}, u32[]{:S(2)}) collective-permute-start(f32[128,1536]{1,0:T(8,128)} %get-tuple-element.44), channel_id=1, source_target_pairs={{0,1},{1,0},{2,3},{3,2},{4,5},{5,4},{6,7},{7,6}} | collective-permute-start | bytes 2359304 | tf_op jit(solution)/shard_map/ppermute | solution.py:491
  129.7 5.0 %collective-permute-start.6 = (f32[128,1536]{1,0:T(8,128)S(1)}, f32[128,1536]{1,0:T(8,128)S(1)}, u32[]{:S(2)}, u32[]{:S(2)}) collective-permute-start(f32[128,1536]{1,0:T(8,128)S(1)} %get-tuple-element.38), channel_id=1, source_target_pairs={{0,1},{1,0},{2,3},{3,2},{4,5},{5,4},{6,7},{7,6}} | collective-permute-start | bytes 2359304 | tf_op jit(solution)/shard_map/ppermute | solution.py:491
  131.5 20.4 %collective-permute-start.8 = (f32[128,1536]{1,0:T(8,128)S(1)}, f32[128,1536]{1,0:T(8,128)S(1)}, u32[]{:S(2)}, u32[]{:S(2)}) collective-permute-start(f32[128,1536]{1,0:T(8,128)S(1)} %add.16), channel_id=1, source_target_pairs={{0,2},{1,3},{2,0},{3,1},{4,6},{5,7},{6,4},{7,5}} | collective-permute-start | bytes 2359304 | tf_op jit(solution)/shard_map/ppermute | solution.py:491
  131.5 21.4 %collective-permute-start.12 = (f32[128,1536]{1,0:T(8,128)}, f32[128,1536]{1,0:T(8,128)S(1)}, u32[]{:S(2)}, u32[]{:S(2)}) collective-permute-start(f32[128,1536]{1,0:T(8,128)} %get-tuple-element.42), channel_id=1, source_target_pairs={{0,1},{1,0},{2,3},{3,2},{4,5},{5,4},{6,7},{7,6}} | collective-permute-start | bytes 2359304 | tf_op jit(solution)/shard_map/ppermute | solution.py:491
  133.4 34.4 %collective-permute-start.14 = (f32[128,1536]{1,0:T(8,128)S(1)}, f32[128,1536]{1,0:T(8,128)S(1)}, u32[]{:S(2)}, u32[]{:S(2)}) collective-permute-start(f32[128,1536]{1,0:T(8,128)S(1)} %add.19), channel_id=1, source_target_pairs={{0,2},{1,3},{2,0},{3,1},{4,6},{5,7},{6,4},{7,5}} | collective-permute-start | bytes 2359304 | tf_op jit(solution)/shard_map/ppermute | solution.py:491
  (25 other events, 140.8 us)
where the time goes:
time: 189 us; the launch traced here: 188 us
  Pallas kernels  99.6 us (53%)
  waiting for transfers between devices  55.2 us (29%)
  local copies, waits for them, and re-layouts  19.4 us (10%)
  starting transfers between devices  9.13 us (5%)
  other arithmetic  3.43 us (2%)
    pallas_call x1, Pallas kernels, expert_bwd(): pl.pallas_call(functools.partial(expert_bwd_kernel, cols // 4), grid=(cou...  56.5 us
    ppermute x15, waiting for transfers between devices, hop(): return lax.ppermute(value, 'expert', [(i, i ^ bits) for i in range(group)])  55.2 us
    unnamed x68, local copies, waits for them, and re-layouts  19.4 us
    pallas_call x1, Pallas kernels, expert_fwd(): pl.pallas_call(expert_fwd_kernel, grid=(count,), out_shape=(part, part, p...  19.3 us
    pallas_call x1, Pallas kernels, attn_bwd(): pl.pallas_call(functools.partial(attn_bwd_kernel, kv_heads, reps, dim), o...  13.6 us
    pallas_call x1, Pallas kernels, attn_fwd(): pl.pallas_call(functools.partial(attn_fwd_kernel, kv_heads, reps, dim), o...  10.2 us
    ppermute x15, starting transfers between devices, hop(): return lax.ppermute(value, 'expert', [(i, i ^ bits) for i in range(group)])  9.13 us
  transfers between devices with their start and end apart: 15, of which 6 were waited for; matrix products, arithmetic and copies ran while one was open for 2% of the time, Pallas kernels for 46%

commit v1 on v0

--- a/solution.py
+++ b/solution.py
@@ -12,6 +12,7 @@
 BF = jnp.bfloat16
 F32 = jnp.float32
 MIB = 1024 * 1024
+CHUNK = 128
 
 
 def nn(a, b):
@@ -122,7 +123,7 @@
             pltpu.VMEM((2 * tokens, model), BF), pltpu.VMEM((q_dim, 2 * tokens), BF), pltpu.VMEM((kv_dim, 2 * tokens), BF), pltpu.VMEM((kv_dim, 2 * tokens), BF),
             pltpu.VMEM((q_dim, 2 * tokens), BF), pltpu.SemaphoreType.DMA((4,)),
         ],
-        compiler_params=pltpu.CompilerParams(vmem_limit_bytes=24 * MIB),
+        compiler_params=pltpu.CompilerParams(vmem_limit_bytes=60 * MIB),
         cost_estimate=pl.CostEstimate(flops=10 ** 10, bytes_accessed=14 * 10 ** 6, transcendentals=0),
         name="attn_fwd",
     )(x_a, x_b, n1, n2, wq, wk, wv, wo)
@@ -210,7 +211,7 @@
             pltpu.VMEM((q_dim, tokens), BF), pltpu.VMEM((q_dim, tokens), BF), pltpu.VMEM((kv_dim, tokens), BF), pltpu.VMEM((kv_dim, tokens), BF),
             pltpu.SemaphoreType.DMA((4,)), pltpu.SemaphoreType.DMA((n_out,)),
         ],
-        compiler_params=pltpu.CompilerParams(vmem_limit_bytes=48 * MIB),
+        compiler_params=pltpu.CompilerParams(vmem_limit_bytes=60 * MIB),
         cost_estimate=pl.CostEstimate(flops=14 * 10 ** 9, bytes_accessed=40 * 10 ** 6, transcendentals=0),
         name="attn_bwd",
     )(s0, s1, t0, dy, h_b, x_b, nb, qkv, ctx, n1, n2, wo, wq, wk, wv)
@@ -219,6 +220,7 @@
 def route_rows(infos, base, expert):
     wide = [ref[...].astype(F32) for ref in infos]
     top_k = wide[0].shape[0] // 6
+    tokens = wide[0].shape[1]
 
     def field(i):
         return jnp.concatenate([w[(base + i) * top_k:(base + i + 1) * top_k] for w in wide], axis=1)
@@ -227,189 +229,306 @@
     hit = (eid == expert.astype(F32)) & (slot >= 0.0)
     slot_row = jnp.sum(jnp.where(hit, slot + 1.0, 0.0), axis=0, keepdims=True) - 1.0
     gate_row = jnp.sum(jnp.where(hit, gate, 0.0), axis=0, keepdims=True)
-    return slot_row, gate_row
-
-
-def expert_bwd_kernel(capacity, d0, d1, d2, d3, i0, i1, i2, i3, u_h, w1_h, w2_h, w3_h,
-                      g1, g2, g3, p0, p1, p2, p3,
-                      rows, us, w1s, w2s, w3s, pick_t, du_all, d_out, hid, da1, da3, o1, o2, o3, parts, rsem, wsem, sems, psem):
+    kept = jnp.where(slot_row >= 0.0, 1.0, 0.0)
+    start = jnp.zeros((1, 1), F32)
+    starts = []
+    for r in range(len(infos)):
+        starts.append(jnp.broadcast_to(start, (1, tokens)))
+        start = start + jnp.sum(kept[:, r * tokens:(r + 1) * tokens], axis=1, keepdims=True)
+    place_row = jnp.where(slot_row >= 0.0, slot_row + jnp.concatenate(starts, axis=1), -1.0).astype(jnp.int32)
+    return slot_row, gate_row, place_row, jnp.sum(kept)
+
+
+def columns_of(slot_row, me, tokens, capacity):
+    device = jnp.bitwise_xor(lax.broadcasted_iota(jnp.int32, slot_row.shape, 1) // tokens, me)
+    return slot_row + (device * capacity).astype(F32)
+
+
+def hits(place_row, first):
+    return lax.broadcasted_iota(jnp.int32, (CHUNK, place_row.shape[1]), 0) + first == place_row
+
+
+def squeeze_rows(hot, col_row, u):
+    col = jnp.sum(jnp.where(hot, col_row + 1.0, 0.0), axis=1, keepdims=True) - 1.0
+    lane = lax.broadcasted_iota(jnp.int32, (CHUNK, u.shape[0]), 1)
+    return nn(jnp.where(lane == col.astype(jnp.int32), 1.0, 0.0).astype(BF), u[...]).astype(BF)
+
+
+def ring_copies(pairs, sem, idx, ring):
+    s = lax.rem(idx, ring)
+    return [pltpu.make_async_copy(src.at[idx], dst.at[s], sem.at[s, i]) for i, (src, dst) in enumerate(pairs)]
+
+
+def row_copies(refs, rows, sem):
+    tokens = rows.shape[0] // len(refs)
+    return [pltpu.make_async_copy(ref, rows.at[r * tokens:(r + 1) * tokens], sem.at[r]) for r, ref in enumerate(refs)]
+
+
+def part_copies(acc, refs, sem):
+    tokens = acc.shape[0] // len(refs)
+    return [pltpu.make_async_copy(acc.at[r * tokens:(r + 1) * tokens], ref, sem.at[r]) for r, ref in enumerate(refs)]
+
+
+def start_all(copies):
+    for c in copies:
+        c.start()
+
+
+def wait_all(copies):
+    for c in copies:
+        c.wait()
+
+
+def mix_into(acc, pick, outs):
+    for n in range(acc.shape[1] // 256):
+        part = slice(n * 256, (n + 1) * 256)
+        acc[:, part] += nn(pick, outs[:, part])
+
+
+def expert_data_kernel(capacity, d0, d1, d2, d3, i0, i1, i2, i3, u_h, w1_h, w2_h, w3_h,
+                       acts, p0, p1, p2, p3,
+                       rows, us, w1s, w2s, w3s, pick, du_two, act, act_b, late_t, acc, rsem, wsem, asem, lsem, psem):
     e = pl.program_id(0)
     count = pl.num_programs(0)
     me = lax.axis_index('expert')
     tokens = rows.shape[0] // 4
+    ring = us.shape[0]
+    ff = w1s.shape[2]
+    model = rows.shape[1]
     slot_e = lax.rem(e, 2)
-    ring = us.shape[0]
-    cols, model = us.shape[1:]
-    ff = w1s.shape[2]
-    padded = du_all.shape[1]
-
-    def fetch(idx):
-        s = lax.rem(idx, ring)
-        return [pltpu.make_async_copy(src.at[idx], dst.at[s], wsem.at[s, i]) for i, (src, dst) in enumerate(((u_h, us), (w1_h, w1s), (w3_h, w3s), (w2_h, w2s)))]
-
-    def arrivals():
-        return [pltpu.make_async_copy(ref, rows.at[r * tokens:(r + 1) * tokens], rsem.at[r]) for r, ref in enumerate((d0, d1, d2, d3))]
+    arrivals = row_copies((d0, d1, d2, d3), rows, rsem)
+    pairs = ((u_h, us), (w1_h, w1s), (w3_h, w3s), (w2_h, w2s))
 
     @pl.when(e == 0)
     def _():
-        for c in arrivals() + fetch(0) + fetch(1):
-            c.start()
-        for c in arrivals():
-            c.wait()
+        start_all(arrivals + ring_copies(pairs, wsem, 0, ring) + ring_copies(pairs, wsem, 1, ring))
+        acc[...] = jnp.zeros_like(acc)
+        wait_all(arrivals)
 
     @pl.when(e + 2 < count)
     def _():
-        for c in fetch(e + 2):
-            c.start()
-
-    slot_row, gate_row = route_rows((i0, i1, i2, i3), 3, me * count + e)
-    lane_dev = lax.broadcasted_iota(jnp.int32, slot_row.shape, 1) // tokens
-    device = jnp.bitwise_xor(lane_dev, me)
-    col_row = jnp.where(slot_row >= 0.0, slot_row.astype(jnp.int32) + device * capacity, -1)
-    hot = lax.broadcasted_iota(jnp.int32, (padded, 4 * tokens), 0) == col_row
-    gated = jnp.where(hot, gate_row, 0.0).astype(BF)
-    plain = jnp.where(hot, 1.0, 0.0).astype(BF)
-    pick_t[:, pl.ds(pl.multiple_of(e * padded, padded), padded)] = jnp.transpose(plain)
-    d_out[...] = nn(gated[0:cols], rows[...]).astype(BF)
-
-    def copies(s, idx):
-        return [pltpu.make_async_copy(src.at[s], dst.at[idx], sems.at[s, i]) for i, (src, dst) in enumerate(((o1, g1), (o2, g2), (o3, g3)))]
-
-    for c in fetch(e):
-        c.wait()
+        start_all(ring_copies(pairs, wsem, e + 2, ring))
+
+    slot_row, gate_row, place_row, filled = route_rows((i0, i1, i2, i3), 3, me * count + e)
+    col_row = columns_of(slot_row, me, tokens, capacity)
+
+    def save(idx):
+        s = lax.rem(idx, 2)
+        return pltpu.make_async_copy(act.at[s], acts.at[idx, 0:CHUNK], asem.at[s])
+
+    @pl.when(e >= 2)
+    def _():
+        save(e - 2).wait()
+
+    wait_all(ring_copies(pairs, wsem, e, ring))
     now = lax.rem(e, ring)
     u, w1, w2, w3 = us.at[now], w1s.at[now], w2s.at[now], w3s.at[now]
-    uv = u[...]
-    dov = d_out[...]
-    half = 256
-    for n in range(ff // half):
-        part = slice(n * half, (n + 1) * half)
-        pre1 = nn(uv, w1[:, part]).astype(BF).astype(F32)
-        pre3 = nn(uv, w3[:, part]).astype(BF).astype(F32)
-        grad_hid = nt(dov, w2[part, :]).astype(BF).astype(F32)
-        sigma = jax.nn.sigmoid(pre1)
-        silu = pre1 * sigma
-        hid[:, part] = (silu * pre3).astype(BF)
-        da1[:, part] = (grad_hid * pre3 * sigma * (1.0 + pre1 * (1.0 - sigma))).astype(BF)
-        da3[:, part] = (grad_hid * silu).astype(BF)
-
-    @pl.when(e >= 2)
-    def _():
-        for c in copies(slot_e, e - 2):
-            c.wait()
-
-    fresh = copies(slot_e, e)
-    for m in range(ff // 256):
-        part = slice(m * 256, (m + 1) * 256)
-        o2[slot_e, part] = tn(hid[:, part], dov)
-    fresh[1].start()
-    for m in range(model // 256):
-        part = slice(m * 256, (m + 1) * 256)
-        o1[slot_e, part] = tn(u[:, part], da1[...])
-        o3[slot_e, part] = tn(u[:, part], da3[...])
-    fresh[0].start()
-    fresh[2].start()
-    for n in range(model // 256):
-        part = slice(n * 256, (n + 1) * 256)
-        du_all[e, 0:cols, part] = (nt(da1[...], w1[part]) + nt(da3[...], w3[part])).astype(BF)
-    du_all[e, cols:padded] = jnp.zeros((padded - cols, model), BF)
+
+    def run(first, keep):
+        hot = hits(place_row, first)
+        d_out = nn(jnp.where(hot, gate_row, 0.0).astype(BF), rows[...]).astype(BF)
+        u_c = squeeze_rows(hot, col_row, u)
+        for n in range(ff // 256):
+            part = slice(n * 256, (n + 1) * 256)
+            pre1 = nn(u_c, w1[:, part]).astype(BF).astype(F32)
+            pre3 = nn(u_c, w3[:, part]).astype(BF).astype(F32)
+            grad_hid = nt(d_out, w2[part, :]).astype(BF).astype(F32)
+            sigma = jax.nn.sigmoid(pre1)
+            silu = pre1 * sigma
+            keep[:, n * 256:(n + 1) * 256] = (silu * pre3).astype(BF)
+            keep[:, ff + n * 256:ff + (n + 1) * 256] = (grad_hid * pre3 * sigma * (1.0 + pre1 * (1.0 - sigma))).astype(BF)
+            keep[:, 2 * ff + n * 256:2 * ff + (n + 1) * 256] = (grad_hid * silu).astype(BF)
+        du = [(nt(keep[:, ff:2 * ff], w1[n * 256:(n + 1) * 256]) + nt(keep[:, 2 * ff:3 * ff], w3[n * 256:(n + 1) * 256])).astype(BF) for n in range(model // 256)]
+        return jnp.transpose(jnp.where(hot, 1.0, 0.0).astype(BF)), du
+
+    chosen, du = run(0, act.at[slot_e])
+    save(e).start()
+    half = pl.ds(pl.multiple_of(slot_e * CHUNK, CHUNK), CHUNK)
+    pick[:, half] = chosen
+    for n, piece in enumerate(du):
+        du_two[half, n * 256:(n + 1) * 256] = piece
+
+    @pl.when(filled > float(CHUNK))
+    def _():
+        more, du_more = run(CHUNK, act_b)
+        c = pltpu.make_async_copy(act_b, acts.at[e, CHUNK:2 * CHUNK], lsem.at[0])
+        c.start()
+        late_t[...] = more
+        for n, piece in enumerate(du_more):
+            acc[:, n * 256:(n + 1) * 256] += nn(late_t[...], piece)
+        c.wait()
+
+    @pl.when(slot_e == 1)
+    def _():
+        mix_into(acc, pick[...], du_two)
 
     @pl.when(e == count - 1)
     def _():
-        for n in range(model // 256):
-            part = slice(n * 256, (n + 1) * 256)
-            parts[:, part] = nn(pick_t[...], du_all[:, :, part].reshape(pick_t.shape[1], 256))
-        sends = [pltpu.make_async_copy(parts.at[r * tokens:(r + 1) * tokens], ref, psem.at[r]) for r, ref in enumerate((p0, p1, p2, p3))]
-        for c in sends:
-            c.start()
-        for back in (1, 0):
-            for c in copies(lax.rem(e + back, 2), e - back):
-                c.wait()
-        for c in sends:
-            c.wait()
+        sends = part_copies(acc, (p0, p1, p2, p3), psem)
+        start_all(sends)
+        save(e - 1).wait()
+        save(e).wait()
+        wait_all(sends)
 
 
 def whole(shape):
     return pl.BlockSpec(shape, lambda e: (0,) * len(shape), pipeline_mode=pl.Buffered(1))
 
 
-def expert_bwd(dys, infos, u, w1, w2, w3):
+def expert_data(dys, infos, u, w1, w2, w3):
     tokens, model = dys[0].shape
     count, cols, _ = u.shape
     ff = w1.shape[2]
-    padded, ring = 256, 3
+    ring = 3
     hb = pl.BlockSpec(memory_space=pl.ANY)
     part = jax.ShapeDtypeStruct((tokens, model), F32)
     return pl.pallas_call(
-        functools.partial(expert_bwd_kernel, cols // 4),
+        functools.partial(expert_data_kernel, cols // 4),
         grid=(count,),
-        out_shape=(jax.ShapeDtypeStruct((count, model, ff), F32), jax.ShapeDtypeStruct((count, ff, model), F32), jax.ShapeDtypeStruct((count, model, ff), F32), part, part, part, part),
+        out_shape=(jax.ShapeDtypeStruct((count, 2 * CHUNK, 3 * ff), BF), part, part, part, part),
         in_specs=[hb] * 4 + [whole(infos[0].shape)] * 4 + [hb] * 4,
-        out_specs=(hb,) * 7,
+        out_specs=(hb,) * 5,
         scratch_shapes=[
             pltpu.VMEM((4 * tokens, model), BF),
             pltpu.VMEM((ring, cols, model), BF), pltpu.VMEM((ring, model, ff), BF), pltpu.VMEM((ring, ff, model), BF), pltpu.VMEM((ring, model, ff), BF),
-            pltpu.VMEM((4 * tokens, count * padded), BF), pltpu.VMEM((count, padded, model), BF),
-            pltpu.VMEM((cols, model), BF), pltpu.VMEM((cols, ff), BF), pltpu.VMEM((cols, ff), BF), pltpu.VMEM((cols, ff), BF),
-            pltpu.VMEM((2, model, ff), F32), pltpu.VMEM((2, ff, model), F32), pltpu.VMEM((2, model, ff), F32),
-            pltpu.VMEM((4 * tokens, model), F32),
-            pltpu.SemaphoreType.DMA((4,)), pltpu.SemaphoreType.DMA((ring, 4)), pltpu.SemaphoreType.DMA((2, 3)), pltpu.SemaphoreType.DMA((4,)),
+            pltpu.VMEM((4 * tokens, 2 * CHUNK), BF), pltpu.VMEM((2 * CHUNK, model), BF),
+            pltpu.VMEM((2, CHUNK, 3 * ff), BF), pltpu.VMEM((CHUNK, 3 * ff), BF), pltpu.VMEM((4 * tokens, CHUNK), BF), pltpu.VMEM((4 * tokens, model), F32),
+            pltpu.SemaphoreType.DMA((4,)), pltpu.SemaphoreType.DMA((ring, 4)), pltpu.SemaphoreType.DMA((2,)), pltpu.SemaphoreType.DMA((1,)), pltpu.SemaphoreType.DMA((4,)),
         ],
         compiler_params=pltpu.CompilerParams(vmem_limit_bytes=60 * MIB, dimension_semantics=("arbitrary",)),
-        cost_estimate=pl.CostEstimate(flops=50 * 10 ** 9, bytes_accessed=150 * 10 ** 6, transcendentals=0),
-        name="expert_bwd",
+        cost_estimate=pl.CostEstimate(flops=20 * 10 ** 9, bytes_accessed=70 * 10 ** 6, transcendentals=0),
+        name="expert_data",
     )(*dys, *infos, u, w1, w2, w3)
 
 
-def expert_fwd_kernel(u0, u1, u2, u3, i0, i1, i2, i3, w1_h, w2_h, w3_h, p0, p1, p2, p3,
-                      rows, w1s, w2s, w3s, pick_t, out_all, late, late_t, rsem, wsem, psem):
+def expert_grad_kernel(capacity, d0, d1, d2, d3, i0, i1, i2, i3, u_h, act_h,
+                       g1, g2, g3,
+                       rows, us, acts, act_b, d_out, u_c, o1, o2, o3, rsem, wsem, lsem, sems):
     e = pl.program_id(0)
     count = pl.num_programs(0)
     me = lax.axis_index('expert')
     tokens = rows.shape[0] // 4
-    ring, model, ff = w1s.shape
-    chunk = 128
+    ring = us.shape[0]
+    model = rows.shape[1]
+    ff = o2.shape[1]
+    slot_e = lax.rem(e, 2)
+    arrivals = row_copies((d0, d1, d2, d3), rows, rsem)
 
     def fetch(idx):
         s = lax.rem(idx, ring)
-        return [pltpu.make_async_copy(src.at[idx], dst.at[s], wsem.at[s, i]) for i, (src, dst) in enumerate(((w1_h, w1s), (w3_h, w3s), (w2_h, w2s)))]
-
-    def arrivals():
-        return [pltpu.make_async_copy(ref, rows.at[r * tokens:(r + 1) * tokens], rsem.at[r]) for r, ref in enumerate((u0, u1, u2, u3))]
+        return [pltpu.make_async_copy(u_h.at[idx], us.at[s], wsem.at[s, 0]), pltpu.make_async_copy(act_h.at[idx, 0:CHUNK], acts.at[s], wsem.at[s, 1])]
+
+    def flush(idx):
+        s = lax.rem(idx, 2)
+        return [pltpu.make_async_copy(src.at[s], dst.at[idx], sems.at[s, i]) for i, (src, dst) in enumerate(((o1, g1), (o2, g2), (o3, g3)))]
 
     @pl.when(e == 0)
     def _():
-        for c in arrivals() + fetch(0) + fetch(1):
-            c.start()
-        late[...] = jnp.zeros_like(late)
-        for c in arrivals():
-            c.wait()
+        start_all(arrivals + fetch(0) + fetch(1))
+        wait_all(arrivals)
 
     @pl.when(e + 2 < count)
     def _():
-        for c in fetch(e + 2):
-            c.start()
-
-    slot_row, gate_row = route_rows((i0, i1, i2, i3), 0, me * count + e)
-    kept = jnp.where(slot_row >= 0.0, 1.0, 0.0)
-    start = jnp.zeros((1, 1), F32)
-    starts = []
-    for r in range(4):
-        starts.append(jnp.broadcast_to(start, (1, tokens)))
-        start = start + jnp.sum(kept[:, r * tokens:(r + 1) * tokens], axis=1, keepdims=True)
-    filled = jnp.sum(kept)
-    col_row = jnp.where(slot_row >= 0.0, slot_row + jnp.concatenate(starts, axis=1), -1.0).astype(jnp.int32)
-
-    for c in fetch(e):
+        start_all(fetch(e + 2))
+
+    slot_row, gate_row, place_row, filled = route_rows((i0, i1, i2, i3), 3, me * count + e)
+    col_row = columns_of(slot_row, me, tokens, capacity)
+    wait_all(fetch(e))
+    now = lax.rem(e, ring)
+
+    def rebuild(first):
+        hot = hits(place_row, first)
+        d_out[...] = nn(jnp.where(hot, gate_row, 0.0).astype(BF), rows[...]).astype(BF)
+        u_c[...] = squeeze_rows(hot, col_row, us.at[now])
+
+    rebuild(0)
+
+    @pl.when(e >= 2)
+    def _():
+        wait_all(flush(e - 2))
+
+    done = flush(e)
+    act = acts.at[now]
+    for m in range(ff // 256):
+        o2[slot_e, m * 256:(m + 1) * 256] = tn(act[:, m * 256:(m + 1) * 256], d_out[...])
+    for m in range(model // 256):
+        part = slice(m * 256, (m + 1) * 256)
+        o1[slot_e, part] = tn(u_c[:, part], act[:, ff:2 * ff])
+        o3[slot_e, part] = tn(u_c[:, part], act[:, 2 * ff:3 * ff])
+
+    @pl.when(filled > float(CHUNK))
+    def _():
+        c = pltpu.make_async_copy(act_h.at[e, CHUNK:2 * CHUNK], act_b, lsem.at[0])
+        c.start()
+        rebuild(CHUNK)
         c.wait()
+        for m in range(ff // 256):
+            o2[slot_e, m * 256:(m + 1) * 256] += tn(act_b[:, m * 256:(m + 1) * 256], d_out[...])
+        for m in range(model // 256):
+            part = slice(m * 256, (m + 1) * 256)
+            o1[slot_e, part] += tn(u_c[:, part], act_b[:, ff:2 * ff])
+            o3[slot_e, part] += tn(u_c[:, part], act_b[:, 2 * ff:3 * ff])
+
+    start_all(done)
+
+    @pl.when(e == count - 1)
+    def _():
+        wait_all(flush(e - 1))
+        wait_all(flush(e))
+
+
+def expert_grad(dys, infos, u, acts):
+    tokens, model = dys[0].shape
+    count, cols, _ = u.shape
+    ff = acts.shape[2] // 3
+    ring = 3
+    hb = pl.BlockSpec(memory_space=pl.ANY)
+    return pl.pallas_call(
+        functools.partial(expert_grad_kernel, cols // 4),
+        grid=(count,),
+        out_shape=(jax.ShapeDtypeStruct((count, model, ff), F32), jax.ShapeDtypeStruct((count, ff, model), F32), jax.ShapeDtypeStruct((count, model, ff), F32)),
+        in_specs=[hb] * 4 + [whole(infos[0].shape)] * 4 + [hb] * 2,
+        out_specs=(hb,) * 3,
+        scratch_shapes=[
+            pltpu.VMEM((4 * tokens, model), BF), pltpu.VMEM((ring, cols, model), BF), pltpu.VMEM((ring, CHUNK, 3 * ff), BF), pltpu.VMEM((CHUNK, 3 * ff), BF),
+            pltpu.VMEM((CHUNK, model), BF), pltpu.VMEM((CHUNK, model), BF),
+            pltpu.VMEM((2, model, ff), F32), pltpu.VMEM((2, ff, model), F32), pltpu.VMEM((2, model, ff), F32),
+            pltpu.SemaphoreType.DMA((4,)), pltpu.SemaphoreType.DMA((ring, 2)), pltpu.SemaphoreType.DMA((1,)), pltpu.SemaphoreType.DMA((2, 3)),
+        ],
+        compiler_params=pltpu.CompilerParams(vmem_limit_bytes=60 * MIB, dimension_semantics=("arbitrary",)),
+        cost_estimate=pl.CostEstimate(flops=35 * 10 ** 9, bytes_accessed=110 * 10 ** 6, transcendentals=0),
+        name="expert_grad",
+    )(*dys, *infos, u, acts)
+
+
+def expert_fwd_kernel(u0, u1, u2, u3, i0, i1, i2, i3, w1_h, w2_h, w3_h, p0, p1, p2, p3,
+                      rows, w1s, w2s, w3s, pick, out_two, acc, late_t, rsem, wsem, psem):
+    e = pl.program_id(0)
+    count = pl.num_programs(0)
+    me = lax.axis_index('expert')
+    ring, _, ff = w1s.shape
+    slot_e = lax.rem(e, 2)
+    arrivals = row_copies((u0, u1, u2, u3), rows, rsem)
+    pairs = ((w1_h, w1s), (w3_h, w3s), (w2_h, w2s))
+
+    @pl.when(e == 0)
+    def _():
+        start_all(arrivals + ring_copies(pairs, wsem, 0, ring) + ring_copies(pairs, wsem, 1, ring))
+        acc[...] = jnp.zeros_like(acc)
+        wait_all(arrivals)
+
+    @pl.when(e + 2 < count)
+    def _():
+        start_all(ring_copies(pairs, wsem, e + 2, ring))
+
+    _, gate_row, place_row, filled = route_rows((i0, i1, i2, i3), 0, me * count + e)
+    wait_all(ring_copies(pairs, wsem, e, ring))
     now = lax.rem(e, ring)
     w1, w2, w3 = w1s.at[now], w2s.at[now], w3s.at[now]
 
     def run(first):
-        hot = lax.broadcasted_iota(jnp.int32, (chunk, 4 * tokens), 0) + first == col_row
-        plain = jnp.where(hot, 1.0, 0.0).astype(BF)
-        gated = jnp.where(hot, gate_row, 0.0).astype(BF)
-        v = nn(plain, rows[...]).astype(BF)
+        hot = hits(place_row, first)
+        v = nn(jnp.where(hot, 1.0, 0.0).astype(BF), rows[...]).astype(BF)
         pieces = []
         for n in range(ff // 256):
             part = slice(n * 256, (n + 1) * 256)
@@ -417,36 +536,34 @@
             a3 = nn(v, w3[:, part]).astype(BF).astype(F32)
             pieces.append((a1 * jax.nn.sigmoid(a1) * a3).astype(BF))
         hidden = jnp.concatenate(pieces, axis=1)
-        return jnp.transpose(gated), nn(hidden, w2[...]).astype(BF)
-
-    first_t, first_out = run(0)
-    pick_t[:, pl.ds(pl.multiple_of(e * chunk, chunk), chunk)] = first_t
-    out_all[e] = first_out
-
-    @pl.when(filled > float(chunk))
-    def _():
-        more_t, more_out = run(chunk)
-        late_t[...] = more_t
-        for n in range(model // 256):
-            part = slice(n * 256, (n + 1) * 256)
-            late[:, part] += nn(late_t[...], more_out[:, part])
+        return jnp.transpose(jnp.where(hot, gate_row, 0.0).astype(BF)), nn(hidden, w2[...]).astype(BF)
+
+    chosen, out = run(0)
+    half = pl.ds(pl.multiple_of(slot_e * CHUNK, CHUNK), CHUNK)
+    pick[:, half] = chosen
+    out_two[half, :] = out
+
+    @pl.when(filled > float(CHUNK))
+    def _():
+        more, out_more = run(CHUNK)
+        late_t[...] = more
+        mix_into(acc, late_t[...], out_more)
+
+    @pl.when(slot_e == 1)
+    def _():
+        mix_into(acc, pick[...], out_two)
 
     @pl.when(e == count - 1)
     def _():
-        for n in range(model // 256):
-            part = slice(n * 256, (n + 1) * 256)
-            late[:, part] += nn(pick_t[...], out_all[:, :, part].reshape(pick_t.shape[1], 256))
-        sends = [pltpu.make_async_copy(late.at[r * tokens:(r + 1) * tokens], ref, psem.at[r]) for r, ref in enumerate((p0, p1, p2, p3))]
-        for c in sends:
-            c.start()
-        for c in sends:
-            c.wait()
+        sends = part_copies(acc, (p0, p1, p2, p3), psem)
+        start_all(sends)
+        wait_all(sends)
 
 
 def expert_fwd(us, infos, w1, w2, w3):
     tokens, model = us[0].shape
     count, _, ff = w1.shape
-    chunk, ring = 128, 3
+    ring = 3
     part = jax.ShapeDtypeStruct((tokens, model), F32)
     hb = pl.BlockSpec(memory_space=pl.ANY)
     return pl.pallas_call(
@@ -458,11 +575,11 @@
         scratch_shapes=[
             pltpu.VMEM((4 * tokens, model), BF),
             pltpu.VMEM((ring, model, ff), BF), pltpu.VMEM((ring, ff, model), BF), pltpu.VMEM((ring, model, ff), BF),
-            pltpu.VMEM((4 * tokens, count * chunk), BF), pltpu.VMEM((count, chunk, model), BF),
-            pltpu.VMEM((4 * tokens, model), F32), pltpu.VMEM((4 * tokens, chunk), BF),
+            pltpu.VMEM((4 * tokens, 2 * CHUNK), BF), pltpu.VMEM((2 * CHUNK, model), BF),
+            pltpu.VMEM((4 * tokens, model), F32), pltpu.VMEM((4 * tokens, CHUNK), BF),
             pltpu.SemaphoreType.DMA((4,)), pltpu.SemaphoreType.DMA((ring, 3)), pltpu.SemaphoreType.DMA((4,)),
         ],
-        compiler_params=pltpu.CompilerParams(vmem_limit_bytes=36 * MIB, dimension_semantics=("arbitrary",)),
+        compiler_params=pltpu.CompilerParams(vmem_limit_bytes=60 * MIB, dimension_semantics=("arbitrary",)),
         cost_estimate=pl.CostEstimate(flops=16 * 10 ** 9, bytes_accessed=50 * 10 ** 6, transcendentals=0),
         name="expert_fwd",
     )(*us, *infos, w1, w2, w3)
@@ -479,7 +596,7 @@
         pack_kernel,
         out_shape=jax.ShapeDtypeStruct((rows, fields[0].shape[1]), BF),
         in_specs=[vm] * len(fields), out_specs=vm,
-        compiler_params=pltpu.CompilerParams(vmem_limit_bytes=4 * MIB),
+        compiler_params=pltpu.CompilerParams(vmem_limit_bytes=60 * MIB),
         name="pack",
     )(*fields)
 
@@ -503,12 +620,15 @@
         h_a, u_a, h_b, nb, qkv_b, ctx_b = attn_fwd(x_a, x_b, norm_1, norm_2, wq_t, wk_t, wv_t, wo, kv_heads, reps, dim)
         dy3 = hop(dy2, 1)
         us = (u_a, hop(u_a, 1), hop(u_a, 2), hop(u_a, 3))
-        g1, g2, g3, b0, b1, b2, b3 = expert_bwd((dy_b, dy1, dy2, dy3), infos, u_b, w_1, w_2, w_3)
-        far_b = hop(b2 + hop(b3, 1), 2)
+        dys = (dy_b, dy1, dy2, dy3)
+        acts, b0, b1, b2, b3 = expert_data(dys, infos, u_b, w_1, w_2, w_3)
+        swap_b = hop(b3, 1)
         near_b = hop(b1, 1)
         a0, a1, a2, a3 = expert_fwd(us, infos, w_1, w_2, w_3)
+        far_b = hop(b2 + swap_b, 2)
         far_a = hop(a2 + hop(a3, 1), 2)
         near_a = hop(a1, 1)
+        g1, g2, g3 = expert_grad(dys, infos, u_b, acts)
         dx_b, g_q, g_k, g_v, g_o, g_n1, g_n2 = attn_bwd(b0, near_b, far_b, dy_b, h_b, x_b, nb, qkv_b, ctx_b, norm_1, norm_2, wo, wq_t, wk_t, wv_t, kv_heads, reps, dim)
         y_a = (h_a.astype(F32) + ((a0 + near_a) + far_a)).astype(BF)
         g_q = g_q.reshape(heads, dim, model).transpose(2, 0, 1)

time: 189 us -> 171 us (0.905)
  the two profiles are of different devices: /device:TPU:0 before, /device:TPU:5 now
where the time goes in v1:
time: 171 us; the launch traced here: 170 us
  Pallas kernels  132 us (77%)
  waiting for transfers between devices  18.7 us (11%)
  starting transfers between devices  12.1 us (7%)
  other arithmetic  3.27 us (2%)
  local copies, waits for them, and re-layouts  3.1 us (2%)
    pallas_call x1, Pallas kernels, expert_data(): pl.pallas_call(functools.partial(expert_data_kernel, cols // 4), grid=(co...  42.2 us
    pallas_call x1, Pallas kernels, expert_grad(): pl.pallas_call(functools.partial(expert_grad_kernel, cols // 4), grid=(co...  38.1 us
    pallas_call x1, Pallas kernels, expert_fwd(): pl.pallas_call(expert_fwd_kernel, grid=(count,), out_shape=(part, part, p...  22.2 us
    ppermute x15, waiting for transfers between devices, hop(): return lax.ppermute(value, 'expert', [(i, i ^ bits) for i in range(group)])  18.7 us
    pallas_call x1, Pallas kernels, attn_bwd(): pl.pallas_call(functools.partial(attn_bwd_kernel, kv_heads, reps, dim), o...  15.7 us
    pallas_call x1, Pallas kernels, attn_fwd(): pl.pallas_call(functools.partial(attn_fwd_kernel, kv_heads, reps, dim), o...  12.7 us
    ppermute x15, starting transfers between devices, hop(): return lax.ppermute(value, 'expert', [(i, i ^ bits) for i in range(group)])  12.1 us
  transfers between devices with their start and end apart: 15, of which 4 were waited for; matrix products, arithmetic and copies ran while one was open for 2% of the time, Pallas kernels for 68%

profile of v1, /device:TPU:5, one launch (start us, length us, event | category | flops | bytes accessed | tf_op | source)
XLA Modules:
  0.0 170.4 jit_solution(965147888677636000)
XLA Ops:
  0.6 1.2 collective-permute-start.10
  1.9 12.7 %attn_fwd.1 = (bf16[128,1536]{1,0:T(8,128)(2,1)}, bf16[128,1536]{1,0:T(8,128)(2,1)}, bf16[128,1536]{1,0:T(8,128)(2,1)}, bf16[128,1536]{1,0:T(8,128)(2,1)}, bf16[...) custom-call(bf16[128,1536]{1,0:T(8,128)(2,1)} %x_a.1, bf16[128,1536]{1,0:T(8,128)(2,1)} %x_b.3, bf16[1536]{0:T(1024)(128)(2,1)} %n1.3, ...), custom_call_target="tpu_custom_call" | custom-call | flops 10000000000 | bytes 14000000 | tf_op jit(solution)/shard_map/attn_fwd/pallas_call | solution.py:116
  14.6 1.1 collective-permute-start.2
  15.7 1.2 collective-permute-start.1
  16.9 1.4 pack.1.i0
  18.3 0.6 collective-permute-start.5
  18.9 15.7 %collective-permute-done.5.i3 = bf16[48,128]{1,0:T(8,128)(2,1)S(1)} collective-permute-done((bf16[48,128]{1,0:T(8,128)(2,1)}, bf16[48,128]{1,0:T(8,128)(2,1)S(1)}, u32[]{:S(2)}, u32[]{:S(2)}) %collective-permute-start.5) | collective-permute-done | bytes 12320 | tf_op jit(solution)/shard_map/ppermute | solution.py:608
  34.7 1.0 collective-permute-start.4
  35.7 1.7 %collective-permute-done.4.i2 = bf16[48,128]{1,0:T(8,128)(2,1)S(1)} collective-permute-done((bf16[48,128]{1,0:T(8,128)(2,1)}, bf16[48,128]{1,0:T(8,128)(2,1)S(1)}, u32[]{:S(2)}, u32[]{:S(2)}) %collective-permute-start.4) | collective-permute-done | bytes 12320 | tf_op jit(solution)/shard_map/ppermute | solution.py:608
  37.4 2.1 %collective-permute-start.3 = (bf16[48,128]{1,0:T(8,128)(2,1)}, bf16[48,128]{1,0:T(8,128)(2,1)S(1)}, u32[]{:S(2)}, u32[]{:S(2)}) collective-permute-start(bf16[48,128]{1,0:T(8,128)(2,1)} %pack.1.i0), channel_id=1, source_target_pairs={{0,1},{1,0},{2,3},{3,2},{4,5},{5,4},{6,7},{7,6}} | collective-permute-start | bytes 36872 | tf_op jit(solution)/shard_map/ppermute | solution.py:608
  39.5 1.0 collective-permute-done.3.i1
  41.2 0.7 copy-done.6
  42.0 0.7 copy-done.8
  42.7 22.2 %expert_fwd.1 = (f32[128,1536]{1,0:T(8,128)}, f32[128,1536]{1,0:T(8,128)}, f32[128,1536]{1,0:T(8,128)}, f32[128,1536]{1,0:T(8,128)}) custom-call(bf16[128,1536]{1,0:T(8,128)(2,1)} %get-tuple-element.37.u0, bf16[128,1536]{1,0:T(8,128)(2,1)} %copy-done.8, bf16[128,1536]{1,0:T(8,128)(2,1)} %copy-done.7, bf16[128,1536]{1,0:T(8,128)(2,1)} %copy-done.6, ...), custom_call_target="tpu_custom_call" | custom-call | flops 16000000000 | bytes 50000000 | tf_op jit(solution)/shard_map/expert_fwd/pallas_call | solution.py:569
  65.3 0.7 copy-done.4
  66.1 0.8 copy-done.5
  66.8 42.2 %expert_data.1 = (bf16[10,256,1536]{2,1,0:T(8,128)(2,1)}, f32[128,1536]{1,0:T(8,128)}, f32[128,1536]{1,0:T(8,128)}, f32[128,1536]{1,0:T(8,128)}, f32[128,1536]{1,0:T(8,128)}) custom-call(bf16[128,1536]{1,0:T(8,128)(2,1)} %d0.3, bf16[128,1536]{1,0:T(8,128)(2,1)} %copy-done.4, bf16[128,1536]{1,0:T(8,128)(2,1)} %copy-done.3, bf16[128,1536]{1,0:T(8,128)(2,1)} %copy-done.5, ...), custom_call_target="tpu_custom_call" | custom-call | flops 20000000000 | bytes 70000000 | tf_op jit(solution)/shard_map/expert_data/pallas_call | solution.py:385
  109.0 0.5 collective-permute-start.6
  109.7 1.7 collective-permute-start.8
  111.5 1.2 add.19
  112.7 1.7 collective-permute-start.14
  114.4 38.1 %expert_grad.1 = (f32[10,1536,512]{2,1,0:T(8,128)}, f32[10,512,1536]{2,1,0:T(8,128)}, f32[10,1536,512]{2,1,0:T(8,128)}) custom-call(bf16[128,1536]{1,0:T(8,128)(2,1)} %d0.3, bf16[128,1536]{1,0:T(8,128)(2,1)} %copy-done.4, bf16[128,1536]{1,0:T(8,128)(2,1)} %copy-done.3, bf16[128,1536]{1,0:T(8,128)(2,1)} %copy-done.5, bf16[48,128]{1,0:T(8,128)(2,1)} %pack.1.i0, ...), custom_call_target="tpu_custom_call" | custom-call | flops 35000000512 | bytes 110000000 | tf_op jit(solution)/shard_map/expert_grad/pallas_call | solution.py:486
  152.6 2.0 %add_convert_fusion = bf16[128,1536]{1,0:T(8,128)(2,1)} fusion(f32[128,1536]{1,0:T(8,128)S(1)} %collective-permute-done.8, f32[128,1536]{1,0:T(8,128)S(1)} %copy-done, f32[128,1536]{1,0:T(8,128)S(1)} %collective-permute-done.6, bf16[128,1536]{1,0:T(8,128)(2,1)} %get-tuple-element.36), kind=kLoop, calls=%fused_computation | loop fusion | flops 983040 | bytes 3145728 | tf_op jit(solution)/shard_map/convert_element_type | solution.py:633
  154.5 15.7 %attn_bwd.1 = (bf16[128,1536]{1,0:T(8,128)(2,1)}, f32[1536,1536]{1,0:T(8,128)}, f32[512,1536]{1,0:T(8,128)}, f32[512,1536]{1,0:T(8,128)}, f32[1536,1536]{1,0:T(8...) custom-call(f32[128,1536]{1,0:T(8,128)} %get-tuple-element.42.s0, f32[128,1536]{1,0:T(8,128)} %collective-permute-done.12.s1, ...), custom_call_target="tpu_custom_call" | custom-call | flops 14000000000 | bytes 40000000 | tf_op jit(solution)/shard_map/attn_bwd/pallas_call | solution.py:200
  (39 shorter events, 1.4 us)
Async XLA Ops:
  0.6 40.3 %collective-permute-start.10 = (bf16[128,1536]{1,0:T(8,128)(2,1)}, bf16[128,1536]{1,0:T(8,128)(2,1)S(1)}, u32[]{:S(2)}, u32[]{:S(2)}) collective-permute-start(bf16[128,1536]{1,0:T(8,128)(2,1)} %d0.3), channel_id=1, source_target_pairs={{0,2},{1,3},{2,0},{3,1},{4,6},{5,7},{6,4},{7,5}} | collective-permute-start | bytes 1179656 | tf_op jit(solution)/shard_map/ppermute | solution.py:608
  1.9 38.7 %copy-start.2 = (bf16[128,1536]{1,0:T(8,128)(2,1)S(1)}, bf16[128,1536]{1,0:T(8,128)(2,1)}, u32[]{:S(2)}) copy-start(bf16[128,1536]{1,0:T(8,128)(2,1)} %d0.3) | copy-start | bytes 1179652
  14.6 26.5 %collective-permute-start.2 = (bf16[128,1536]{1,0:T(8,128)(2,1)}, bf16[128,1536]{1,0:T(8,128)(2,1)S(1)}, u32[]{:S(2)}, u32[]{:S(2)}) collective-permute-start(bf16[128,1536]{1,0:T(8,128)(2,1)} %get-tuple-element.37.u0), channel_id=1, source_target_pairs={{0,3},{1,2},{2,1},{3,0},{4,7},{5,6},{6,5},{7,4}} | collective-permute-start | bytes 1179656 | tf_op jit(solution)/shard_map/ppermute | solution.py:608
  15.7 25.4 %collective-permute-start.1 = (bf16[128,1536]{1,0:T(8,128)(2,1)}, bf16[128,1536]{1,0:T(8,128)(2,1)S(1)}, u32[]{:S(2)}, u32[]{:S(2)}) collective-permute-start(bf16[128,1536]{1,0:T(8,128)(2,1)} %get-tuple-element.37.u0), channel_id=1, source_target_pairs={{0,2},{1,3},{2,0},{3,1},{4,6},{5,7},{6,4},{7,5}} | collective-permute-start | bytes 1179656 | tf_op jit(solution)/shard_map/ppermute | solution.py:608
  16.9 24.2 %collective-permute-start = (bf16[128,1536]{1,0:T(8,128)(2,1)}, bf16[128,1536]{1,0:T(8,128)(2,1)S(1)}, u32[]{:S(2)}, u32[]{:S(2)}) collective-permute-start(bf16[128,1536]{1,0:T(8,128)(2,1)} %get-tuple-element.37.u0), channel_id=1, source_target_pairs={{0,1},{1,0},{2,3},{3,2},{4,5},{5,4},{6,7},{7,6}} | collective-permute-start | bytes 1179656 | tf_op jit(solution)/shard_map/ppermute | solution.py:608
  18.3 16.4 %collective-permute-start.5 = (bf16[48,128]{1,0:T(8,128)(2,1)}, bf16[48,128]{1,0:T(8,128)(2,1)S(1)}, u32[]{:S(2)}, u32[]{:S(2)}) collective-permute-start(bf16[48,128]{1,0:T(8,128)(2,1)} %pack.1.i0), channel_id=1, source_target_pairs={{0,3},{1,2},{2,1},{3,0},{4,7},{5,6},{6,5},{7,4}} | collective-permute-start | bytes 36872 | tf_op jit(solution)/shard_map/ppermute | solution.py:608
  34.7 6.5 %copy-start.9 = (bf16[48,128]{1,0:T(8,128)(2,1)}, bf16[48,128]{1,0:T(8,128)(2,1)S(1)}, u32[]{:S(2)}) copy-start(bf16[48,128]{1,0:T(8,128)(2,1)S(1)} %collective-permute-done.5.i3) | copy-start | bytes 36868
  34.7 2.8 %collective-permute-start.4 = (bf16[48,128]{1,0:T(8,128)(2,1)}, bf16[48,128]{1,0:T(8,128)(2,1)S(1)}, u32[]{:S(2)}, u32[]{:S(2)}) collective-permute-start(bf16[48,128]{1,0:T(8,128)(2,1)} %pack.1.i0), channel_id=1, source_target_pairs={{0,2},{1,3},{2,0},{3,1},{4,6},{5,7},{6,4},{7,5}} | collective-permute-start | bytes 36872 | tf_op jit(solution)/shard_map/ppermute | solution.py:608
  37.4 3.7 %copy-start.10 = (bf16[48,128]{1,0:T(8,128)(2,1)}, bf16[48,128]{1,0:T(8,128)(2,1)S(1)}, u32[]{:S(2)}) copy-start(bf16[48,128]{1,0:T(8,128)(2,1)S(1)} %collective-permute-done.4.i2) | copy-start | bytes 36868
  37.4 3.1 %collective-permute-start.3 = (bf16[48,128]{1,0:T(8,128)(2,1)}, bf16[48,128]{1,0:T(8,128)(2,1)S(1)}, u32[]{:S(2)}, u32[]{:S(2)}) collective-permute-start(bf16[48,128]{1,0:T(8,128)(2,1)} %pack.1.i0), channel_id=1, source_target_pairs={{0,1},{1,0},{2,3},{3,2},{4,5},{5,4},{6,7},{7,6}} | collective-permute-start | bytes 36872 | tf_op jit(solution)/shard_map/ppermute | solution.py:608
  40.6 24.7 %collective-permute-start.9 = (bf16[128,1536]{1,0:T(8,128)(2,1)S(1)}, bf16[128,1536]{1,0:T(8,128)(2,1)S(1)}, u32[]{:S(2)}, u32[]{:S(2)}) collective-permute-start(bf16[128,1536]{1,0:T(8,128)(2,1)S(1)} %copy-done.2), channel_id=1, source_target_pairs={{0,1},{1,0},{2,3},{3,2},{4,5},{5,4},{6,7},{7,6}} | collective-permute-start | bytes 1179656 | tf_op jit(solution)/shard_map/ppermute | solution.py:608
  40.9 24.0 %copy-start.3 = (bf16[128,1536]{1,0:T(8,128)(2,1)}, bf16[128,1536]{1,0:T(8,128)(2,1)S(1)}, u32[]{:S(2)}) copy-start(bf16[128,1536]{1,0:T(8,128)(2,1)S(1)} %collective-permute-done.10.d2) | copy-start | bytes 1179652
  40.9 24.4 %collective-permute-start.11 = (bf16[128,1536]{1,0:T(8,128)(2,1)S(1)}, bf16[128,1536]{1,0:T(8,128)(2,1)S(1)}, u32[]{:S(2)}, u32[]{:S(2)}) collective-permute-start(bf16[128,1536]{1,0:T(8,128)(2,1)S(1)} %collective-permute-done.10.d2), channel_id=1, source_target_pairs={{0,1},{1,0},{2,3},{3,2},{4,5},{5,4},{6,7},{7,6}} | collective-permute-start | bytes 1179656 | tf_op jit(solution)/shard_map/ppermute | solution.py:608
  41.1 0.7 copy-start.6
  41.1 0.9 copy-start.7
  64.9 44.6 %copy-start.1 = (f32[128,1536]{1,0:T(8,128)S(1)}, f32[128,1536]{1,0:T(8,128)}, u32[]{:S(2)}) copy-start(f32[128,1536]{1,0:T(8,128)} %get-tuple-element.40) | copy-start | bytes 2359300
  64.9 44.6 %collective-permute-start.7 = (f32[128,1536]{1,0:T(8,128)}, f32[128,1536]{1,0:T(8,128)S(1)}, u32[]{:S(2)}, u32[]{:S(2)}) collective-permute-start(f32[128,1536]{1,0:T(8,128)} %get-tuple-element.41), channel_id=1, source_target_pairs={{0,1},{1,0},{2,3},{3,2},{4,5},{5,4},{6,7},{7,6}} | collective-permute-start | bytes 2359304 | tf_op jit(solution)/shard_map/ppermute | solution.py:608
  66.1 0.8 copy-start.5
  109.0 2.5 %collective-permute-start.13 = (f32[128,1536]{1,0:T(8,128)}, f32[128,1536]{1,0:T(8,128)S(1)}, u32[]{:S(2)}, u32[]{:S(2)}) collective-permute-start(f32[128,1536]{1,0:T(8,128)} %get-tuple-element.45), channel_id=1, source_target_pairs={{0,1},{1,0},{2,3},{3,2},{4,5},{5,4},{6,7},{7,6}} | collective-permute-start | bytes 2359304 | tf_op jit(solution)/shard_map/ppermute | solution.py:608
  109.0 43.5 %collective-permute-start.6 = (f32[128,1536]{1,0:T(8,128)}, f32[128,1536]{1,0:T(8,128)S(1)}, u32[]{:S(2)}, u32[]{:S(2)}) collective-permute-start(f32[128,1536]{1,0:T(8,128)} %get-tuple-element.39), channel_id=1, source_target_pairs={{0,1},{1,0},{2,3},{3,2},{4,5},{5,4},{6,7},{7,6}} | collective-permute-start | bytes 2359304 | tf_op jit(solution)/shard_map/ppermute | solution.py:608
  109.5 45.0 %collective-permute-start.12 = (f32[128,1536]{1,0:T(8,128)}, f32[128,1536]{1,0:T(8,128)}, u32[]{:S(2)}, u32[]{:S(2)}) collective-permute-start(f32[128,1536]{1,0:T(8,128)} %get-tuple-element.43), channel_id=1, source_target_pairs={{0,1},{1,0},{2,3},{3,2},{4,5},{5,4},{6,7},{7,6}} | collective-permute-start | bytes 2359304 | tf_op jit(solution)/shard_map/ppermute | solution.py:608
  109.7 42.9 %collective-permute-start.8 = (f32[128,1536]{1,0:T(8,128)S(1)}, f32[128,1536]{1,0:T(8,128)S(1)}, u32[]{:S(2)}, u32[]{:S(2)}) collective-permute-start(f32[128,1536]{1,0:T(8,128)S(1)} %add.16), channel_id=1, source_target_pairs={{0,2},{1,3},{2,0},{3,1},{4,6},{5,7},{6,4},{7,5}} | collective-permute-start | bytes 2359304 | tf_op jit(solution)/shard_map/ppermute | solution.py:608
  112.7 41.8 %collective-permute-start.14 = (f32[128,1536]{1,0:T(8,128)S(1)}, f32[128,1536]{1,0:T(8,128)}, u32[]{:S(2)}, u32[]{:S(2)}) collective-permute-start(f32[128,1536]{1,0:T(8,128)S(1)} %add.19), channel_id=1, source_target_pairs={{0,2},{1,3},{2,0},{3,1},{4,6},{5,7},{6,4},{7,5}} | collective-permute-start | bytes 2359304 | tf_op jit(solution)/shard_map/ppermute | solution.py:608
  114.4 38.1 %copy-start = (f32[128,1536]{1,0:T(8,128)S(1)}, f32[128,1536]{1,0:T(8,128)}, u32[]{:S(2)}) copy-start(f32[128,1536]{1,0:T(8,128)} %get-tuple-element.38) | copy-start | bytes 2359300
  (3 other events, 2.1 us)

commit v2 on v0

v2 whole, which is shorter than its diff:
```python
import functools

import jax
import jax.numpy as jnp
from jax import lax
from jax.experimental import pallas as pl
from jax.experimental.pallas import tpu as pltpu
from jax.sharding import PartitionSpec as P


NORM_EPS = 1e-6
BF = jnp.bfloat16
F32 = jnp.float32
MIB = 1024 * 1024
CHUNK = 128


def nn(a, b):
    return lax.dot_general(a, b, (((1,), (0,)), ((), ())), preferred_element_type=F32)


def nt(a, b):
    return lax.dot_general(a, b, (((1,), (1,)), ((), ())), preferred_element_type=F32)


def tn(a, b):
    return lax.dot_general(a, b, (((0,), (0,)), ((), ())), preferred_element_type=F32)


def row_of(ref):
    return ref[...].astype(F32).reshape(1, ref.shape[0])


def rms_scale(wide):
    return lax.rsqrt(jnp.mean(wide * wide, axis=-1, keepdims=True) + NORM_EPS)


def rms_rows(values, gain):
    wide = values.astype(F32)
    return (wide * rms_scale(wide) * gain).astype(BF)


def rms_pull(wide, gain, cot):
    scale = rms_scale(wide)
    scaled = wide * scale
    grad_gain = jnp.sum(cot * scaled, axis=0, keepdims=True).astype(BF).astype(F32)
    inner = cot * gain
    pull = jnp.mean(inner * wide, axis=-1, keepdims=True)
    grad = scale * inner - scaled * (scale * scale * pull)
    return grad.astype(BF).astype(F32), grad_gain


def probs_of(scores_t):
    rows = lax.broadcasted_iota(jnp.int32, scores_t.shape, 0)
    cols = lax.broadcasted_iota(jnp.int32, scores_t.shape, 1) % scores_t.shape[0]
    masked = jnp.where(rows <= cols, scores_t, -1e30)
    top = jnp.max(masked, axis=0, keepdims=True)
    unnorm = jnp.exp(masked - top)
    return unnorm / jnp.sum(unnorm, axis=0, keepdims=True)


def heads_to_lanes(ref, group, reps, dim, lanes):
    return jnp.concatenate([ref[(group * reps + r) * dim:(group * reps + r + 1) * dim, lanes] for r in range(reps)], axis=1)


def attn_fwd_kernel(kv_heads, reps, dim, xa_h, xb_h, n1, n2, wq_h, wk_h, wv_h, wo_h,
                    ha_h, ua_h, hb_h, nb_h, qkv_h, ctx_h,
                    xs, wq, wk, wv, wo, nrm, nrm_t, q_t, k_t, v_t, ctx, q_b, ctx_b, hs, ua, sems, osems):
    tokens = xs.shape[0] // 2
    heads = kv_heads * reps
    first, second = slice(0, tokens), slice(tokens, 2 * tokens)
    half = heads * dim // 2
    moves = ((xa_h, xs.at[first]), (xb_h, xs.at[second]), (wk_h, wk), (wv_h, wv), (wq_h.at[0:half], wq.at[0:half]), (wq_h.at[half:], wq.at[half:]), (wo_h, wo))
    copies = [pltpu.make_async_copy(s, d, sems.at[i]) for i, (s, d) in enumerate(moves)]
    start_all(copies)
    outs = []

    def flush(src, dst):
        c = pltpu.make_async_copy(src, dst, osems.at[len(outs)])
        c.start()
        outs.append(c)

    wait_all(copies[0:2])
    nrm[...] = rms_rows(xs[...], row_of(n1))
    nrm_t[...] = jnp.transpose(nrm[...])
    flush(nrm.at[second], nb_h)
    copies[2].wait()
    k_t[...] = nn(wk[...], nrm_t[...]).astype(BF)
    copies[3].wait()
    v_t[...] = nn(wv[...], nrm_t[...]).astype(BF)
    for i in range(2):
        copies[4 + i].wait()
        part = slice(i * half, (i + 1) * half)
        q_t[part] = nn(wq[part], nrm_t[...]).astype(BF)
    q_b[0:heads * dim] = q_t[:, second]
    q_b[heads * dim:(heads + kv_heads) * dim] = k_t[:, second]
    q_b[(heads + kv_heads) * dim:] = v_t[:, second]
    flush(q_b, qkv_h)
    for lanes in (second, first):
        for g in range(kv_heads):
            kg = k_t[g * dim:(g + 1) * dim, lanes]
            vg = v_t[g * dim:(g + 1) * dim, lanes]
            qg = heads_to_lanes(q_t, g, reps, dim, lanes)
            probs = probs_of(tn(kg, qg) * dim ** -0.5).astype(BF)
            out = nn(vg, probs).astype(BF)
            for r in range(reps):
                ctx[(g * reps + r) * dim:(g * reps + r + 1) * dim, lanes] = out[:, r * tokens:(r + 1) * tokens]
    ctx_b[...] = ctx[:, second]
    flush(ctx_b, ctx_h)
    copies[6].wait()
    hs[...] = (xs[...].astype(F32) + tn(ctx[...], wo[...]).astype(BF).astype(F32)).astype(BF)
    flush(hs.at[first], ha_h)
    flush(hs.at[second], hb_h)
    ua[...] = rms_rows(hs[first], row_of(n2))
    flush(ua, ua_h)
    wait_all(outs)


def attn_fwd(x_a, x_b, n1, n2, wq, wk, wv, wo, kv_heads, reps, dim):
    tokens, model = x_a.shape
    q_dim, kv_dim = kv_heads * reps * dim, kv_heads * dim
    vm = pl.BlockSpec(memory_space=pltpu.VMEM)
    hb = pl.BlockSpec(memory_space=pl.ANY)
    row = jax.ShapeDtypeStruct((tokens, model), BF)
    return pl.pallas_call(
        functools.partial(attn_fwd_kernel, kv_heads, reps, dim),
        out_shape=(row, row, row, row, jax.ShapeDtypeStruct((q_dim + 2 * kv_dim, tokens), BF), jax.ShapeDtypeStruct((q_dim, tokens), BF)),
        in_specs=[hb] * 2 + [vm] * 2 + [hb] * 4,
        out_specs=(hb,) * 6,
        scratch_shapes=[
            pltpu.VMEM((2 * tokens, model), BF),
            pltpu.VMEM((q_dim, model), BF), pltpu.VMEM((kv_dim, model), BF), pltpu.VMEM((kv_dim, model), BF), pltpu.VMEM((q_dim, model), BF),
            pltpu.VMEM((2 * tokens, model), BF), pltpu.VMEM((model, 2 * tokens), BF),
            pltpu.VMEM((q_dim, 2 * tokens), BF), pltpu.VMEM((kv_dim, 2 * tokens), BF), pltpu.VMEM((kv_dim, 2 * tokens), BF), pltpu.VMEM((q_dim, 2 * tokens), BF),
            pltpu.VMEM((q_dim + 2 * kv_dim, tokens), BF), pltpu.VMEM((q_dim, tokens), BF), pltpu.VMEM((2 * tokens, model), BF), pltpu.VMEM((tokens, model), BF),
            pltpu.SemaphoreType.DMA((7,)), pltpu.SemaphoreType.DMA((6,)),
        ],
        compiler_params=pltpu.CompilerParams(vmem_limit_bytes=60 * MIB),
        cost_estimate=pl.CostEstimate(flops=10 ** 10, bytes_accessed=14 * 10 ** 6, transcendentals=0),
        name="attn_fwd",
    )(x_a, x_b, n1, n2, wq, wk, wv, wo)


def attn_bwd_kernel(kv_heads, reps, dim, s0, s1, t0, dy, h_b, x_b, nb, qkv, ctx, n1, n2, wo_h, wq_h, wk_h, wv_h,
                    dx, gq, gk, gv, go, gn1, gn2,
                    wo, wq, wk, wv, oq, ok, ov, oo, dctx, dq, dk, dv, sems, osems):
    copies = [pltpu.make_async_copy(s, d, sems.at[i]) for i, (s, d) in enumerate(((wo_h, wo), (wq_h, wq), (wk_h, wk), (wv_h, wv)))]
    for c in copies:
        c.start()
    tokens = x_b.shape[0]
    q_dim, kv_dim = kv_heads * reps * dim, kv_heads * dim
    du = ((s0[...] + s1[...]) + t0[...]).astype(BF).astype(F32)
    grad_h, g2 = rms_pull(h_b[...].astype(F32), row_of(n2), du)
    gn2[...] = g2
    dh = (dy[...].astype(F32) + grad_h).astype(BF)
    copies[0].wait()
    outs = []

    def flush(src, dst):
        c = pltpu.make_async_copy(src, dst, osems.at[len(outs)])
        c.start()
        outs.append(c)

    step = q_dim // 4
    for i in range(4):
        dctx[i * step:(i + 1) * step] = nt(wo[i * step:(i + 1) * step], dh).astype(BF)
    for i in range(4):
        part = slice(i * step, (i + 1) * step)
        oo[part] = nn(ctx[part], dh).astype(BF).astype(F32)
        flush(oo.at[part], go.at[part])
    every = slice(0, tokens)
    normed = nb[...]
    for g in range(kv_heads):
        kv = slice(g * dim, (g + 1) * dim)
        kg = qkv[q_dim + g * dim:q_dim + (g + 1) * dim]
        vg = qkv[q_dim + kv_dim + g * dim:q_dim + kv_dim + (g + 1) * dim]
        qg = heads_to_lanes(qkv, g, reps, dim, every)
        dg = heads_to_lanes(dctx, g, reps, dim, every)
        probs = probs_of(tn(kg, qg) * dim ** -0.5)
        dprobs = tn(vg, dg).astype(BF).astype(F32)
        weighted = probs * dprobs
        dscores = ((weighted - probs * jnp.sum(weighted, axis=0, keepdims=True)) * dim ** -0.5).astype(BF)
        dv[kv] = nt(dg, probs.astype(BF)).astype(BF)
        dk[kv] = nt(qg, dscores).astype(BF)
        dqg = nn(kg, dscores).astype(BF)
        for r in range(reps):
            dq[(g * reps + r) * dim:(g * reps + r + 1) * dim] = dqg[:, r * tokens:(r + 1) * tokens]
        if g % 2 == 1:
            part = slice((g - 1) * reps * dim, (g + 1) * reps * dim)
            oq[part] = nn(dq[part], normed).astype(BF).astype(F32)
            flush(oq.at[part], gq.at[part])
    ok[...] = nn(dk[...], normed).astype(BF).astype(F32)
    flush(ok, gk)
    ov[...] = nn(dv[...], normed).astype(BF).astype(F32)
    flush(ov, gv)
    for c in copies[1:]:
        c.wait()
    dn = (tn(dq[...], wq[...]) + tn(dk[...], wk[...]) + tn(dv[...], wv[...])).astype(BF).astype(F32)
    grad_x, g1 = rms_pull(x_b[...].astype(F32), row_of(n1), dn)
    gn1[...] = g1
    dx[...] = (dh.astype(F32) + grad_x).astype(BF)
    for c in outs:
        c.wait()


def attn_bwd(s0, s1, t0, dy, h_b, x_b, nb, qkv, ctx, n1, n2, wo, wq, wk, wv, kv_heads, reps, dim):
    tokens, model = x_b.shape
    q_dim, kv_dim = kv_heads * reps * dim, kv_heads * dim
    vm = pl.BlockSpec(memory_space=pltpu.VMEM)
    hb = pl.BlockSpec(memory_space=pl.ANY)
    n_out = 4 + kv_heads // 2 + 2
    return pl.pallas_call(
        functools.partial(attn_bwd_kernel, kv_heads, reps, dim),
        out_shape=(
            jax.ShapeDtypeStruct((tokens, model), BF), jax.ShapeDtypeStruct((q_dim, model), F32), jax.ShapeDtypeStruct((kv_dim, model), F32),
            jax.ShapeDtypeStruct((kv_dim, model), F32), jax.ShapeDtypeStruct((q_dim, model), F32), jax.ShapeDtypeStruct((1, model), F32), jax.ShapeDtypeStruct((1, model), F32),
        ),
        in_specs=[vm] * 11 + [hb] * 4,
        out_specs=(vm, hb, hb, hb, hb, vm, vm),
        scratch_shapes=[
            pltpu.VMEM((q_dim, model), BF), pltpu.VMEM((q_dim, model), BF), pltpu.VMEM((kv_dim, model), BF), pltpu.VMEM((kv_dim, model), BF),
            pltpu.VMEM((q_dim, model), F32), pltpu.VMEM((kv_dim, model), F32), pltpu.VMEM((kv_dim, model), F32), pltpu.VMEM((q_dim, model), F32),
            pltpu.VMEM((q_dim, tokens), BF), pltpu.VMEM((q_dim, tokens), BF), pltpu.VMEM((kv_dim, tokens), BF), pltpu.VMEM((kv_dim, tokens), BF),
            pltpu.SemaphoreType.DMA((4,)), pltpu.SemaphoreType.DMA((n_out,)),
        ],
        compiler_params=pltpu.CompilerParams(vmem_limit_bytes=60 * MIB),
        cost_estimate=pl.CostEstimate(flops=14 * 10 ** 9, bytes_accessed=40 * 10 ** 6, transcendentals=0),
        name="attn_bwd",
    )(s0, s1, t0, dy, h_b, x_b, nb, qkv, ctx, n1, n2, wo, wq, wk, wv)


def route_rows(info, base, expert):
    group, _, width = info.shape
    tokens = width // 3
    top_k = info.shape[1] // 2
    wide = [info[r].astype(F32)[base * top_k:(base + 1) * top_k] for r in range(group)]

    def field(i):
        return jnp.concatenate([w[:, i * tokens:(i + 1) * tokens] for w in wide], axis=1)

    eid, slot, gate = field(0), field(1), field(2)
    hit = (eid == expert.astype(F32)) & (slot >= 0.0)
    slot_row = jnp.sum(jnp.where(hit, slot + 1.0, 0.0), axis=0, keepdims=True) - 1.0
    gate_row = jnp.sum(jnp.where(hit, gate, 0.0), axis=0, keepdims=True)
    return slot_row, gate_row


def places(slot_row, group):
    tokens = slot_row.shape[1] // group
    kept = jnp.where(slot_row >= 0.0, 1.0, 0.0)
    start = jnp.zeros((1, 1), F32)
    starts = []
    for r in range(group):
        starts.append(jnp.broadcast_to(start, (1, tokens)))
        start = start + jnp.sum(kept[:, r * tokens:(r + 1) * tokens], axis=1, keepdims=True)
    place_row = jnp.where(slot_row >= 0.0, slot_row + jnp.concatenate(starts, axis=1), -1.0).astype(jnp.int32)
    return place_row, jnp.sum(kept)


def hits(place_row, first):
    return lax.broadcasted_iota(jnp.int32, (CHUNK, place_row.shape[1]), 0) + first == place_row


def ring_copies(pairs, sem, idx, ring):
    s = lax.rem(idx, ring)
    return [pltpu.make_async_copy(src.at[idx], dst.at[s], sem.at[s, i]) for i, (src, dst) in enumerate(pairs)]


def row_copies(refs, rows, sem):
    tokens = rows.shape[0] // len(refs)
    return [pltpu.make_async_copy(ref.at[0:tokens], rows.at[r * tokens:(r + 1) * tokens], sem.at[r]) for r, ref in enumerate(refs)]


def info_copies(refs, info, sem):
    _, depth, width = info.shape
    first = refs[0].shape[0] - depth
    return [pltpu.make_async_copy(ref.at[first:first + depth, 0:width], info.at[r], sem.at[len(refs) + r]) for r, ref in enumerate(refs)]


def part_copies(acc, refs, sem):
    tokens = acc.shape[0] // len(refs)
    return [pltpu.make_async_copy(acc.at[r * tokens:(r + 1) * tokens], ref, sem.at[r]) for r, ref in enumerate(refs)]


def start_all(copies):
    for c in copies:
        c.start()


def wait_all(copies):
    for c in copies:
        c.wait()


def mix_into(acc, pick, outs):
    for n in range(acc.shape[1] // 256):
        part = slice(n * 256, (n + 1) * 256)
        acc[:, part] += nn(pick, outs[:, part])


def expert_bwd_kernel(capacity, d0, d1, d2, d3, u_h, w1_h, w2_h, w3_h,
                      g1, g2, g3, p0, p1, p2, p3,
                      rows, info, us, w1s, w2s, w3s, pick, du_two, d_out, hid, da1, da3, o1, o2, o3, acc, rsem, wsem, sems, psem):
    e = pl.program_id(0)
    count = pl.num_programs(0)
    me = lax.axis_index('expert')
    slot_e = lax.rem(e, 2)
    ring, cols, model = us.shape
    tokens = rows.shape[0] // 4
    ff = w1s.shape[2]
    padded = du_two.shape[0] // 2
    heads = (d0, d1, d2, d3)
    arrivals = info_copies(heads, info, rsem) + row_copies(heads, rows, rsem)
    pairs = ((u_h, us), (w1_h, w1s), (w3_h, w3s), (w2_h, w2s))

    @pl.when(e == 0)
    def _():
        start_all(arrivals + ring_copies(pairs, wsem, 0, ring) + ring_copies(pairs, wsem, 1, ring))
        acc[...] = jnp.zeros_like(acc)
        du_two[...] = jnp.zeros_like(du_two)
        wait_all(arrivals)

    @pl.when(e + 2 < count)
    def _():
        start_all(ring_copies(pairs, wsem, e + 2, ring))

    slot_row, gate_row = route_rows(info, 1, me * count + e)
    device = jnp.bitwise_xor(lax.broadcasted_iota(jnp.int32, slot_row.shape, 1) // tokens, me)
    col_row = jnp.where(slot_row >= 0.0, slot_row.astype(jnp.int32) + device * capacity, -1)
    hot = lax.broadcasted_iota(jnp.int32, (padded, 4 * tokens), 0) == col_row
    pick[:, pl.ds(pl.multiple_of(slot_e * padded, padded), padded)] = jnp.transpose(jnp.where(hot, 1.0, 0.0).astype(BF))
    d_out[...] = nn(jnp.where(hot, gate_row, 0.0).astype(BF)[0:cols], rows[...]).astype(BF)

    def flush(idx):
        s = lax.rem(idx, 2)
        return [pltpu.make_async_copy(src.at[s], dst.at[idx], sems.at[s, i]) for i, (src, dst) in enumerate(((o1, g1), (o2, g2), (o3, g3)))]

    wait_all(ring_copies(pairs, wsem, e, ring))
    now = lax.rem(e, ring)
    u, w1, w2, w3 = us.at[now], w1s.at[now], w2s.at[now], w3s.at[now]
    uv = u[...]
    dov = d_out[...]
    for n in range(ff // 256):
        part = slice(n * 256, (n + 1) * 256)
        pre1 = nn(uv, w1[:, part]).astype(BF).astype(F32)
        pre3 = nn(uv, w3[:, part]).astype(BF).astype(F32)
        grad_hid = nt(dov, w2[part, :]).astype(BF).astype(F32)
        sigma = jax.nn.sigmoid(pre1)
        silu = pre1 * sigma
        hid[:, part] = (silu * pre3).astype(BF)
        da1[:, part] = (grad_hid * pre3 * sigma * (1.0 + pre1 * (1.0 - sigma))).astype(BF)
        da3[:, part] = (grad_hid * silu).astype(BF)

    @pl.when(e >= 2)
    def _():
        wait_all(flush(e - 2))

    fresh = flush(e)
    for m in range(ff // 256):
        part = slice(m * 256, (m + 1) * 256)
        o2[slot_e, part] = tn(hid[:, part], dov)
    fresh[1].start()
    for m in range(model // 256):
        part = slice(m * 256, (m + 1) * 256)
        o1[slot_e, part] = tn(u[:, part], da1[...])
        o3[slot_e, part] = tn(u[:, part], da3[...])
    fresh[0].start()
    fresh[2].start()
    live = pl.ds(pl.multiple_of(slot_e * padded, padded), cols)
    for n in range(model // 256):
        part = slice(n * 256, (n + 1) * 256)
        du_two[live, part] = (nt(da1[...], w1[part]) + nt(da3[...], w3[part])).astype(BF)

    @pl.when(slot_e == 1)
    def _():
        mix_into(acc, pick[...], du_two)

    @pl.when(e == count - 1)
    def _():
        sends = part_copies(acc, (p0, p1, p2, p3), psem)
        start_all(sends)
        wait_all(flush(e - 1))
        wait_all(flush(e))
        wait_all(sends)


def expert_bwd(dys, u, w1, w2, w3, tokens):
    model = dys[0].shape[1]
    count, cols, _ = u.shape
    ff = w1.shape[2]
    padded, ring = 256, 3
    hb = pl.BlockSpec(memory_space=pl.ANY)
    part = jax.ShapeDtypeStruct((tokens, model), F32)
    return pl.pallas_call(
        functools.partial(expert_bwd_kernel, cols // 4),
        grid=(count,),
        out_shape=(jax.ShapeDtypeStruct((count, model, ff), F32), jax.ShapeDtypeStruct((count, ff, model), F32), jax.ShapeDtypeStruct((count, model, ff), F32), part, part, part, part),
        in_specs=[hb] * 8,
        out_specs=(hb,) * 7,
        scratch_shapes=[
            pltpu.VMEM((4 * tokens, model), BF), pltpu.VMEM((4, dys[0].shape[0] - tokens, 3 * tokens), BF),
            pltpu.VMEM((ring, cols, model), BF), pltpu.VMEM((ring, model, ff), BF), pltpu.VMEM((ring, ff, model), BF), pltpu.VMEM((ring, model, ff), BF),
            pltpu.VMEM((4 * tokens, 2 * padded), BF), pltpu.VMEM((2 * padded, model), BF),
            pltpu.VMEM((cols, model), BF), pltpu.VMEM((cols, ff), BF), pltpu.VMEM((cols, ff), BF), pltpu.VMEM((cols, ff), BF),
            pltpu.VMEM((2, model, ff), F32), pltpu.VMEM((2, ff, model), F32), pltpu.VMEM((2, model, ff), F32),
            pltpu.VMEM((4 * tokens, model), F32),
            pltpu.SemaphoreType.DMA((8,)), pltpu.SemaphoreType.DMA((ring, 4)), pltpu.SemaphoreType.DMA((2, 3)), pltpu.SemaphoreType.DMA((4,)),
        ],
        compiler_params=pltpu.CompilerParams(vmem_limit_bytes=60 * MIB, dimension_semantics=("arbitrary",)),
        cost_estimate=pl.CostEstimate(flops=50 * 10 ** 9, bytes_accessed=150 * 10 ** 6, transcendentals=0),
        name="expert_bwd",
    )(*dys, u, w1, w2, w3)


def expert_fwd_kernel(u0, u1, u2, u3, d0, d1, d2, d3, w1_h, w2_h, w3_h, p0, p1, p2, p3,
                      rows, info, w1s, w2s, w3s, pick, out_two, acc, late_t, rsem, wsem, psem):
    e = pl.program_id(0)
    count = pl.num_programs(0)
    me = lax.axis_index('expert')
    ring, _, ff = w1s.shape
    slot_e = lax.rem(e, 2)
    arrivals = info_copies((d0, d1, d2, d3), info, rsem) + row_copies((u0, u1, u2, u3), rows, rsem)
    pairs = ((w1_h, w1s), (w3_h, w3s), (w2_h, w2s))

    @pl.when(e == 0)
    def _():
        start_all(arrivals + ring_copies(pairs, wsem, 0, ring) + ring_copies(pairs, wsem, 1, ring))
        acc[...] = jnp.zeros_like(acc)
        wait_all(arrivals)

    @pl.when(e + 2 < count)
    def _():
        start_all(ring_copies(pairs, wsem, e + 2, ring))

    slot_row, gate_row = route_rows(info, 0, me * count + e)
    place_row, filled = places(slot_row, 4)
    wait_all(ring_copies(pairs, wsem, e, ring))
    now = lax.rem(e, ring)
    w1, w2, w3 = w1s.at[now], w2s.at[now], w3s.at[now]

    def run(first):
        hot = hits(place_row, first)
        v = nn(jnp.where(hot, 1.0, 0.0).astype(BF), rows[...]).astype(BF)
        pieces = []
        for n in range(ff // 256):
            part = slice(n * 256, (n + 1) * 256)
            a1 = nn(v, w1[:, part]).astype(BF).astype(F32)
            a3 = nn(v, w3[:, part]).astype(BF).astype(F32)
            pieces.append((a1 * jax.nn.sigmoid(a1) * a3).astype(BF))
        hidden = jnp.concatenate(pieces, axis=1)
        return jnp.transpose(jnp.where(hot, gate_row, 0.0).astype(BF)), nn(hidden, w2[...]).astype(BF)

    chosen, out = run(0)
    half = pl.ds(pl.multiple_of(slot_e * CHUNK, CHUNK), CHUNK)
    pick[:, half] = chosen
    out_two[half, :] = out

    @pl.when(filled > float(CHUNK))
    def _():
        more, out_more = run(CHUNK)
        late_t[...] = more
        mix_into(acc, late_t[...], out_more)

    @pl.when(slot_e == 1)
    def _():
        mix_into(acc, pick[...], out_two)

    @pl.when(e == count - 1)
    def _():
        sends = part_copies(acc, (p0, p1, p2, p3), psem)
        start_all(sends)
        wait_all(sends)


def expert_fwd(us, dys, w1, w2, w3):
    tokens, model = us[0].shape
    count, _, ff = w1.shape
    ring = 3
    part = jax.ShapeDtypeStruct((tokens, model), F32)
    hb = pl.BlockSpec(memory_space=pl.ANY)
    return pl.pallas_call(
        expert_fwd_kernel,
        grid=(count,),
        out_shape=(part, part, part, part),
        in_specs=[hb] * 11,
        out_specs=(hb,) * 4,
        scratch_shapes=[
            pltpu.VMEM((4 * tokens, model), BF), pltpu.VMEM((4, dys[0].shape[0] - tokens, 3 * tokens), BF),
            pltpu.VMEM((ring, model, ff), BF), pltpu.VMEM((ring, ff, model), BF), pltpu.VMEM((ring, model, ff), BF),
            pltpu.VMEM((4 * tokens, 2 * CHUNK), BF), pltpu.VMEM((2 * CHUNK, model), BF),
            pltpu.VMEM((4 * tokens, model), F32), pltpu.VMEM((4 * tokens, CHUNK), BF),
            pltpu.SemaphoreType.DMA((8,)), pltpu.SemaphoreType.DMA((ring, 3)), pltpu.SemaphoreType.DMA((4,)),
        ],
        compiler_params=pltpu.CompilerParams(vmem_limit_bytes=60 * MIB, dimension_semantics=("arbitrary",)),
        cost_estimate=pl.CostEstimate(flops=16 * 10 ** 9, bytes_accessed=50 * 10 ** 6, transcendentals=0),
        name="expert_fwd",
    )(*us, *dys, w1, w2, w3)


def pack_kernel(dy, *refs):
    out = refs[-1]
    tokens = dy.shape[0]
    fields = [r[...].astype(F32) for r in refs[:-1]]
    both = jnp.concatenate([jnp.concatenate(fields[0:3], axis=1), jnp.concatenate(fields[3:6], axis=1)], axis=0)
    out[0:tokens] = dy[...]
    out[tokens:] = jnp.concatenate([both, jnp.zeros((both.shape[0], dy.shape[1] - both.shape[1]), F32)], axis=1).astype(BF)


def pack(dy, fields):
    vm = pl.BlockSpec(memory_space=pltpu.VMEM)
    depth = 2 * fields[0].shape[0]
    return pl.pallas_call(
        pack_kernel,
        out_shape=jax.ShapeDtypeStruct((dy.shape[0] + depth, dy.shape[1]), BF),
        in_specs=[vm] * 7, out_specs=vm,
        compiler_params=pltpu.CompilerParams(vmem_limit_bytes=60 * MIB),
        name="pack",
    )(dy, *fields)


def solution(mesh):
    group = mesh.shape['expert']

    def hop(value, bits):
        return lax.ppermute(value, 'expert', [(i, i ^ bits) for i in range(group)])

    def local_step(x_a, x_b, dy_b, eid_a, slot_a, gate_a, eid_b, slot_b, gate_b, u_b, norm_1, norm_2, w_q, w_k, w_v, w_o, w_1, w_2, w_3):
        model, heads, dim = w_q.shape
        kv_heads = w_k.shape[1]
        reps = heads // kv_heads
        load = pack(dy_b, [a.T for a in (eid_a, slot_a, gate_a, eid_b, slot_b, gate_b)])
        dy2 = hop(load, 2)
        dy1 = hop(load, 1)
        wq_t, wk_t, wv_t = (w.transpose(1, 2, 0).reshape(-1, model) for w in (w_q, w_k, w_v))
        wo = w_o.reshape(-1, model)
        h_a, u_a, h_b, nb, qkv_b, ctx_b = attn_fwd(x_a, x_b, norm_1, norm_2, wq_t, wk_t, wv_t, wo, kv_heads, reps, dim)
        dys = (load, dy1, dy2, hop(dy2, 1))
        us = (u_a, hop(u_a, 1), hop(u_a, 2), hop(u_a, 3))
        g1, g2, g3, b0, b1, b2, b3 = expert_bwd(dys, u_b, w_1, w_2, w_3, x_a.shape[0])
        far_b = hop(b2 + hop(b3, 1), 2)
        near_b = hop(b1, 1)
        a0, a1, a2, a3 = expert_fwd(us, dys, w_1, w_2, w_3)
        far_a = hop(a2 + hop(a3, 1), 2)
        near_a = hop(a1, 1)
        dx_b, g_q, g_k, g_v, g_o, g_n1, g_n2 = attn_bwd(b0, near_b, far_b, dy_b, h_b, x_b, nb, qkv_b, ctx_b, norm_1, norm_2, wo, wq_t, wk_t, wv_t, kv_heads, reps, dim)
        y_a = (h_a.astype(F32) + ((a0 + near_a) + far_a)).astype(BF)
        g_q = g_q.reshape(heads, dim, model).transpose(2, 0, 1)
        g_k = g_k.reshape(kv_heads, dim, model).transpose(2, 0, 1)
        g_v = g_v.reshape(kv_heads, dim, model).transpose(2, 0, 1)
        g_o = g_o.reshape(heads, dim, model)
        return (y_a, dx_b, g1, g2, g3, g_q[None], g_k[None], g_v[None], g_o[None], g_n1, g_n2)

    row_spec = P(('data', 'expert'), None)
    cube_spec = P(('data', 'expert'), None, None)
    quad_spec = P(('data', 'expert'), None, None, None)
    expert_spec = P('expert', None, None)
    in_specs = (row_spec, row_spec, row_spec, row_spec, row_spec, row_spec, row_spec, row_spec, row_spec, cube_spec, P(), P(), P(), P(), P(), P(), expert_spec, expert_spec, expert_spec)
    out_specs = (row_spec, row_spec, cube_spec, cube_spec, cube_spec, quad_spec, quad_spec, quad_spec, quad_spec, row_spec, row_spec)
    return jax.shard_map(local_step, mesh=mesh, in_specs=in_specs, out_specs=out_specs, check_vma=False)
```

time: 189 us -> 185 us (0.979)
  local copies, waits for them, and re-layouts: 19.4 us -> 2.69 us
  Pallas kernels: 99.6 us -> 108 us
  waiting for transfers between devices: 55.2 us -> 59.2 us
  starting transfers between devices: 9.13 us -> 11.2 us
    unnamed x68 -> x24, local copies, waits for them, and re-layouts: 19.4 us -> 2.69 us
    ppermute x15 -> x12, waiting for transfers between devices: 55.2 us -> 59.2 us  [hop(): return lax.ppermute(value, 'expert', [(i, i ^ bits) for i in range(group)])]
    pallas_call x1, Pallas kernels: 10.2 us -> 13.4 us  [attn_fwd(): pl.pallas_call(functools.partial(attn_fwd_kernel, kv_heads, reps, dim), o...]
    pallas_call x1, Pallas kernels: 13.6 us -> 15.7 us  [attn_bwd(): pl.pallas_call(functools.partial(attn_bwd_kernel, kv_heads, reps, dim), o...]
    ppermute x15 -> x12, starting transfers between devices: 9.13 us -> 11.2 us  [hop(): return lax.ppermute(value, 'expert', [(i, i ^ bits) for i in range(group)])]
  transfers between devices with their start and end apart: 15 -> 12, of which waited for: 6 -> 5; matrix products, arithmetic and copies ran while one was open for 2% -> 1% of each run, Pallas kernels for 46% -> 38%
where the time goes in v2:
time: 185 us
  Pallas kernels  108 us (58%)
  waiting for transfers between devices  59.2 us (32%)
  starting transfers between devices  11.2 us (6%)
  local copies, waits for them, and re-layouts  2.69 us (1%)
  other arithmetic  2.31 us (1%)
    ppermute x12, waiting for transfers between devices, hop(): return lax.ppermute(value, 'expert', [(i, i ^ bits) for i in range(group)])  59.2 us
    pallas_call x1, Pallas kernels, expert_bwd(): pl.pallas_call(functools.partial(expert_bwd_kernel, cols // 4), grid=(cou...  56.5 us
    pallas_call x1, Pallas kernels, expert_fwd(): pl.pallas_call(expert_fwd_kernel, grid=(count,), out_shape=(part, part, p...  20.9 us
    pallas_call x1, Pallas kernels, attn_bwd(): pl.pallas_call(functools.partial(attn_bwd_kernel, kv_heads, reps, dim), o...  15.7 us
    pallas_call x1, Pallas kernels, attn_fwd(): pl.pallas_call(functools.partial(attn_fwd_kernel, kv_heads, reps, dim), o...  13.4 us
    ppermute x12, starting transfers between devices, hop(): return lax.ppermute(value, 'expert', [(i, i ^ bits) for i in range(group)])  11.2 us
  transfers between devices with their start and end apart: 12, of which 5 were waited for; matrix products, arithmetic and copies ran while one was open for 1% of the time, Pallas kernels for 38%

profile of v2, /device:TPU:0, one launch (start us, length us, event | category | flops | bytes accessed | tf_op | source)
XLA Modules:
  0.0 184.7 jit_solution(6289703084903942505)
XLA Ops:
  0.6 1.9 %pack.1.d0 = bf16[144,1536]{1,0:T(8,128)(2,1)} custom-call(bf16[128,1536]{1,0:T(8,128)(2,1)} %dy.3, s32[8,128]{1,0:T(8,128)} %bitcast.32, s32[8,128]{1,0:T(8,128)} %bitcast.33, bf16[8,128]{1,0:T(8,128)(2,1)} %bitcast.36, s32[8,128]{1,0:T(8,128)} %bitcast.34, s32[8,128]{1,0:T(8,128)} %bitcast.35, bf16[8,128]{1,0:T(8,128)(2,1)} %bitcast.37), custom_call_target="tpu_custom_call" | custom-call | tf_op jit(solution)/shard_map/pack/pallas_call | solution.py:512
  2.5 3.3 %collective-permute-start.4 = (bf16[144,1536]{1,0:T(8,128)(2,1)}, bf16[144,1536]{1,0:T(8,128)(2,1)S(1)}, u32[]{:S(2)}, u32[]{:S(2)}) collective-permute-start(bf16[144,1536]{1,0:T(8,128)(2,1)} %pack.1.d0), channel_id=1, source_target_pairs={{0,2},{1,3},{2,0},{3,1},{4,6},{5,7},{6,4},{7,5}} | collective-permute-start | bytes 1327112 | tf_op jit(solution)/shard_map/ppermute | solution.py:525
  5.8 10.4 %collective-permute-done.4.d2 = bf16[144,1536]{1,0:T(8,128)(2,1)S(1)} collective-permute-done((bf16[144,1536]{1,0:T(8,128)(2,1)}, bf16[144,1536]{1,0:T(8,128)(2,1)S(1)}, u32[]{:S(2)}, u32[]{:S(2)}) %collective-permute-start.4) | collective-permute-done | bytes 442400 | tf_op jit(solution)/shard_map/ppermute | solution.py:525
  16.2 13.4 %attn_fwd.1 = (bf16[128,1536]{1,0:T(8,128)(2,1)}, bf16[128,1536]{1,0:T(8,128)(2,1)}, bf16[128,1536]{1,0:T(8,128)(2,1)}, bf16[128,1536]{1,0:T(8,128)(2,1)}, bf16[...) custom-call(bf16[128,1536]{1,0:T(8,128)(2,1)} %xa_h.1, bf16[128,1536]{1,0:T(8,128)(2,1)} %x_b.1, bf16[1536]{0:T(1024)(128)(2,1)} %n1.3, ...), custom_call_target="tpu_custom_call" | custom-call | flops 10000000000 | bytes 14000000 | tf_op jit(solution)/shard_map/attn_fwd/pallas_call | solution.py:125
  29.6 1.8 collective-permute-start.2
  31.4 0.3 collective-permute-start.1
  31.7 9.5 %collective-permute-done.2.u3 = bf16[128,1536]{1,0:T(8,128)(2,1)S(1)} collective-permute-done((bf16[128,1536]{1,0:T(8,128)(2,1)}, bf16[128,1536]{1,0:T(8,128)(2,1)S(1)}, u32[]{:S(2)}, u32[]{:S(2)}) %collective-permute-start.2) | collective-permute-done | bytes 393248 | tf_op jit(solution)/shard_map/ppermute | solution.py:525
  41.3 8.5 %collective-permute-done.1.u2 = bf16[128,1536]{1,0:T(8,128)(2,1)S(1)} collective-permute-done((bf16[128,1536]{1,0:T(8,128)(2,1)}, bf16[128,1536]{1,0:T(8,128)(2,1)S(1)}, u32[]{:S(2)}, u32[]{:S(2)}) %collective-permute-start.1) | collective-permute-done | bytes 393248 | tf_op jit(solution)/shard_map/ppermute | solution.py:525
  49.8 0.7 copy-done.10
  50.6 0.1 copy-done.7
  50.8 0.8 copy-done.8
  51.5 20.9 %expert_fwd.1 = (f32[128,1536]{1,0:T(8,128)}, f32[128,1536]{1,0:T(8,128)}, f32[128,1536]{1,0:T(8,128)}, f32[128,1536]{1,0:T(8,128)}) custom-call(bf16[128,1536]{1,0:T(8,128)(2,1)} %get-tuple-element.36.u0, bf16[128,1536]{1,0:T(8,128)(2,1)} %copy-done.11, bf16[128,1536]{1,0:T(8,128)(2,1)} %copy-done.10, bf16[128,1536]{1,0:T(8,128)(2,1)} %copy-done.9, ...), custom_call_target="tpu_custom_call" | custom-call | flops 16000000000 | bytes 50000000 | tf_op jit(solution)/shard_map/expert_fwd/pallas_call | solution.py:481
  72.5 1.1 collective-permute-start.7
  73.6 56.5 %expert_bwd.1 = (f32[10,1536,512]{2,1,0:T(8,128)}, f32[10,512,1536]{2,1,0:T(8,128)}, f32[10,1536,512]{2,1,0:T(8,128)}, f32[128,1536]{1,0:T(8,128)}, f32[128,1536...) custom-call(bf16[144,1536]{1,0:T(8,128)(2,1)} %pack.1.d0, bf16[144,1536]{1,0:T(8,128)(2,1)} %copy-done.7, ...), custom_call_target="tpu_custom_call" | custom-call | flops 49999998976 | bytes 150000000 | tf_op jit(solution)/shard_map/expert_bwd/pallas_call | solution.py:394
  130.1 0.2 collective-permute-start.10
  130.2 0.4 collective-permute-start.6
  130.7 2.3 %collective-permute-start.8 = (f32[128,1536]{1,0:T(8,128)S(1)}, f32[128,1536]{1,0:T(8,128)S(1)}, u32[]{:S(2)}, u32[]{:S(2)}) collective-permute-start(f32[128,1536]{1,0:T(8,128)S(1)} %add.16), channel_id=1, source_target_pairs={{0,2},{1,3},{2,0},{3,1},{4,6},{5,7},{6,4},{7,5}} | collective-permute-start | bytes 2359304 | tf_op jit(solution)/shard_map/ppermute | solution.py:525
  133.1 1.2 add.19
  134.3 1.8 collective-permute-start.11
  136.1 15.3 %collective-permute-done.8 = f32[128,1536]{1,0:T(8,128)S(1)} collective-permute-done((f32[128,1536]{1,0:T(8,128)S(1)}, f32[128,1536]{1,0:T(8,128)S(1)}, u32[]{:S(2)}, u32[]{:S(2)}) %collective-permute-start.8) | collective-permute-done | bytes 786464 | tf_op jit(solution)/shard_map/ppermute | solution.py:525
  151.4 1.0 add_convert_fusion
  152.4 15.5 %collective-permute-done.11.t0 = f32[128,1536]{1,0:T(8,128)S(1)} collective-permute-done((f32[128,1536]{1,0:T(8,128)S(1)}, f32[128,1536]{1,0:T(8,128)S(1)}, u32[]{:S(2)}, u32[]{:S(2)}) %collective-permute-start.11) | collective-permute-done | bytes 786464 | tf_op jit(solution)/shard_map/ppermute | solution.py:525
  167.9 0.9 copy-done.5
  168.8 15.7 %attn_bwd.1 = (bf16[128,1536]{1,0:T(8,128)(2,1)}, f32[1536,1536]{1,0:T(8,128)}, f32[512,1536]{1,0:T(8,128)}, f32[512,1536]{1,0:T(8,128)}, f32[1536,1536]{1,0:T(8...) custom-call(f32[128,1536]{1,0:T(8,128)} %get-tuple-element.41.s0, f32[128,1536]{1,0:T(8,128)} %copy-done.4, ...), custom_call_target="tpu_custom_call" | custom-call | flops 14000000000 | bytes 40000000 | tf_op jit(solution)/shard_map/attn_bwd/pallas_call | solution.py:212
  (32 shorter events, 0.4 us)
Async XLA Ops:
  2.5 13.7 %collective-permute-start.4 = (bf16[144,1536]{1,0:T(8,128)(2,1)}, bf16[144,1536]{1,0:T(8,128)(2,1)S(1)}, u32[]{:S(2)}, u32[]{:S(2)}) collective-permute-start(bf16[144,1536]{1,0:T(8,128)(2,1)} %pack.1.d0), channel_id=1, source_target_pairs={{0,2},{1,3},{2,0},{3,1},{4,6},{5,7},{6,4},{7,5}} | collective-permute-start | bytes 1327112 | tf_op jit(solution)/shard_map/ppermute | solution.py:525
  5.8 43.9 %collective-permute-start.3 = (bf16[144,1536]{1,0:T(8,128)(2,1)}, bf16[144,1536]{1,0:T(8,128)(2,1)S(1)}, u32[]{:S(2)}, u32[]{:S(2)}) collective-permute-start(bf16[144,1536]{1,0:T(8,128)(2,1)} %pack.1.d0), channel_id=1, source_target_pairs={{0,1},{1,0},{2,3},{3,2},{4,5},{5,4},{6,7},{7,6}} | collective-permute-start | bytes 1327112 | tf_op jit(solution)/shard_map/ppermute | solution.py:525
  16.2 13.4 %copy-start.6 = (bf16[144,1536]{1,0:T(8,128)(2,1)}, bf16[144,1536]{1,0:T(8,128)(2,1)S(1)}, u32[]{:S(2)}) copy-start(bf16[144,1536]{1,0:T(8,128)(2,1)S(1)} %collective-permute-done.4.d2) | copy-start | bytes 1327108
  16.2 33.6 %collective-permute-start.5 = (bf16[144,1536]{1,0:T(8,128)(2,1)S(1)}, bf16[144,1536]{1,0:T(8,128)(2,1)S(1)}, u32[]{:S(2)}, u32[]{:S(2)}) collective-permute-start(bf16[144,1536]{1,0:T(8,128)(2,1)S(1)} %collective-permute-done.4.d2), channel_id=1, source_target_pairs={{0,1},{1,0},{2,3},{3,2},{4,5},{5,4},{6,7},{7,6}} | collective-permute-start | bytes 1327112 | tf_op jit(solution)/shard_map/ppermute | solution.py:525
  29.6 11.6 %collective-permute-start.2 = (bf16[128,1536]{1,0:T(8,128)(2,1)}, bf16[128,1536]{1,0:T(8,128)(2,1)S(1)}, u32[]{:S(2)}, u32[]{:S(2)}) collective-permute-start(bf16[128,1536]{1,0:T(8,128)(2,1)} %get-tuple-element.36.u0), channel_id=1, source_target_pairs={{0,3},{1,2},{2,1},{3,0},{4,7},{5,6},{6,5},{7,4}} | collective-permute-start | bytes 1179656 | tf_op jit(solution)/shard_map/ppermute | solution.py:525
  31.4 18.3 %collective-permute-start.1 = (bf16[128,1536]{1,0:T(8,128)(2,1)}, bf16[128,1536]{1,0:T(8,128)(2,1)S(1)}, u32[]{:S(2)}, u32[]{:S(2)}) collective-permute-start(bf16[128,1536]{1,0:T(8,128)(2,1)} %get-tuple-element.36.u0), channel_id=1, source_target_pairs={{0,2},{1,3},{2,0},{3,1},{4,6},{5,7},{6,4},{7,5}} | collective-permute-start | bytes 1179656 | tf_op jit(solution)/shard_map/ppermute | solution.py:525
  31.7 18.0 %collective-permute-start = (bf16[128,1536]{1,0:T(8,128)(2,1)}, bf16[128,1536]{1,0:T(8,128)(2,1)S(1)}, u32[]{:S(2)}, u32[]{:S(2)}) collective-permute-start(bf16[128,1536]{1,0:T(8,128)(2,1)} %get-tuple-element.36.u0), channel_id=1, source_target_pairs={{0,1},{1,0},{2,3},{3,2},{4,5},{5,4},{6,7},{7,6}} | collective-permute-start | bytes 1179656 | tf_op jit(solution)/shard_map/ppermute | solution.py:525
  41.2 8.5 %copy-start.9 = (bf16[128,1536]{1,0:T(8,128)(2,1)}, bf16[128,1536]{1,0:T(8,128)(2,1)S(1)}, u32[]{:S(2)}) copy-start(bf16[128,1536]{1,0:T(8,128)(2,1)S(1)} %collective-permute-done.2.u3) | copy-start | bytes 1179652
  49.7 0.7 copy-start.10
  49.7 0.9 copy-start.11
  49.8 1.0 copy-start.7
  50.8 0.8 copy-start.8
  72.5 57.8 %copy-start.3 = (f32[128,1536]{1,0:T(8,128)S(1)}, f32[128,1536]{1,0:T(8,128)}, u32[]{:S(2)}) copy-start(f32[128,1536]{1,0:T(8,128)} %get-tuple-element.38) | copy-start | bytes 2359300
  72.5 58.1 %copy-start.1 = (f32[128,1536]{1,0:T(8,128)S(1)}, f32[128,1536]{1,0:T(8,128)}, u32[]{:S(2)}) copy-start(f32[128,1536]{1,0:T(8,128)} %get-tuple-element.39) | copy-start | bytes 2359300
  72.5 78.9 %copy-start = (f32[128,1536]{1,0:T(8,128)S(1)}, f32[128,1536]{1,0:T(8,128)}, u32[]{:S(2)}) copy-start(f32[128,1536]{1,0:T(8,128)} %get-tuple-element.37) | copy-start | bytes 2359300
  72.5 78.9 %copy-start.2 = (bf16[128,1536]{1,0:T(8,128)(2,1)S(1)}, bf16[128,1536]{1,0:T(8,128)(2,1)}, u32[]{:S(2)}) copy-start(bf16[128,1536]{1,0:T(8,128)(2,1)} %get-tuple-element.35) | copy-start | bytes 1179652
  72.5 58.1 %collective-permute-start.7 = (f32[128,1536]{1,0:T(8,128)}, f32[128,1536]{1,0:T(8,128)S(1)}, u32[]{:S(2)}, u32[]{:S(2)}) collective-permute-start(f32[128,1536]{1,0:T(8,128)} %get-tuple-element.40), channel_id=1, source_target_pairs={{0,1},{1,0},{2,3},{3,2},{4,5},{5,4},{6,7},{7,6}} | collective-permute-start | bytes 2359304 | tf_op jit(solution)/shard_map/ppermute | solution.py:525
  130.1 3.0 %collective-permute-start.10 = (f32[128,1536]{1,0:T(8,128)}, f32[128,1536]{1,0:T(8,128)S(1)}, u32[]{:S(2)}, u32[]{:S(2)}) collective-permute-start(f32[128,1536]{1,0:T(8,128)} %get-tuple-element.44), channel_id=1, source_target_pairs={{0,1},{1,0},{2,3},{3,2},{4,5},{5,4},{6,7},{7,6}} | collective-permute-start | bytes 2359304 | tf_op jit(solution)/shard_map/ppermute | solution.py:525
  130.2 5.9 %collective-permute-start.6 = (f32[128,1536]{1,0:T(8,128)S(1)}, f32[128,1536]{1,0:T(8,128)S(1)}, u32[]{:S(2)}, u32[]{:S(2)}) collective-permute-start(f32[128,1536]{1,0:T(8,128)S(1)} %copy-done.3), channel_id=1, source_target_pairs={{0,1},{1,0},{2,3},{3,2},{4,5},{5,4},{6,7},{7,6}} | collective-permute-start | bytes 2359304 | tf_op jit(solution)/shard_map/ppermute | solution.py:525
  130.7 20.7 %collective-permute-start.8 = (f32[128,1536]{1,0:T(8,128)S(1)}, f32[128,1536]{1,0:T(8,128)S(1)}, u32[]{:S(2)}, u32[]{:S(2)}) collective-permute-start(f32[128,1536]{1,0:T(8,128)S(1)} %add.16), channel_id=1, source_target_pairs={{0,2},{1,3},{2,0},{3,1},{4,6},{5,7},{6,4},{7,5}} | collective-permute-start | bytes 2359304 | tf_op jit(solution)/shard_map/ppermute | solution.py:525
  133.0 19.4 %collective-permute-start.9 = (f32[128,1536]{1,0:T(8,128)}, f32[128,1536]{1,0:T(8,128)S(1)}, u32[]{:S(2)}, u32[]{:S(2)}) collective-permute-start(f32[128,1536]{1,0:T(8,128)} %get-tuple-element.42), channel_id=1, source_target_pairs={{0,1},{1,0},{2,3},{3,2},{4,5},{5,4},{6,7},{7,6}} | collective-permute-start | bytes 2359304 | tf_op jit(solution)/shard_map/ppermute | solution.py:525
  134.3 33.6 %collective-permute-start.11 = (f32[128,1536]{1,0:T(8,128)S(1)}, f32[128,1536]{1,0:T(8,128)S(1)}, u32[]{:S(2)}, u32[]{:S(2)}) collective-permute-start(f32[128,1536]{1,0:T(8,128)S(1)} %add.19), channel_id=1, source_target_pairs={{0,2},{1,3},{2,0},{3,1},{4,6},{5,7},{6,4},{7,5}} | collective-permute-start | bytes 2359304 | tf_op jit(solution)/shard_map/ppermute | solution.py:525
  152.4 15.5 %copy-start.4 = (f32[128,1536]{1,0:T(8,128)}, f32[128,1536]{1,0:T(8,128)S(1)}, u32[]{:S(2)}) copy-start(f32[128,1536]{1,0:T(8,128)S(1)} %collective-permute-done.9.s1) | copy-start | bytes 2359300
  167.9 0.9 copy-start.5

commit v3 on v2

--- a/solution.py
+++ b/solution.py
@@ -12,7 +12,6 @@
 BF = jnp.bfloat16
 F32 = jnp.float32
 MIB = 1024 * 1024
-CHUNK = 128
 
 
 def nn(a, b):
@@ -63,14 +62,31 @@
     return jnp.concatenate([ref[(group * reps + r) * dim:(group * reps + r + 1) * dim, lanes] for r in range(reps)], axis=1)
 
 
-def attn_fwd_kernel(kv_heads, reps, dim, xa_h, xb_h, n1, n2, wq_h, wk_h, wv_h, wo_h,
-                    ha_h, ua_h, hb_h, nb_h, qkv_h, ctx_h,
-                    xs, wq, wk, wv, wo, nrm, nrm_t, q_t, k_t, v_t, ctx, q_b, ctx_b, hs, ua, sems, osems):
+def neighbours():
+    me = lax.axis_index('expert')
+    return me + 1 - 2 * (me % 2), (me + 2) % 4
+
+
+def greet(peers):
+    barrier = pltpu.get_barrier_semaphore()
+    for peer in peers:
+        pl.semaphore_signal(barrier, inc=1, device_id={'expert': peer}, device_id_type=pl.DeviceIdType.MESH)
+    pl.semaphore_wait(barrier, len(peers))
+
+
+def remote(src, dst, send, recv, peer):
+    return pltpu.make_async_remote_copy(src_ref=src, dst_ref=dst, send_sem=send, recv_sem=recv, device_id={'expert': peer}, device_id_type=pl.DeviceIdType.MESH)
+
+
+def attn_fwd_kernel(kv_heads, reps, dim, xa_h, xb_h, dy_h, ea, sa, ga, eb, sb, gb, n1, n2, wq_h, wk_h, wv_h, wo_h,
+                    ha_h, ua_h, hb_h, nb_h, qkv_h, ctx_h, load_h,
+                    xs, wq, wk, wv, wo, nrm, nrm_t, q_t, k_t, v_t, ctx, q_b, ctx_b, hs, ua, mine, far_in, sems, osems, ssem, rsem):
+    near, far = neighbours()
     tokens = xs.shape[0] // 2
     heads = kv_heads * reps
     first, second = slice(0, tokens), slice(tokens, 2 * tokens)
     half = heads * dim // 2
-    moves = ((xa_h, xs.at[first]), (xb_h, xs.at[second]), (wk_h, wk), (wv_h, wv), (wq_h.at[0:half], wq.at[0:half]), (wq_h.at[half:], wq.at[half:]), (wo_h, wo))
+    moves = ((dy_h, mine.at[0:tokens]), (xa_h, xs.at[first]), (xb_h, xs.at[second]), (wk_h, wk), (wv_h, wv), (wq_h.at[0:half], wq.at[0:half]), (wq_h.at[half:], wq.at[half:]), (wo_h, wo))
     copies = [pltpu.make_async_copy(s, d, sems.at[i]) for i, (s, d) in enumerate(moves)]
     start_all(copies)
     outs = []
@@ -80,16 +96,28 @@
         c.start()
         outs.append(c)
 
-    wait_all(copies[0:2])
+    fields = [r[...].astype(F32) for r in (ea, sa, ga, eb, sb, gb)]
+    both = jnp.concatenate([jnp.concatenate(fields[0:3], axis=1), jnp.concatenate(fields[3:6], axis=1)], axis=0)
+    mine[tokens:] = jnp.concatenate([both, jnp.zeros((both.shape[0], mine.shape[1] - both.shape[1]), F32)], axis=1).astype(BF)
+    greet((near, far))
+    copies[0].wait()
+    to_far = remote(mine, far_in, ssem.at[0], rsem.at[0], far)
+    to_near = remote(mine, load_h.at[1], ssem.at[1], rsem.at[1], near)
+    relay = remote(far_in, load_h.at[3], ssem.at[2], rsem.at[2], near)
+    to_far.start()
+    to_near.start()
+    flush(mine, load_h.at[0])
+
+    wait_all(copies[1:3])
     nrm[...] = rms_rows(xs[...], row_of(n1))
     nrm_t[...] = jnp.transpose(nrm[...])
     flush(nrm.at[second], nb_h)
-    copies[2].wait()
+    copies[3].wait()
     k_t[...] = nn(wk[...], nrm_t[...]).astype(BF)
-    copies[3].wait()
+    copies[4].wait()
     v_t[...] = nn(wv[...], nrm_t[...]).astype(BF)
     for i in range(2):
-        copies[4 + i].wait()
+        copies[5 + i].wait()
         part = slice(i * half, (i + 1) * half)
         q_t[part] = nn(wq[part], nrm_t[...]).astype(BF)
     q_b[0:heads * dim] = q_t[:, second]
@@ -107,41 +135,49 @@
                 ctx[(g * reps + r) * dim:(g * reps + r + 1) * dim, lanes] = out[:, r * tokens:(r + 1) * tokens]
     ctx_b[...] = ctx[:, second]
     flush(ctx_b, ctx_h)
-    copies[6].wait()
+    to_far.wait_recv()
+    relay.start()
+    flush(far_in, load_h.at[2])
+    copies[7].wait()
     hs[...] = (xs[...].astype(F32) + tn(ctx[...], wo[...]).astype(BF).astype(F32)).astype(BF)
     flush(hs.at[first], ha_h)
     flush(hs.at[second], hb_h)
     ua[...] = rms_rows(hs[first], row_of(n2))
     flush(ua, ua_h)
+    to_far.wait_send()
+    to_near.wait()
+    relay.wait()
     wait_all(outs)
 
 
-def attn_fwd(x_a, x_b, n1, n2, wq, wk, wv, wo, kv_heads, reps, dim):
+def attn_fwd(x_a, x_b, dy, fields, n1, n2, wq, wk, wv, wo, kv_heads, reps, dim):
     tokens, model = x_a.shape
     q_dim, kv_dim = kv_heads * reps * dim, kv_heads * dim
+    depth = 2 * fields[0].shape[0]
     vm = pl.BlockSpec(memory_space=pltpu.VMEM)
     hb = pl.BlockSpec(memory_space=pl.ANY)
     row = jax.ShapeDtypeStruct((tokens, model), BF)
     return pl.pallas_call(
         functools.partial(attn_fwd_kernel, kv_heads, reps, dim),
-        out_shape=(row, row, row, row, jax.ShapeDtypeStruct((q_dim + 2 * kv_dim, tokens), BF), jax.ShapeDtypeStruct((q_dim, tokens), BF)),
-        in_specs=[hb] * 2 + [vm] * 2 + [hb] * 4,
-        out_specs=(hb,) * 6,
+        out_shape=(row, row, row, row, jax.ShapeDtypeStruct((q_dim + 2 * kv_dim, tokens), BF), jax.ShapeDtypeStruct((q_dim, tokens), BF), jax.ShapeDtypeStruct((4, tokens + depth, model), BF)),
+        in_specs=[hb] * 3 + [vm] * 8 + [hb] * 4,
+        out_specs=(hb,) * 7,
         scratch_shapes=[
             pltpu.VMEM((2 * tokens, model), BF),
             pltpu.VMEM((q_dim, model), BF), pltpu.VMEM((kv_dim, model), BF), pltpu.VMEM((kv_dim, model), BF), pltpu.VMEM((q_dim, model), BF),
             pltpu.VMEM((2 * tokens, model), BF), pltpu.VMEM((model, 2 * tokens), BF),
             pltpu.VMEM((q_dim, 2 * tokens), BF), pltpu.VMEM((kv_dim, 2 * tokens), BF), pltpu.VMEM((kv_dim, 2 * tokens), BF), pltpu.VMEM((q_dim, 2 * tokens), BF),
             pltpu.VMEM((q_dim + 2 * kv_dim, tokens), BF), pltpu.VMEM((q_dim, tokens), BF), pltpu.VMEM((2 * tokens, model), BF), pltpu.VMEM((tokens, model), BF),
-            pltpu.SemaphoreType.DMA((7,)), pltpu.SemaphoreType.DMA((6,)),
+            pltpu.VMEM((tokens + depth, model), BF), pltpu.VMEM((tokens + depth, model), BF),
+            pltpu.SemaphoreType.DMA((8,)), pltpu.SemaphoreType.DMA((8,)), pltpu.SemaphoreType.DMA((3,)), pltpu.SemaphoreType.DMA((3,)),
         ],
-        compiler_params=pltpu.CompilerParams(vmem_limit_bytes=60 * MIB),
+        compiler_params=pltpu.CompilerParams(vmem_limit_bytes=60 * MIB, collective_id=0, has_side_effects=True),
         cost_estimate=pl.CostEstimate(flops=10 ** 10, bytes_accessed=14 * 10 ** 6, transcendentals=0),
         name="attn_fwd",
-    )(x_a, x_b, n1, n2, wq, wk, wv, wo)
-
-
-def attn_bwd_kernel(kv_heads, reps, dim, s0, s1, t0, dy, h_b, x_b, nb, qkv, ctx, n1, n2, wo_h, wq_h, wk_h, wv_h,
+    )(x_a, x_b, dy, *fields, n1, n2, wq, wk, wv, wo)
+
+
+def attn_bwd_kernel(kv_heads, reps, dim, du_in, dy, h_b, x_b, nb, qkv, ctx, n1, n2, wo_h, wq_h, wk_h, wv_h,
                     dx, gq, gk, gv, go, gn1, gn2,
                     wo, wq, wk, wv, oq, ok, ov, oo, dctx, dq, dk, dv, sems, osems):
     copies = [pltpu.make_async_copy(s, d, sems.at[i]) for i, (s, d) in enumerate(((wo_h, wo), (wq_h, wq), (wk_h, wk), (wv_h, wv)))]
@@ -149,7 +185,7 @@
         c.start()
     tokens = x_b.shape[0]
     q_dim, kv_dim = kv_heads * reps * dim, kv_heads * dim
-    du = ((s0[...] + s1[...]) + t0[...]).astype(BF).astype(F32)
+    du = du_in[...].astype(F32)
     grad_h, g2 = rms_pull(h_b[...].astype(F32), row_of(n2), du)
     gn2[...] = g2
     dh = (dy[...].astype(F32) + grad_h).astype(BF)
@@ -203,7 +239,7 @@
         c.wait()
 
 
-def attn_bwd(s0, s1, t0, dy, h_b, x_b, nb, qkv, ctx, n1, n2, wo, wq, wk, wv, kv_heads, reps, dim):
+def attn_bwd(du, dy, h_b, x_b, nb, qkv, ctx, n1, n2, wo, wq, wk, wv, kv_heads, reps, dim):
     tokens, model = x_b.shape
     q_dim, kv_dim = kv_heads * reps * dim, kv_heads * dim
     vm = pl.BlockSpec(memory_space=pltpu.VMEM)
@@ -215,7 +251,7 @@
             jax.ShapeDtypeStruct((tokens, model), BF), jax.ShapeDtypeStruct((q_dim, model), F32), jax.ShapeDtypeStruct((kv_dim, model), F32),
             jax.ShapeDtypeStruct((kv_dim, model), F32), jax.ShapeDtypeStruct((q_dim, model), F32), jax.ShapeDtypeStruct((1, model), F32), jax.ShapeDtypeStruct((1, model), F32),
         ),
-        in_specs=[vm] * 11 + [hb] * 4,
+        in_specs=[vm] * 9 + [hb] * 4,
         out_specs=(vm, hb, hb, hb, hb, vm, vm),
         scratch_shapes=[
             pltpu.VMEM((q_dim, model), BF), pltpu.VMEM((q_dim, model), BF), pltpu.VMEM((kv_dim, model), BF), pltpu.VMEM((kv_dim, model), BF),
@@ -226,7 +262,7 @@
         compiler_params=pltpu.CompilerParams(vmem_limit_bytes=60 * MIB),
         cost_estimate=pl.CostEstimate(flops=14 * 10 ** 9, bytes_accessed=40 * 10 ** 6, transcendentals=0),
         name="attn_bwd",
-    )(s0, s1, t0, dy, h_b, x_b, nb, qkv, ctx, n1, n2, wo, wq, wk, wv)
+    )(du, dy, h_b, x_b, nb, qkv, ctx, n1, n2, wo, wq, wk, wv)
 
 
 def route_rows(info, base, expert):
@@ -245,22 +281,6 @@
     return slot_row, gate_row
 
 
-def places(slot_row, group):
-    tokens = slot_row.shape[1] // group
-    kept = jnp.where(slot_row >= 0.0, 1.0, 0.0)
-    start = jnp.zeros((1, 1), F32)
-    starts = []
-    for r in range(group):
-        starts.append(jnp.broadcast_to(start, (1, tokens)))
-        start = start + jnp.sum(kept[:, r * tokens:(r + 1) * tokens], axis=1, keepdims=True)
-    place_row = jnp.where(slot_row >= 0.0, slot_row + jnp.concatenate(starts, axis=1), -1.0).astype(jnp.int32)
-    return place_row, jnp.sum(kept)
-
-
-def hits(place_row, first):
-    return lax.broadcasted_iota(jnp.int32, (CHUNK, place_row.shape[1]), 0) + first == place_row
-
-
 def ring_copies(pairs, sem, idx, ring):
     s = lax.rem(idx, ring)
     return [pltpu.make_async_copy(src.at[idx], dst.at[s], sem.at[s, i]) for i, (src, dst) in enumerate(pairs)]
@@ -271,10 +291,10 @@
     return [pltpu.make_async_copy(ref.at[0:tokens], rows.at[r * tokens:(r + 1) * tokens], sem.at[r]) for r, ref in enumerate(refs)]
 
 
-def info_copies(refs, info, sem):
+def info_copy(loads, info, sem):
     _, depth, width = info.shape
-    first = refs[0].shape[0] - depth
-    return [pltpu.make_async_copy(ref.at[first:first + depth, 0:width], info.at[r], sem.at[len(refs) + r]) for r, ref in enumerate(refs)]
+    first = loads.shape[1] - depth
+    return [pltpu.make_async_copy(loads.at[:, first:first + depth, 0:width], info, sem.at[4])]
 
 
 def part_copies(acc, refs, sem):
@@ -298,7 +318,7 @@
         acc[:, part] += nn(pick, outs[:, part])
 
 
-def expert_bwd_kernel(capacity, d0, d1, d2, d3, u_h, w1_h, w2_h, w3_h,
+def expert_bwd_kernel(capacity, loads, u_h, w1_h, w2_h, w3_h,
                       g1, g2, g3, p0, p1, p2, p3,
                       rows, info, us, w1s, w2s, w3s, pick, du_two, d_out, hid, da1, da3, o1, o2, o3, acc, rsem, wsem, sems, psem):
     e = pl.program_id(0)
@@ -309,8 +329,7 @@
     tokens = rows.shape[0] // 4
     ff = w1s.shape[2]
     padded = du_two.shape[0] // 2
-    heads = (d0, d1, d2, d3)
-    arrivals = info_copies(heads, info, rsem) + row_copies(heads, rows, rsem)
+    arrivals = info_copy(loads, info, rsem) + row_copies([loads.at[r] for r in range(4)], rows, rsem)
     pairs = ((u_h, us), (w1_h, w1s), (w3_h, w3s), (w2_h, w2s))
 
     @pl.when(e == 0)
@@ -384,8 +403,8 @@
         wait_all(sends)
 
 
-def expert_bwd(dys, u, w1, w2, w3, tokens):
-    model = dys[0].shape[1]
+def expert_bwd(loads, u, w1, w2, w3, tokens):
+    model = loads.shape[2]
     count, cols, _ = u.shape
     ff = w1.shape[2]
     padded, ring = 256, 3
@@ -395,71 +414,81 @@
         functools.partial(expert_bwd_kernel, cols // 4),
         grid=(count,),
         out_shape=(jax.ShapeDtypeStruct((count, model, ff), F32), jax.ShapeDtypeStruct((count, ff, model), F32), jax.ShapeDtypeStruct((count, model, ff), F32), part, part, part, part),
-        in_specs=[hb] * 8,
+        in_specs=[hb] * 5,
         out_specs=(hb,) * 7,
         scratch_shapes=[
-            pltpu.VMEM((4 * tokens, model), BF), pltpu.VMEM((4, dys[0].shape[0] - tokens, 3 * tokens), BF),
+            pltpu.VMEM((4 * tokens, model), BF), pltpu.VMEM((4, loads.shape[1] - tokens, 3 * tokens), BF),
             pltpu.VMEM((ring, cols, model), BF), pltpu.VMEM((ring, model, ff), BF), pltpu.VMEM((ring, ff, model), BF), pltpu.VMEM((ring, model, ff), BF),
             pltpu.VMEM((4 * tokens, 2 * padded), BF), pltpu.VMEM((2 * padded, model), BF),
             pltpu.VMEM((cols, model), BF), pltpu.VMEM((cols, ff), BF), pltpu.VMEM((cols, ff), BF), pltpu.VMEM((cols, ff), BF),
             pltpu.VMEM((2, model, ff), F32), pltpu.VMEM((2, ff, model), F32), pltpu.VMEM((2, model, ff), F32),
             pltpu.VMEM((4 * tokens, model), F32),
-            pltpu.SemaphoreType.DMA((8,)), pltpu.SemaphoreType.DMA((ring, 4)), pltpu.SemaphoreType.DMA((2, 3)), pltpu.SemaphoreType.DMA((4,)),
+            pltpu.SemaphoreType.DMA((5,)), pltpu.SemaphoreType.DMA((ring, 4)), pltpu.SemaphoreType.DMA((2, 3)), pltpu.SemaphoreType.DMA((4,)),
         ],
         compiler_params=pltpu.CompilerParams(vmem_limit_bytes=60 * MIB, dimension_semantics=("arbitrary",)),
         cost_estimate=pl.CostEstimate(flops=50 * 10 ** 9, bytes_accessed=150 * 10 ** 6, transcendentals=0),
         name="expert_bwd",
-    )(*dys, u, w1, w2, w3)
-
-
-def expert_fwd_kernel(u0, u1, u2, u3, d0, d1, d2, d3, w1_h, w2_h, w3_h, p0, p1, p2, p3,
-                      rows, info, w1s, w2s, w3s, pick, out_two, acc, late_t, rsem, wsem, psem):
+    )(loads, u, w1, w2, w3)
+
+
+def expert_fwd_kernel(capacity, u0, u1, u2, u3, loads, b0, b1, b2, b3, w1_h, w2_h, w3_h, du_o, mine_o, out_o,
+                      rows, info, w1s, w2s, w3s, pick, out_two, acc, loc0, loc2, rx1, rx3, rxf, ra1, ra3, rsem, wsem, bsem, ssem, xsem):
     e = pl.program_id(0)
     count = pl.num_programs(0)
     me = lax.axis_index('expert')
+    near, far = neighbours()
     ring, _, ff = w1s.shape
-    slot_e = lax.rem(e, 2)
-    arrivals = info_copies((d0, d1, d2, d3), info, rsem) + row_copies((u0, u1, u2, u3), rows, rsem)
+    slot_e = e % 2
+    tokens = rows.shape[0] // 4
+    cols = 4 * capacity
+    padded = out_two.shape[0] // 2
+    arrivals = info_copy(loads, info, rsem) + row_copies((u0, u1, u2, u3), rows, rsem)
     pairs = ((w1_h, w1s), (w3_h, w3s), (w2_h, w2s))
+    local = [pltpu.make_async_copy(b0, loc0, bsem.at[0]), pltpu.make_async_copy(b2, loc2, bsem.at[1])]
+    swap3 = remote(b3, rx3, ssem.at[0], xsem.at[0], near)
+    swap1 = remote(b1, rx1, ssem.at[1], xsem.at[1], near)
+    over = remote(loc2, rxf, ssem.at[2], xsem.at[2], far)
+    part = [slice(r * tokens, (r + 1) * tokens) for r in range(4)]
+    late3 = remote(acc.at[part[3]], ra3, ssem.at[3], xsem.at[3], near)
+    late1 = remote(acc.at[part[1]], ra1, ssem.at[4], xsem.at[4], near)
 
     @pl.when(e == 0)
     def _():
-        start_all(arrivals + ring_copies(pairs, wsem, 0, ring) + ring_copies(pairs, wsem, 1, ring))
+        start_all(arrivals + ring_copies(pairs, wsem, 0, ring) + ring_copies(pairs, wsem, 1, ring) + local)
+        greet((near, far))
+        swap3.start()
+        swap1.start()
         acc[...] = jnp.zeros_like(acc)
+        out_two[...] = jnp.zeros_like(out_two)
         wait_all(arrivals)
 
+    @pl.when(e == 1)
+    def _():
+        wait_all(local)
+        swap3.wait()
+        loc2[...] += rx3[...]
+        over.start()
+
     @pl.when(e + 2 < count)
     def _():
         start_all(ring_copies(pairs, wsem, e + 2, ring))
 
     slot_row, gate_row = route_rows(info, 0, me * count + e)
-    place_row, filled = places(slot_row, 4)
+    group = lax.broadcasted_iota(jnp.int32, slot_row.shape, 1) // tokens
+    col_row = jnp.where(slot_row >= 0.0, slot_row.astype(jnp.int32) + group * capacity, -1)
+    hot = lax.broadcasted_iota(jnp.int32, (padded, 4 * tokens), 0) == col_row
+    pick[:, pl.ds(pl.multiple_of(slot_e * padded, padded), padded)] = jnp.transpose(jnp.where(hot, gate_row, 0.0).astype(BF))
+    v = nn(jnp.where(hot, 1.0, 0.0).astype(BF)[0:cols], rows[...]).astype(BF)
     wait_all(ring_copies(pairs, wsem, e, ring))
-    now = lax.rem(e, ring)
+    now = e % ring
     w1, w2, w3 = w1s.at[now], w2s.at[now], w3s.at[now]
-
-    def run(first):
-        hot = hits(place_row, first)
-        v = nn(jnp.where(hot, 1.0, 0.0).astype(BF), rows[...]).astype(BF)
-        pieces = []
-        for n in range(ff // 256):
-            part = slice(n * 256, (n + 1) * 256)
-            a1 = nn(v, w1[:, part]).astype(BF).astype(F32)
-            a3 = nn(v, w3[:, part]).astype(BF).astype(F32)
-            pieces.append((a1 * jax.nn.sigmoid(a1) * a3).astype(BF))
-        hidden = jnp.concatenate(pieces, axis=1)
-        return jnp.transpose(jnp.where(hot, gate_row, 0.0).astype(BF)), nn(hidden, w2[...]).astype(BF)
-
-    chosen, out = run(0)
-    half = pl.ds(pl.multiple_of(slot_e * CHUNK, CHUNK), CHUNK)
-    pick[:, half] = chosen
-    out_two[half, :] = out
-
-    @pl.when(filled > float(CHUNK))
-    def _():
-        more, out_more = run(CHUNK)
-        late_t[...] = more
-        mix_into(acc, late_t[...], out_more)
+    pieces = []
+    for n in range(ff // 256):
+        lanes = slice(n * 256, (n + 1) * 256)
+        a1 = nn(v, w1[:, lanes]).astype(BF).astype(F32)
+        a3 = nn(v, w3[:, lanes]).astype(BF).astype(F32)
+        pieces.append((a1 * jax.nn.sigmoid(a1) * a3).astype(BF))
+    out_two[pl.ds(pl.multiple_of(slot_e * padded, padded), cols), :] = nn(jnp.concatenate(pieces, axis=1), w2[...]).astype(BF)
 
     @pl.when(slot_e == 1)
     def _():
@@ -467,55 +496,45 @@
 
     @pl.when(e == count - 1)
     def _():
-        sends = part_copies(acc, (p0, p1, p2, p3), psem)
-        start_all(sends)
-        wait_all(sends)
-
-
-def expert_fwd(us, dys, w1, w2, w3):
+        late3.start()
+        late1.start()
+        swap1.wait()
+        over.wait()
+        du_o[...] = ((loc0[...] + rx1[...]) + rxf[...]).astype(BF)
+        late3.wait()
+        out_o[...] = acc[part[2]] + ra3[...]
+        late1.wait()
+        mine_o[...] = acc[part[0]] + ra1[...]
+
+
+def whole(shape):
+    return pl.BlockSpec(shape, lambda e: (0,) * len(shape), pipeline_mode=pl.Buffered(1))
+
+
+def expert_fwd(us, loads, sums, w1, w2, w3, capacity):
     tokens, model = us[0].shape
     count, _, ff = w1.shape
-    ring = 3
+    padded, ring = 256, 3
     part = jax.ShapeDtypeStruct((tokens, model), F32)
     hb = pl.BlockSpec(memory_space=pl.ANY)
+    tile = pltpu.VMEM((tokens, model), F32)
     return pl.pallas_call(
-        expert_fwd_kernel,
+        functools.partial(expert_fwd_kernel, capacity),
         grid=(count,),
-        out_shape=(part, part, part, part),
-        in_specs=[hb] * 11,
-        out_specs=(hb,) * 4,
+        out_shape=(jax.ShapeDtypeStruct((tokens, model), BF), part, part),
+        in_specs=[hb] * 12,
+        out_specs=(whole((tokens, model)),) * 3,
         scratch_shapes=[
-            pltpu.VMEM((4 * tokens, model), BF), pltpu.VMEM((4, dys[0].shape[0] - tokens, 3 * tokens), BF),
+            pltpu.VMEM((4 * tokens, model), BF), pltpu.VMEM((4, loads.shape[1] - tokens, 3 * tokens), BF),
             pltpu.VMEM((ring, model, ff), BF), pltpu.VMEM((ring, ff, model), BF), pltpu.VMEM((ring, model, ff), BF),
-            pltpu.VMEM((4 * tokens, 2 * CHUNK), BF), pltpu.VMEM((2 * CHUNK, model), BF),
-            pltpu.VMEM((4 * tokens, model), F32), pltpu.VMEM((4 * tokens, CHUNK), BF),
-            pltpu.SemaphoreType.DMA((8,)), pltpu.SemaphoreType.DMA((ring, 3)), pltpu.SemaphoreType.DMA((4,)),
+            pltpu.VMEM((4 * tokens, 2 * padded), BF), pltpu.VMEM((2 * padded, model), BF), pltpu.VMEM((4 * tokens, model), F32),
+            tile, tile, tile, tile, tile, tile, tile,
+            pltpu.SemaphoreType.DMA((5,)), pltpu.SemaphoreType.DMA((ring, 3)), pltpu.SemaphoreType.DMA((2,)), pltpu.SemaphoreType.DMA((5,)), pltpu.SemaphoreType.DMA((5,)),
         ],
-        compiler_params=pltpu.CompilerParams(vmem_limit_bytes=60 * MIB, dimension_semantics=("arbitrary",)),
+        compiler_params=pltpu.CompilerParams(vmem_limit_bytes=60 * MIB, dimension_semantics=("arbitrary",), collective_id=1, has_side_effects=True),
         cost_estimate=pl.CostEstimate(flops=16 * 10 ** 9, bytes_accessed=50 * 10 ** 6, transcendentals=0),
         name="expert_fwd",
-    )(*us, *dys, w1, w2, w3)
-
-
-def pack_kernel(dy, *refs):
-    out = refs[-1]
-    tokens = dy.shape[0]
-    fields = [r[...].astype(F32) for r in refs[:-1]]
-    both = jnp.concatenate([jnp.concatenate(fields[0:3], axis=1), jnp.concatenate(fields[3:6], axis=1)], axis=0)
-    out[0:tokens] = dy[...]
-    out[tokens:] = jnp.concatenate([both, jnp.zeros((both.shape[0], dy.shape[1] - both.shape[1]), F32)], axis=1).astype(BF)
-
-
-def pack(dy, fields):
-    vm = pl.BlockSpec(memory_space=pltpu.VMEM)
-    depth = 2 * fields[0].shape[0]
-    return pl.pallas_call(
-        pack_kernel,
-        out_shape=jax.ShapeDtypeStruct((dy.shape[0] + depth, dy.shape[1]), BF),
-        in_specs=[vm] * 7, out_specs=vm,
-        compiler_params=pltpu.CompilerParams(vmem_limit_bytes=60 * MIB),
-        name="pack",
-    )(dy, *fields)
+    )(*us, loads, *sums, w1, w2, w3)
 
 
 def solution(mesh):
@@ -528,22 +547,16 @@
         model, heads, dim = w_q.shape
         kv_heads = w_k.shape[1]
         reps = heads // kv_heads
-        load = pack(dy_b, [a.T for a in (eid_a, slot_a, gate_a, eid_b, slot_b, gate_b)])
-        dy2 = hop(load, 2)
-        dy1 = hop(load, 1)
         wq_t, wk_t, wv_t = (w.transpose(1, 2, 0).reshape(-1, model) for w in (w_q, w_k, w_v))
         wo = w_o.reshape(-1, model)
-        h_a, u_a, h_b, nb, qkv_b, ctx_b = attn_fwd(x_a, x_b, norm_1, norm_2, wq_t, wk_t, wv_t, wo, kv_heads, reps, dim)
-        dys = (load, dy1, dy2, hop(dy2, 1))
+        fields = [a.T for a in (eid_a, slot_a, gate_a, eid_b, slot_b, gate_b)]
+        h_a, u_a, h_b, nb, qkv_b, ctx_b, loads = attn_fwd(x_a, x_b, dy_b, fields, norm_1, norm_2, wq_t, wk_t, wv_t, wo, kv_heads, reps, dim)
         us = (u_a, hop(u_a, 1), hop(u_a, 2), hop(u_a, 3))
-        g1, g2, g3, b0, b1, b2, b3 = expert_bwd(dys, u_b, w_1, w_2, w_3, x_a.shape[0])
-        far_b = hop(b2 + hop(b3, 1), 2)
-        near_b = hop(b1, 1)
-        a0, a1, a2, a3 = expert_fwd(us, dys, w_1, w_2, w_3)
-        far_a = hop(a2 + hop(a3, 1), 2)
-        near_a = hop(a1, 1)
-        dx_b, g_q, g_k, g_v, g_o, g_n1, g_n2 = attn_bwd(b0, near_b, far_b, dy_b, h_b, x_b, nb, qkv_b, ctx_b, norm_1, norm_2, wo, wq_t, wk_t, wv_t, kv_heads, reps, dim)
-        y_a = (h_a.astype(F32) + ((a0 + near_a) + far_a)).astype(BF)
+        g1, g2, g3, *sums = expert_bwd(loads, u_b, w_1, w_2, w_3, x_a.shape[0])
+        du, mine_a, out_a = expert_fwd(us, loads, sums, w_1, w_2, w_3, u_b.shape[1] // group)
+        far_a = hop(out_a, 2)
+        dx_b, g_q, g_k, g_v, g_o, g_n1, g_n2 = attn_bwd(du, dy_b, h_b, x_b, nb, qkv_b, ctx_b, norm_1, norm_2, wo, wq_t, wk_t, wv_t, kv_heads, reps, dim)
+        y_a = (h_a.astype(F32) + (mine_a + far_a)).astype(BF)
         g_q = g_q.reshape(heads, dim, model).transpose(2, 0, 1)
         g_k = g_k.reshape(kv_heads, dim, model).transpose(2, 0, 1)
         g_v = g_v.reshape(kv_heads, dim, model).transpose(2, 0, 1)

time: 185 us -> 132 us (0.71)
  waiting for transfers between devices: 59.2 us -> 4.04 us
  Pallas kernels: 108 us -> 123 us
  starting transfers between devices: 11.2 us -> 2.66 us
    ppermute x12 -> x4, waiting for transfers between devices: 59.2 us -> 4.04 us  [hop(): return lax.ppermute(value, 'expert', [(i, i ^ bits) for i in range(group)])]
    pallas_call x2 -> x1, Pallas kernels: 22.8 us -> 32.8 us  [expert_fwd(): pl.pallas_call(functools.partial(expert_fwd_kernel, capacity), grid=(coun...]
    ppermute x12 -> x4, starting transfers between devices: 11.2 us -> 2.66 us  [hop(): return lax.ppermute(value, 'expert', [(i, i ^ bits) for i in range(group)])]
    pallas_call x1, Pallas kernels: 13.4 us -> 17.9 us  [attn_fwd(): pl.pallas_call(functools.partial(attn_fwd_kernel, kv_heads, reps, dim), o...]
  transfers between devices with their start and end apart: 12 -> 4, of which waited for: 5 -> 1; matrix products, arithmetic and copies ran while one was open for 1% -> 0% of each run, Pallas kernels for 38% -> 54%
where the time goes in v3:
time: 132 us
  Pallas kernels  123 us (93%)
  waiting for transfers between devices  4.04 us (3%)
  starting transfers between devices  2.66 us (2%)
    pallas_call x1, Pallas kernels, expert_bwd(): pl.pallas_call(functools.partial(expert_bwd_kernel, cols // 4), grid=(cou...  56.5 us
    pallas_call x1, Pallas kernels, expert_fwd(): pl.pallas_call(functools.partial(expert_fwd_kernel, capacity), grid=(coun...  32.8 us
    pallas_call x1, Pallas kernels, attn_fwd(): pl.pallas_call(functools.partial(attn_fwd_kernel, kv_heads, reps, dim), o...  17.9 us
    pallas_call x1, Pallas kernels, attn_bwd(): pl.pallas_call(functools.partial(attn_bwd_kernel, kv_heads, reps, dim), o...  15.2 us
    ppermute x4, waiting for transfers between devices, hop(): return lax.ppermute(value, 'expert', [(i, i ^ bits) for i in range(group)])  4.04 us
    ppermute x4, starting transfers between devices, hop(): return lax.ppermute(value, 'expert', [(i, i ^ bits) for i in range(group)])  2.66 us
  transfers between devices with their start and end apart: 4, of which 1 were waited for; matrix products, arithmetic and copies ran while one was open for 0% of the time, Pallas kernels for 54%

profile of v3, /device:TPU:0, one launch (start us, length us, event | category | flops | bytes accessed | tf_op | source)
XLA Modules:
  0.0 131.8 jit_solution(16718687445418788110)
XLA Ops:
  0.6 17.9 %attn_fwd.1 = (bf16[128,1536]{1,0:T(8,128)(2,1)}, bf16[128,1536]{1,0:T(8,128)(2,1)}, bf16[128,1536]{1,0:T(8,128)(2,1)}, bf16[128,1536]{1,0:T(8,128)(2,1)}, bf16[...) custom-call(bf16[128,1536]{1,0:T(8,128)(2,1)} %xa_h.1, bf16[128,1536]{1,0:T(8,128)(2,1)} %x_b.1, ...), custom_call_target="tpu_custom_call" | custom-call | flops 10000000000 | bytes 14000000 | tf_op jit(solution)/shard_map/attn_fwd/pallas_call | solution.py:160
  18.6 0.0 collective-permute-start.2
  18.6 1.1 collective-permute-start.1
  19.7 0.7 collective-permute-start
  20.5 56.5 %expert_bwd.1 = (f32[10,1536,512]{2,1,0:T(8,128)}, f32[10,512,1536]{2,1,0:T(8,128)}, f32[10,1536,512]{2,1,0:T(8,128)}, f32[128,1536]{1,0:T(8,128)}, f32[128,1536...) custom-call(bf16[4,144,1536]{2,1,0:T(8,128)(2,1)} %get-tuple-element.37.loads, bf16[10,224,1536]{2,1,0:T(8,128)(2,1)} %u_h.1, ...), custom_call_target="tpu_custom_call" | custom-call | flops 49999998976 | bytes 150000000 | tf_op jit(solution)/shard_map/expert_bwd/pallas_call | solution.py:413
  77.0 0.0 collective-permute-done.2.u3
  77.0 0.0 copy-start.2
  77.0 0.0 collective-permute-done.1.u2
  77.0 0.0 copy-start.3
  77.0 0.0 collective-permute-done.u1
  77.0 0.0 copy-start.4
  77.1 0.7 copy-done.2
  77.8 0.1 copy-done.3
  77.9 0.1 copy-done.4
  78.0 32.8 %expert_fwd.1 = (bf16[128,1536]{1,0:T(8,128)(2,1)}, f32[128,1536]{1,0:T(8,128)}, f32[128,1536]{1,0:T(8,128)}) custom-call(bf16[128,1536]{1,0:T(8,128)(2,1)} %get-tuple-element.36.u0, bf16[128,1536]{1,0:T(8,128)(2,1)} %copy-done.4, bf16[128,1536]{1,0:T(8,128)(2,1)} %copy-done.3, bf16[128,1536]{1,0:T(8,128)(2,1)} %copy-done.2, ...), custom_call_target="tpu_custom_call" | custom-call | flops 16000000000 | bytes 50000000 | tf_op jit(solution)/shard_map/expert_fwd/pallas_call | solution.py:521
  110.9 0.8 collective-permute-start.3
  111.6 0.0 copy-start
  111.6 0.0 copy-start.1
  111.6 15.2 %attn_bwd.1 = (bf16[128,1536]{1,0:T(8,128)(2,1)}, f32[1536,1536]{1,0:T(8,128)}, f32[512,1536]{1,0:T(8,128)}, f32[512,1536]{1,0:T(8,128)}, f32[1536,1536]{1,0:T(8...) custom-call(bf16[128,1536]{1,0:T(8,128)(2,1)} %get-tuple-element.44.du_in, bf16[128,1536]{1,0:T(8,128)(2,1)} %dy.1, ...), custom_call_target="tpu_custom_call" | custom-call | flops 14000000000 | bytes 40000000 | tf_op jit(solution)/shard_map/attn_bwd/pallas_call | solution.py:248
  126.9 4.0 %collective-permute-done.3 = f32[128,1536]{1,0:T(8,128)S(1)} collective-permute-done((f32[128,1536]{1,0:T(8,128)}, f32[128,1536]{1,0:T(8,128)S(1)}, u32[]{:S(2)}, u32[]{:S(2)}) %collective-permute-start.3) | collective-permute-done | bytes 786464 | tf_op jit(solution)/shard_map/ppermute | solution.py:544
  130.9 0.0 copy-done
  130.9 0.0 copy-done.1
  130.9 0.9 add_convert_fusion
Async XLA Ops:
  18.6 58.4 %collective-permute-start.2 = (bf16[128,1536]{1,0:T(8,128)(2,1)}, bf16[128,1536]{1,0:T(8,128)(2,1)S(1)}, u32[]{:S(2)}, u32[]{:S(2)}) collective-permute-start(bf16[128,1536]{1,0:T(8,128)(2,1)} %get-tuple-element.36.u0), channel_id=1, source_target_pairs={{0,3},{1,2},{2,1},{3,0},{4,7},{5,6},{6,5},{7,4}} | collective-permute-start | bytes 1179656 | tf_op jit(solution)/shard_map/ppermute | solution.py:544
  18.6 58.4 %collective-permute-start.1 = (bf16[128,1536]{1,0:T(8,128)(2,1)}, bf16[128,1536]{1,0:T(8,128)(2,1)S(1)}, u32[]{:S(2)}, u32[]{:S(2)}) collective-permute-start(bf16[128,1536]{1,0:T(8,128)(2,1)} %get-tuple-element.36.u0), channel_id=1, source_target_pairs={{0,2},{1,3},{2,0},{3,1},{4,6},{5,7},{6,4},{7,5}} | collective-permute-start | bytes 1179656 | tf_op jit(solution)/shard_map/ppermute | solution.py:544
  19.7 57.3 %collective-permute-start = (bf16[128,1536]{1,0:T(8,128)(2,1)}, bf16[128,1536]{1,0:T(8,128)(2,1)S(1)}, u32[]{:S(2)}, u32[]{:S(2)}) collective-permute-start(bf16[128,1536]{1,0:T(8,128)(2,1)} %get-tuple-element.36.u0), channel_id=1, source_target_pairs={{0,1},{1,0},{2,3},{3,2},{4,5},{5,4},{6,7},{7,6}} | collective-permute-start | bytes 1179656 | tf_op jit(solution)/shard_map/ppermute | solution.py:544
  77.0 0.8 copy-start.2
  77.0 0.9 copy-start.3
  77.0 1.0 copy-start.4
  110.9 20.0 %collective-permute-start.3 = (f32[128,1536]{1,0:T(8,128)}, f32[128,1536]{1,0:T(8,128)S(1)}, u32[]{:S(2)}, u32[]{:S(2)}) collective-permute-start(f32[128,1536]{1,0:T(8,128)} %get-tuple-element.43), channel_id=1, source_target_pairs={{0,2},{1,3},{2,0},{3,1},{4,6},{5,7},{6,4},{7,5}} | collective-permute-start | bytes 2359304 | tf_op jit(solution)/shard_map/ppermute | solution.py:544
  111.6 19.3 %copy-start = (f32[128,1536]{1,0:T(8,128)S(1)}, f32[128,1536]{1,0:T(8,128)}, u32[]{:S(2)}) copy-start(f32[128,1536]{1,0:T(8,128)} %get-tuple-element.42) | copy-start | bytes 2359300
  111.6 19.3 %copy-start.1 = (bf16[128,1536]{1,0:T(8,128)(2,1)S(1)}, bf16[128,1536]{1,0:T(8,128)(2,1)}, u32[]{:S(2)}) copy-start(bf16[128,1536]{1,0:T(8,128)(2,1)} %get-tuple-element.35) | copy-start | bytes 1179652

commit v4 on v3

--- a/solution.py
+++ b/solution.py
@@ -11,7 +11,9 @@
 NORM_EPS = 1e-6
 BF = jnp.bfloat16
 F32 = jnp.float32
-MIB = 1024 * 1024
+VMEM_BYTES = 67043328
+QUAD = 4
+BLOCK = 64
 
 
 def nn(a, b):
@@ -135,11 +137,11 @@
                 ctx[(g * reps + r) * dim:(g * reps + r + 1) * dim, lanes] = out[:, r * tokens:(r + 1) * tokens]
     ctx_b[...] = ctx[:, second]
     flush(ctx_b, ctx_h)
+    copies[7].wait()
+    hs[...] = (xs[...].astype(F32) + tn(ctx[...], wo[...]).astype(BF).astype(F32)).astype(BF)
     to_far.wait_recv()
     relay.start()
     flush(far_in, load_h.at[2])
-    copies[7].wait()
-    hs[...] = (xs[...].astype(F32) + tn(ctx[...], wo[...]).astype(BF).astype(F32)).astype(BF)
     flush(hs.at[first], ha_h)
     flush(hs.at[second], hb_h)
     ua[...] = rms_rows(hs[first], row_of(n2))
@@ -171,7 +173,7 @@
             pltpu.VMEM((tokens + depth, model), BF), pltpu.VMEM((tokens + depth, model), BF),
             pltpu.SemaphoreType.DMA((8,)), pltpu.SemaphoreType.DMA((8,)), pltpu.SemaphoreType.DMA((3,)), pltpu.SemaphoreType.DMA((3,)),
         ],
-        compiler_params=pltpu.CompilerParams(vmem_limit_bytes=60 * MIB, collective_id=0, has_side_effects=True),
+        compiler_params=pltpu.CompilerParams(vmem_limit_bytes=VMEM_BYTES, collective_id=0, has_side_effects=True),
         cost_estimate=pl.CostEstimate(flops=10 ** 10, bytes_accessed=14 * 10 ** 6, transcendentals=0),
         name="attn_fwd",
     )(x_a, x_b, dy, *fields, n1, n2, wq, wk, wv, wo)
@@ -259,7 +261,7 @@
             pltpu.VMEM((q_dim, tokens), BF), pltpu.VMEM((q_dim, tokens), BF), pltpu.VMEM((kv_dim, tokens), BF), pltpu.VMEM((kv_dim, tokens), BF),
             pltpu.SemaphoreType.DMA((4,)), pltpu.SemaphoreType.DMA((n_out,)),
         ],
-        compiler_params=pltpu.CompilerParams(vmem_limit_bytes=60 * MIB),
+        compiler_params=pltpu.CompilerParams(vmem_limit_bytes=VMEM_BYTES),
         cost_estimate=pl.CostEstimate(flops=14 * 10 ** 9, bytes_accessed=40 * 10 ** 6, transcendentals=0),
         name="attn_bwd",
     )(du, dy, h_b, x_b, nb, qkv, ctx, n1, n2, wo, wq, wk, wv)
@@ -291,15 +293,16 @@
     return [pltpu.make_async_copy(ref.at[0:tokens], rows.at[r * tokens:(r + 1) * tokens], sem.at[r]) for r, ref in enumerate(refs)]
 
 
-def info_copy(loads, info, sem):
-    _, depth, width = info.shape
-    first = loads.shape[1] - depth
-    return [pltpu.make_async_copy(loads.at[:, first:first + depth, 0:width], info, sem.at[4])]
-
-
-def part_copies(acc, refs, sem):
-    tokens = acc.shape[0] // len(refs)
-    return [pltpu.make_async_copy(acc.at[r * tokens:(r + 1) * tokens], ref, sem.at[r]) for r, ref in enumerate(refs)]
+def info_copy(load, info, sem):
+    depth, width = info.shape
+    first = load.shape[0] - depth
+    return pltpu.make_async_copy(load.at[first:first + depth, 0:width], info, sem)
+
+
+def hits(slot_row, tokens, capacity):
+    source = lax.broadcasted_iota(jnp.int32, slot_row.shape, 1) // tokens
+    col_row = jnp.where(slot_row >= 0.0, slot_row.astype(jnp.int32) + source * capacity, -1)
+    return lax.broadcasted_iota(jnp.int32, (4 * capacity, slot_row.shape[1]), 0) == col_row
 
 
 def start_all(copies):
@@ -312,31 +315,51 @@
         c.wait()
 
 
-def mix_into(acc, pick, outs):
-    for n in range(acc.shape[1] // 256):
-        part = slice(n * 256, (n + 1) * 256)
-        acc[:, part] += nn(pick, outs[:, part])
+def keep_routes(slots, gates, q, slot_row, gate_row):
+    slots[pl.ds(q, 1), :] = slot_row
+    gates[pl.ds(q, 1), :] = gate_row
+
+
+def stash(outs, q, capacity, lanes, res):
+    for r in range(outs.shape[0]):
+        outs[r, pl.ds(pl.multiple_of(q * BLOCK, BLOCK), capacity), lanes] = res[r * capacity:(r + 1) * capacity].astype(BF)
+
+
+def mix_into(acc, outs, slots, gates, q, weighted):
+    tokens = acc.shape[0] // outs.shape[0]
+    depth = lax.broadcasted_iota(jnp.int32, (BLOCK, tokens), 0).astype(F32)
+    for r in range(outs.shape[0]):
+        lanes = slice(r * tokens, (r + 1) * tokens)
+        blocks = []
+        for k in range(QUAD):
+            weight = gates[k:k + 1, lanes] if weighted else 1.0
+            slot = jnp.where(q >= k, slots[k:k + 1, lanes], -1.0)
+            blocks.append(jnp.where(depth == slot, weight, 0.0))
+        pick = jnp.transpose(jnp.concatenate(blocks, axis=0).astype(BF))
+        for n in range(acc.shape[1] // 512):
+            part = slice(n * 512, (n + 1) * 512)
+            acc[lanes, part] += nn(pick, outs[r, :, part])
 
 
 def expert_bwd_kernel(capacity, loads, u_h, w1_h, w2_h, w3_h,
                       g1, g2, g3, p0, p1, p2, p3,
-                      rows, info, us, w1s, w2s, w3s, pick, du_two, d_out, hid, da1, da3, o1, o2, o3, acc, rsem, wsem, sems, psem):
+                      rows, info, us, w1s, w2s, w3s, slots, gates, du_all, d_out, hid, da1, da3, o1, o2, o3, acc, rsem, wsem, sems, psem):
     e = pl.program_id(0)
     count = pl.num_programs(0)
     me = lax.axis_index('expert')
     slot_e = lax.rem(e, 2)
-    ring, cols, model = us.shape
+    ring, _, model = us.shape
     tokens = rows.shape[0] // 4
     ff = w1s.shape[2]
-    padded = du_two.shape[0] // 2
-    arrivals = info_copy(loads, info, rsem) + row_copies([loads.at[r] for r in range(4)], rows, rsem)
+    order = [jnp.bitwise_xor(me, r) for r in range(4)]
+    arrivals = row_copies([loads.at[p] for p in order], rows, rsem) + [info_copy(loads.at[p], info.at[r], rsem.at[4 + r]) for r, p in enumerate(order)]
     pairs = ((u_h, us), (w1_h, w1s), (w3_h, w3s), (w2_h, w2s))
 
     @pl.when(e == 0)
     def _():
         start_all(arrivals + ring_copies(pairs, wsem, 0, ring) + ring_copies(pairs, wsem, 1, ring))
         acc[...] = jnp.zeros_like(acc)
-        du_two[...] = jnp.zeros_like(du_two)
+        du_all[...] = jnp.zeros_like(du_all)
         wait_all(arrivals)
 
     @pl.when(e + 2 < count)
@@ -344,11 +367,10 @@
         start_all(ring_copies(pairs, wsem, e + 2, ring))
 
     slot_row, gate_row = route_rows(info, 1, me * count + e)
-    device = jnp.bitwise_xor(lax.broadcasted_iota(jnp.int32, slot_row.shape, 1) // tokens, me)
-    col_row = jnp.where(slot_row >= 0.0, slot_row.astype(jnp.int32) + device * capacity, -1)
-    hot = lax.broadcasted_iota(jnp.int32, (padded, 4 * tokens), 0) == col_row
-    pick[:, pl.ds(pl.multiple_of(slot_e * padded, padded), padded)] = jnp.transpose(jnp.where(hot, 1.0, 0.0).astype(BF))
-    d_out[...] = nn(jnp.where(hot, gate_row, 0.0).astype(BF)[0:cols], rows[...]).astype(BF)
+    q = lax.rem(e, QUAD)
+    keep_routes(slots, gates, q, slot_row, gate_row)
+    hot = hits(slot_row, tokens, capacity)
+    d_out[...] = nn(jnp.where(hot, gate_row, 0.0).astype(BF), rows[...]).astype(BF)
 
     def flush(idx):
         s = lax.rem(idx, 2)
@@ -385,18 +407,17 @@
         o3[slot_e, part] = tn(u[:, part], da3[...])
     fresh[0].start()
     fresh[2].start()
-    live = pl.ds(pl.multiple_of(slot_e * padded, padded), cols)
     for n in range(model // 256):
         part = slice(n * 256, (n + 1) * 256)
-        du_two[live, part] = (nt(da1[...], w1[part]) + nt(da3[...], w3[part])).astype(BF)
-
-    @pl.when(slot_e == 1)
-    def _():
-        mix_into(acc, pick[...], du_two)
+        stash(du_all, q, capacity, part, nt(da1[...], w1[part]) + nt(da3[...], w3[part]))
+
+    @pl.when((q == QUAD - 1) | (e == count - 1))
+    def _():
+        mix_into(acc, du_all, slots, gates, q, False)
 
     @pl.when(e == count - 1)
     def _():
-        sends = part_copies(acc, (p0, p1, p2, p3), psem)
+        sends = [pltpu.make_async_copy(acc.at[pl.ds(pl.multiple_of(p * tokens, tokens), tokens)], ref, psem.at[r]) for r, (p, ref) in enumerate(zip(order, (p0, p1, p2, p3)))]
         start_all(sends)
         wait_all(flush(e - 1))
         wait_all(flush(e))
@@ -407,7 +428,7 @@
     model = loads.shape[2]
     count, cols, _ = u.shape
     ff = w1.shape[2]
-    padded, ring = 256, 3
+    ring = 3
     hb = pl.BlockSpec(memory_space=pl.ANY)
     part = jax.ShapeDtypeStruct((tokens, model), F32)
     return pl.pallas_call(
@@ -419,30 +440,28 @@
         scratch_shapes=[
             pltpu.VMEM((4 * tokens, model), BF), pltpu.VMEM((4, loads.shape[1] - tokens, 3 * tokens), BF),
             pltpu.VMEM((ring, cols, model), BF), pltpu.VMEM((ring, model, ff), BF), pltpu.VMEM((ring, ff, model), BF), pltpu.VMEM((ring, model, ff), BF),
-            pltpu.VMEM((4 * tokens, 2 * padded), BF), pltpu.VMEM((2 * padded, model), BF),
+            pltpu.VMEM((8, 4 * tokens), F32), pltpu.VMEM((8, 4 * tokens), F32), pltpu.VMEM((4, QUAD * BLOCK, model), BF),
             pltpu.VMEM((cols, model), BF), pltpu.VMEM((cols, ff), BF), pltpu.VMEM((cols, ff), BF), pltpu.VMEM((cols, ff), BF),
             pltpu.VMEM((2, model, ff), F32), pltpu.VMEM((2, ff, model), F32), pltpu.VMEM((2, model, ff), F32),
             pltpu.VMEM((4 * tokens, model), F32),
-            pltpu.SemaphoreType.DMA((5,)), pltpu.SemaphoreType.DMA((ring, 4)), pltpu.SemaphoreType.DMA((2, 3)), pltpu.SemaphoreType.DMA((4,)),
+            pltpu.SemaphoreType.DMA((8,)), pltpu.SemaphoreType.DMA((ring, 4)), pltpu.SemaphoreType.DMA((2, 3)), pltpu.SemaphoreType.DMA((4,)),
         ],
-        compiler_params=pltpu.CompilerParams(vmem_limit_bytes=60 * MIB, dimension_semantics=("arbitrary",)),
+        compiler_params=pltpu.CompilerParams(vmem_limit_bytes=VMEM_BYTES, dimension_semantics=("arbitrary",)),
         cost_estimate=pl.CostEstimate(flops=50 * 10 ** 9, bytes_accessed=150 * 10 ** 6, transcendentals=0),
         name="expert_bwd",
     )(loads, u, w1, w2, w3)
 
 
 def expert_fwd_kernel(capacity, u0, u1, u2, u3, loads, b0, b1, b2, b3, w1_h, w2_h, w3_h, du_o, mine_o, out_o,
-                      rows, info, w1s, w2s, w3s, pick, out_two, acc, loc0, loc2, rx1, rx3, rxf, ra1, ra3, rsem, wsem, bsem, ssem, xsem):
+                      rows, info, w1s, w2s, w3s, slots, gates, out_all, acc, loc0, loc2, rx1, rx3, rxf, ra1, ra3, rsem, wsem, bsem, ssem, xsem):
     e = pl.program_id(0)
     count = pl.num_programs(0)
     me = lax.axis_index('expert')
     near, far = neighbours()
-    ring, _, ff = w1s.shape
-    slot_e = e % 2
+    ring, model, ff = w1s.shape
+    q = e % QUAD
     tokens = rows.shape[0] // 4
-    cols = 4 * capacity
-    padded = out_two.shape[0] // 2
-    arrivals = info_copy(loads, info, rsem) + row_copies((u0, u1, u2, u3), rows, rsem)
+    arrivals = row_copies((u0, u1, u2, u3), rows, rsem) + [info_copy(loads.at[r], info.at[r], rsem.at[4 + r]) for r in range(4)]
     pairs = ((w1_h, w1s), (w3_h, w3s), (w2_h, w2s))
     local = [pltpu.make_async_copy(b0, loc0, bsem.at[0]), pltpu.make_async_copy(b2, loc2, bsem.at[1])]
     swap3 = remote(b3, rx3, ssem.at[0], xsem.at[0], near)
@@ -459,10 +478,10 @@
         swap3.start()
         swap1.start()
         acc[...] = jnp.zeros_like(acc)
-        out_two[...] = jnp.zeros_like(out_two)
+        out_all[...] = jnp.zeros_like(out_all)
         wait_all(arrivals)
 
-    @pl.when(e == 1)
+    @pl.when(e == 3)
     def _():
         wait_all(local)
         swap3.wait()
@@ -474,11 +493,8 @@
         start_all(ring_copies(pairs, wsem, e + 2, ring))
 
     slot_row, gate_row = route_rows(info, 0, me * count + e)
-    group = lax.broadcasted_iota(jnp.int32, slot_row.shape, 1) // tokens
-    col_row = jnp.where(slot_row >= 0.0, slot_row.astype(jnp.int32) + group * capacity, -1)
-    hot = lax.broadcasted_iota(jnp.int32, (padded, 4 * tokens), 0) == col_row
-    pick[:, pl.ds(pl.multiple_of(slot_e * padded, padded), padded)] = jnp.transpose(jnp.where(hot, gate_row, 0.0).astype(BF))
-    v = nn(jnp.where(hot, 1.0, 0.0).astype(BF)[0:cols], rows[...]).astype(BF)
+    keep_routes(slots, gates, q, slot_row, gate_row)
+    v = nn(jnp.where(hits(slot_row, tokens, capacity), 1.0, 0.0).astype(BF), rows[...]).astype(BF)
     wait_all(ring_copies(pairs, wsem, e, ring))
     now = e % ring
     w1, w2, w3 = w1s.at[now], w2s.at[now], w3s.at[now]
@@ -488,11 +504,14 @@
         a1 = nn(v, w1[:, lanes]).astype(BF).astype(F32)
         a3 = nn(v, w3[:, lanes]).astype(BF).astype(F32)
         pieces.append((a1 * jax.nn.sigmoid(a1) * a3).astype(BF))
-    out_two[pl.ds(pl.multiple_of(slot_e * padded, padded), cols), :] = nn(jnp.concatenate(pieces, axis=1), w2[...]).astype(BF)
-
-    @pl.when(slot_e == 1)
-    def _():
-        mix_into(acc, pick[...], out_two)
+    hidden = jnp.concatenate(pieces, axis=1)
+    for n in range(model // 256):
+        lanes = slice(n * 256, (n + 1) * 256)
+        stash(out_all, q, capacity, lanes, nn(hidden, w2[:, lanes]))
+
+    @pl.when((q == QUAD - 1) | (e == count - 1))
+    def _():
+        mix_into(acc, out_all, slots, gates, q, True)
 
     @pl.when(e == count - 1)
     def _():
@@ -514,7 +533,7 @@
 def expert_fwd(us, loads, sums, w1, w2, w3, capacity):
     tokens, model = us[0].shape
     count, _, ff = w1.shape
-    padded, ring = 256, 3
+    ring = 3
     part = jax.ShapeDtypeStruct((tokens, model), F32)
     hb = pl.BlockSpec(memory_space=pl.ANY)
     tile = pltpu.VMEM((tokens, model), F32)
@@ -527,11 +546,11 @@
         scratch_shapes=[
             pltpu.VMEM((4 * tokens, model), BF), pltpu.VMEM((4, loads.shape[1] - tokens, 3 * tokens), BF),
             pltpu.VMEM((ring, model, ff), BF), pltpu.VMEM((ring, ff, model), BF), pltpu.VMEM((ring, model, ff), BF),
-            pltpu.VMEM((4 * tokens, 2 * padded), BF), pltpu.VMEM((2 * padded, model), BF), pltpu.VMEM((4 * tokens, model), F32),
+            pltpu.VMEM((8, 4 * tokens), F32), pltpu.VMEM((8, 4 * tokens), F32), pltpu.VMEM((4, QUAD * BLOCK, model), BF), pltpu.VMEM((4 * tokens, model), F32),
             tile, tile, tile, tile, tile, tile, tile,
-            pltpu.SemaphoreType.DMA((5,)), pltpu.SemaphoreType.DMA((ring, 3)), pltpu.SemaphoreType.DMA((2,)), pltpu.SemaphoreType.DMA((5,)), pltpu.SemaphoreType.DMA((5,)),
+            pltpu.SemaphoreType.DMA((8,)), pltpu.SemaphoreType.DMA((ring, 3)), pltpu.SemaphoreType.DMA((2,)), pltpu.SemaphoreType.DMA((5,)), pltpu.SemaphoreType.DMA((5,)),
         ],
-        compiler_params=pltpu.CompilerParams(vmem_limit_bytes=60 * MIB, dimension_semantics=("arbitrary",), collective_id=1, has_side_effects=True),
+        compiler_params=pltpu.CompilerParams(vmem_limit_bytes=VMEM_BYTES, dimension_semantics=("arbitrary",), collective_id=1, has_side_effects=True),
         cost_estimate=pl.CostEstimate(flops=16 * 10 ** 9, bytes_accessed=50 * 10 ** 6, transcendentals=0),
         name="expert_fwd",
     )(*us, loads, *sums, w1, w2, w3)

time: 132 us -> 127 us (0.962)
  Pallas kernels: 123 us -> 117 us
  other arithmetic: 0.87 us -> 2.34 us
    pallas_call x1, Pallas kernels: 32.8 us -> 30.1 us  [expert_fwd(): pl.pallas_call(functools.partial(expert_fwd_kernel, capacity), grid=(coun...]
    pallas_call x1, Pallas kernels: 56.5 us -> 54.8 us  [expert_bwd(): pl.pallas_call(functools.partial(expert_bwd_kernel, cols // 4), grid=(cou...]
    convert_element_type x1, other arithmetic: 0.87 us -> 2.34 us  [local_step(): y_a = (h_a.astype(F32) + (mine_a + far_a)).astype(BF)]
  transfers between devices with their start and end apart: 4 -> 4, of which waited for: 1 -> 1; matrix products, arithmetic and copies ran while one was open for 0% -> 0% of each run, Pallas kernels for 54% -> 55%
where the time goes in v4:
time: 127 us
  Pallas kernels  117 us (92%)
  waiting for transfers between devices  3.4 us (3%)
  starting transfers between devices  3.19 us (3%)
  other arithmetic  2.34 us (2%)
    pallas_call x1, Pallas kernels, expert_bwd(): pl.pallas_call(functools.partial(expert_bwd_kernel, cols // 4), grid=(cou...  54.8 us
    pallas_call x1, Pallas kernels, expert_fwd(): pl.pallas_call(functools.partial(expert_fwd_kernel, capacity), grid=(coun...  30.1 us
    pallas_call x1, Pallas kernels, attn_fwd(): pl.pallas_call(functools.partial(attn_fwd_kernel, kv_heads, reps, dim), o...  17 us
    pallas_call x1, Pallas kernels, attn_bwd(): pl.pallas_call(functools.partial(attn_bwd_kernel, kv_heads, reps, dim), o...  15.1 us
    ppermute x4, waiting for transfers between devices, hop(): return lax.ppermute(value, 'expert', [(i, i ^ bits) for i in range(group)])  3.4 us
    ppermute x4, starting transfers between devices, hop(): return lax.ppermute(value, 'expert', [(i, i ^ bits) for i in range(group)])  3.19 us
  transfers between devices with their start and end apart: 4, of which 1 were waited for; matrix products, arithmetic and copies ran while one was open for 0% of the time, Pallas kernels for 55%

profile of v4, /device:TPU:0, one launch (start us, length us, event | category | flops | bytes accessed | tf_op | source)
XLA Modules:
  0.0 126.7 jit_solution(10093686685293471696)
XLA Ops:
  0.6 17.0 %attn_fwd.1 = (bf16[128,1536]{1,0:T(8,128)(2,1)}, bf16[128,1536]{1,0:T(8,128)(2,1)}, bf16[128,1536]{1,0:T(8,128)(2,1)}, bf16[128,1536]{1,0:T(8,128)(2,1)}, bf16[...) custom-call(bf16[128,1536]{1,0:T(8,128)(2,1)} %xa_h.1, bf16[128,1536]{1,0:T(8,128)(2,1)} %x_b.1, ...), custom_call_target="tpu_custom_call" | custom-call | flops 10000000000 | bytes 14000000 | tf_op jit(solution)/shard_map/attn_fwd/pallas_call | solution.py:162
  17.7 0.8 collective-permute-start.2
  18.5 1.3 %collective-permute-start.1 = (bf16[128,1536]{1,0:T(8,128)(2,1)}, bf16[128,1536]{1,0:T(8,128)(2,1)}, u32[]{:S(2)}, u32[]{:S(2)}) collective-permute-start(bf16[128,1536]{1,0:T(8,128)(2,1)} %get-tuple-element.36.u0), channel_id=1, source_target_pairs={{0,2},{1,3},{2,0},{3,1},{4,6},{5,7},{6,4},{7,5}} | collective-permute-start | bytes 1179656 | tf_op jit(solution)/shard_map/ppermute | solution.py:563
  19.7 0.0 collective-permute-start
  19.7 54.8 %expert_bwd.1 = (f32[10,1536,512]{2,1,0:T(8,128)}, f32[10,512,1536]{2,1,0:T(8,128)}, f32[10,1536,512]{2,1,0:T(8,128)}, f32[128,1536]{1,0:T(8,128)}, f32[128,1536...) custom-call(bf16[4,144,1536]{2,1,0:T(8,128)(2,1)} %get-tuple-element.37.loads, bf16[10,224,1536]{2,1,0:T(8,128)(2,1)} %u_h.1, ...), custom_call_target="tpu_custom_call" | custom-call | flops 49999998976 | bytes 150000000 | tf_op jit(solution)/shard_map/expert_bwd/pallas_call | solution.py:434
  74.5 0.0 collective-permute-done.2.u3
  74.5 0.0 collective-permute-done.1.u2
  74.6 0.0 collective-permute-done.u1
  74.6 30.1 %expert_fwd.1 = (bf16[128,1536]{1,0:T(8,128)(2,1)}, f32[128,1536]{1,0:T(8,128)}, f32[128,1536]{1,0:T(8,128)}) custom-call(bf16[128,1536]{1,0:T(8,128)(2,1)} %get-tuple-element.36.u0, bf16[128,1536]{1,0:T(8,128)(2,1)} %collective-permute-done.u1, bf16[128,1536]{1,0:T(8,128)(2,1)} %collective-permute-done.1.u2, bf16[128,1536]{1,0:T(8,128)(2,1)} %collective-permute-done.2.u3, ...), custom_call_target="tpu_custom_call" | custom-call | flops 16000000000 | bytes 50000000 | tf_op jit(solution)/shard_map/expert_fwd/pallas_call | solution.py:540
  104.7 1.2 collective-permute-start.3
  105.8 15.1 %attn_bwd.1 = (bf16[128,1536]{1,0:T(8,128)(2,1)}, f32[1536,1536]{1,0:T(8,128)}, f32[512,1536]{1,0:T(8,128)}, f32[512,1536]{1,0:T(8,128)}, f32[1536,1536]{1,0:T(8...) custom-call(bf16[128,1536]{1,0:T(8,128)(2,1)} %get-tuple-element.44.du_in, bf16[128,1536]{1,0:T(8,128)(2,1)} %dy.1, ...), custom_call_target="tpu_custom_call" | custom-call | flops 14000000000 | bytes 40000000 | tf_op jit(solution)/shard_map/attn_bwd/pallas_call | solution.py:250
  121.0 3.4 %collective-permute-done.3 = f32[128,1536]{1,0:T(8,128)} collective-permute-done((f32[128,1536]{1,0:T(8,128)}, f32[128,1536]{1,0:T(8,128)}, u32[]{:S(2)}, u32[]{:S(2)}) %collective-permute-start.3) | collective-permute-done | bytes 786464 | tf_op jit(solution)/shard_map/ppermute | solution.py:563
  124.4 2.3 %add_convert_fusion = bf16[128,1536]{1,0:T(8,128)(2,1)} fusion(f32[128,1536]{1,0:T(8,128)} %get-tuple-element.42, f32[128,1536]{1,0:T(8,128)} %collective-permute-done.3, bf16[128,1536]{1,0:T(8,128)(2,1)} %get-tuple-element.35), kind=kLoop, calls=%fused_computation | loop fusion | flops 786432 | bytes 2359296 | tf_op jit(solution)/shard_map/convert_element_type | solution.py:578
Async XLA Ops:
  17.7 56.8 %collective-permute-start.2 = (bf16[128,1536]{1,0:T(8,128)(2,1)}, bf16[128,1536]{1,0:T(8,128)(2,1)}, u32[]{:S(2)}, u32[]{:S(2)}) collective-permute-start(bf16[128,1536]{1,0:T(8,128)(2,1)} %get-tuple-element.36.u0), channel_id=1, source_target_pairs={{0,3},{1,2},{2,1},{3,0},{4,7},{5,6},{6,5},{7,4}} | collective-permute-start | bytes 1179656 | tf_op jit(solution)/shard_map/ppermute | solution.py:563
  18.5 56.1 %collective-permute-start.1 = (bf16[128,1536]{1,0:T(8,128)(2,1)}, bf16[128,1536]{1,0:T(8,128)(2,1)}, u32[]{:S(2)}, u32[]{:S(2)}) collective-permute-start(bf16[128,1536]{1,0:T(8,128)(2,1)} %get-tuple-element.36.u0), channel_id=1, source_target_pairs={{0,2},{1,3},{2,0},{3,1},{4,6},{5,7},{6,4},{7,5}} | collective-permute-start | bytes 1179656 | tf_op jit(solution)/shard_map/ppermute | solution.py:563
  19.7 54.8 %collective-permute-start = (bf16[128,1536]{1,0:T(8,128)(2,1)}, bf16[128,1536]{1,0:T(8,128)(2,1)}, u32[]{:S(2)}, u32[]{:S(2)}) collective-permute-start(bf16[128,1536]{1,0:T(8,128)(2,1)} %get-tuple-element.36.u0), channel_id=1, source_target_pairs={{0,1},{1,0},{2,3},{3,2},{4,5},{5,4},{6,7},{7,6}} | collective-permute-start | bytes 1179656 | tf_op jit(solution)/shard_map/ppermute | solution.py:563
  104.7 19.7 %collective-permute-start.3 = (f32[128,1536]{1,0:T(8,128)}, f32[128,1536]{1,0:T(8,128)}, u32[]{:S(2)}, u32[]{:S(2)}) collective-permute-start(f32[128,1536]{1,0:T(8,128)} %get-tuple-element.43), channel_id=1, source_target_pairs={{0,2},{1,3},{2,0},{3,1},{4,6},{5,7},{6,4},{7,5}} | collective-permute-start | bytes 2359304 | tf_op jit(solution)/shard_map/ppermute | solution.py:563

commit v5 on v4

--- a/solution.py
+++ b/solution.py
@@ -82,15 +82,17 @@
 
 def attn_fwd_kernel(kv_heads, reps, dim, xa_h, xb_h, dy_h, ea, sa, ga, eb, sb, gb, n1, n2, wq_h, wk_h, wv_h, wo_h,
                     ha_h, ua_h, hb_h, nb_h, qkv_h, ctx_h, load_h,
-                    xs, wq, wk, wv, wo, nrm, nrm_t, q_t, k_t, v_t, ctx, q_b, ctx_b, hs, ua, mine, far_in, sems, osems, ssem, rsem):
+                    xs, wq, wk, wv, wo, nrm, nrm_t, q_t, k_t, v_t, ctx, q_b, ctx_b, hs, ua, mine, far_in, ints, gates, sems, osems, ssem, rsem, tsem):
     near, far = neighbours()
     tokens = xs.shape[0] // 2
+    small = ((ea, ints.at[0]), (sa, ints.at[1]), (eb, ints.at[2]), (sb, ints.at[3]), (ga, gates.at[0]), (gb, gates.at[1]))
+    tiny = [pltpu.make_async_copy(s, d, tsem.at[i]) for i, (s, d) in enumerate(small)]
     heads = kv_heads * reps
     first, second = slice(0, tokens), slice(tokens, 2 * tokens)
     half = heads * dim // 2
     moves = ((dy_h, mine.at[0:tokens]), (xa_h, xs.at[first]), (xb_h, xs.at[second]), (wk_h, wk), (wv_h, wv), (wq_h.at[0:half], wq.at[0:half]), (wq_h.at[half:], wq.at[half:]), (wo_h, wo))
     copies = [pltpu.make_async_copy(s, d, sems.at[i]) for i, (s, d) in enumerate(moves)]
-    start_all(copies)
+    start_all(copies[0:1] + tiny + copies[1:])
     outs = []
 
     def flush(src, dst):
@@ -98,10 +100,11 @@
         c.start()
         outs.append(c)
 
-    fields = [r[...].astype(F32) for r in (ea, sa, ga, eb, sb, gb)]
+    greet((near, far))
+    wait_all(tiny)
+    fields = [v.astype(F32) for v in (ints[0], ints[1], gates[0], ints[2], ints[3], gates[1])]
     both = jnp.concatenate([jnp.concatenate(fields[0:3], axis=1), jnp.concatenate(fields[3:6], axis=1)], axis=0)
     mine[tokens:] = jnp.concatenate([both, jnp.zeros((both.shape[0], mine.shape[1] - both.shape[1]), F32)], axis=1).astype(BF)
-    greet((near, far))
     copies[0].wait()
     to_far = remote(mine, far_in, ssem.at[0], rsem.at[0], far)
     to_near = remote(mine, load_h.at[1], ssem.at[1], rsem.at[1], near)
@@ -162,7 +165,7 @@
     return pl.pallas_call(
         functools.partial(attn_fwd_kernel, kv_heads, reps, dim),
         out_shape=(row, row, row, row, jax.ShapeDtypeStruct((q_dim + 2 * kv_dim, tokens), BF), jax.ShapeDtypeStruct((q_dim, tokens), BF), jax.ShapeDtypeStruct((4, tokens + depth, model), BF)),
-        in_specs=[hb] * 3 + [vm] * 8 + [hb] * 4,
+        in_specs=[hb] * 9 + [vm] * 2 + [hb] * 4,
         out_specs=(hb,) * 7,
         scratch_shapes=[
             pltpu.VMEM((2 * tokens, model), BF),
@@ -171,7 +174,8 @@
             pltpu.VMEM((q_dim, 2 * tokens), BF), pltpu.VMEM((kv_dim, 2 * tokens), BF), pltpu.VMEM((kv_dim, 2 * tokens), BF), pltpu.VMEM((q_dim, 2 * tokens), BF),
             pltpu.VMEM((q_dim + 2 * kv_dim, tokens), BF), pltpu.VMEM((q_dim, tokens), BF), pltpu.VMEM((2 * tokens, model), BF), pltpu.VMEM((tokens, model), BF),
             pltpu.VMEM((tokens + depth, model), BF), pltpu.VMEM((tokens + depth, model), BF),
-            pltpu.SemaphoreType.DMA((8,)), pltpu.SemaphoreType.DMA((8,)), pltpu.SemaphoreType.DMA((3,)), pltpu.SemaphoreType.DMA((3,)),
+            pltpu.VMEM((4,) + fields[0].shape, jnp.int32), pltpu.VMEM((2,) + fields[2].shape, BF),
+            pltpu.SemaphoreType.DMA((8,)), pltpu.SemaphoreType.DMA((8,)), pltpu.SemaphoreType.DMA((3,)), pltpu.SemaphoreType.DMA((3,)), pltpu.SemaphoreType.DMA((6,)),
         ],
         compiler_params=pltpu.CompilerParams(vmem_limit_bytes=VMEM_BYTES, collective_id=0, has_side_effects=True),
         cost_estimate=pl.CostEstimate(flops=10 ** 10, bytes_accessed=14 * 10 ** 6, transcendentals=0),
@@ -261,7 +265,7 @@
             pltpu.VMEM((q_dim, tokens), BF), pltpu.VMEM((q_dim, tokens), BF), pltpu.VMEM((kv_dim, tokens), BF), pltpu.VMEM((kv_dim, tokens), BF),
             pltpu.SemaphoreType.DMA((4,)), pltpu.SemaphoreType.DMA((n_out,)),
         ],
-        compiler_params=pltpu.CompilerParams(vmem_limit_bytes=VMEM_BYTES),
+        compiler_params=pltpu.CompilerParams(vmem_limit_bytes=60 * 1024 * 1024),
         cost_estimate=pl.CostEstimate(flops=14 * 10 ** 9, bytes_accessed=40 * 10 ** 6, transcendentals=0),
         name="attn_bwd",
     )(du, dy, h_b, x_b, nb, qkv, ctx, n1, n2, wo, wq, wk, wv)
@@ -476,17 +480,17 @@
         start_all(arrivals + ring_copies(pairs, wsem, 0, ring) + ring_copies(pairs, wsem, 1, ring) + local)
         greet((near, far))
         swap3.start()
-        swap1.start()
         acc[...] = jnp.zeros_like(acc)
         out_all[...] = jnp.zeros_like(out_all)
         wait_all(arrivals)
 
-    @pl.when(e == 3)
+    @pl.when(e == 1)
     def _():
         wait_all(local)
         swap3.wait()
         loc2[...] += rx3[...]
         over.start()
+        swap1.start()
 
     @pl.when(e + 2 < count)
     def _():

time: 127 us -> 127 us (level)
  other arithmetic: 2.34 us -> 0.87 us
    pallas_call x1, Pallas kernels: 17 us -> 19.4 us  [attn_fwd(): pl.pallas_call(functools.partial(attn_fwd_kernel, kv_heads, reps, dim), o...]
    convert_element_type x1, other arithmetic: 2.34 us -> 0.87 us  [local_step(): y_a = (h_a.astype(F32) + (mine_a + far_a)).astype(BF)]
where the time goes in v5:
time: 127 us
  Pallas kernels  118 us (93%)
  waiting for transfers between devices  4.54 us (4%)
  starting transfers between devices  2.05 us (2%)
    pallas_call x1, Pallas kernels, expert_bwd(): pl.pallas_call(functools.partial(expert_bwd_kernel, cols // 4), grid=(cou...  54.8 us
    pallas_call x1, Pallas kernels, expert_fwd(): pl.pallas_call(functools.partial(expert_fwd_kernel, capacity), grid=(coun...  29.1 us
    pallas_call x1, Pallas kernels, attn_fwd(): pl.pallas_call(functools.partial(attn_fwd_kernel, kv_heads, reps, dim), o...  19.4 us
    pallas_call x1, Pallas kernels, attn_bwd(): pl.pallas_call(functools.partial(attn_bwd_kernel, kv_heads, reps, dim), o...  15.2 us
    ppermute x4, waiting for transfers between devices, hop(): return lax.ppermute(value, 'expert', [(i, i ^ bits) for i in range(group)])  4.54 us
  transfers between devices with their start and end apart: 4, of which 1 were waited for; matrix products, arithmetic and copies ran while one was open for 0% of the time, Pallas kernels for 55%

profile of v5, /device:TPU:0, one launch (start us, length us, event | category | flops | bytes accessed | tf_op | source)
XLA Modules:
  0.0 126.7 jit_solution(17172117921678904627)
XLA Ops:
  0.6 19.4 %attn_fwd.1 = (bf16[128,1536]{1,0:T(8,128)(2,1)}, bf16[128,1536]{1,0:T(8,128)(2,1)}, bf16[128,1536]{1,0:T(8,128)(2,1)}, bf16[128,1536]{1,0:T(8,128)(2,1)}, bf16[...) custom-call(bf16[128,1536]{1,0:T(8,128)(2,1)} %xa_h.1, bf16[128,1536]{1,0:T(8,128)(2,1)} %x_b.1, ...), custom_call_target="tpu_custom_call" | custom-call | flops 10000000000 | bytes 14000000 | tf_op jit(solution)/shard_map/attn_fwd/pallas_call | solution.py:165
  20.0 0.2 collective-permute-start.2
  20.2 1.8 %collective-permute-start.1 = (bf16[128,1536]{1,0:T(8,128)(2,1)}, bf16[128,1536]{1,0:T(8,128)(2,1)}, u32[]{:S(2)}, u32[]{:S(2)}) collective-permute-start(bf16[128,1536]{1,0:T(8,128)(2,1)} %get-tuple-element.36.u0), channel_id=1, source_target_pairs={{0,2},{1,3},{2,0},{3,1},{4,6},{5,7},{6,4},{7,5}} | collective-permute-start | bytes 1179656 | tf_op jit(solution)/shard_map/ppermute | solution.py:567
  22.1 0.0 collective-permute-start
  22.1 54.8 %expert_bwd.1 = (f32[10,1536,512]{2,1,0:T(8,128)}, f32[10,512,1536]{2,1,0:T(8,128)}, f32[10,1536,512]{2,1,0:T(8,128)}, f32[128,1536]{1,0:T(8,128)}, f32[128,1536...) custom-call(bf16[4,144,1536]{2,1,0:T(8,128)(2,1)} %get-tuple-element.37.loads, bf16[10,224,1536]{2,1,0:T(8,128)(2,1)} %u_h.1, ...), custom_call_target="tpu_custom_call" | custom-call | flops 49999998976 | bytes 150000000 | tf_op jit(solution)/shard_map/expert_bwd/pallas_call | solution.py:438
  76.8 0.0 collective-permute-done.2.u3
  76.8 0.0 collective-permute-done.1.u2
  76.8 0.0 collective-permute-done.u1
  76.9 29.1 %expert_fwd.1 = (bf16[128,1536]{1,0:T(8,128)(2,1)}, f32[128,1536]{1,0:T(8,128)}, f32[128,1536]{1,0:T(8,128)}) custom-call(bf16[128,1536]{1,0:T(8,128)(2,1)} %get-tuple-element.36.u0, bf16[128,1536]{1,0:T(8,128)(2,1)} %collective-permute-done.u1, bf16[128,1536]{1,0:T(8,128)(2,1)} %collective-permute-done.1.u2, bf16[128,1536]{1,0:T(8,128)(2,1)} %collective-permute-done.2.u3, ...), custom_call_target="tpu_custom_call" | custom-call | flops 16000000000 | bytes 50000000 | tf_op jit(solution)/shard_map/expert_fwd/pallas_call | solution.py:544
  106.0 0.0 collective-permute-start.3
  106.0 0.0 copy-start
  106.0 0.0 copy-start.1
  106.0 15.2 %attn_bwd.1 = (bf16[128,1536]{1,0:T(8,128)(2,1)}, f32[1536,1536]{1,0:T(8,128)}, f32[512,1536]{1,0:T(8,128)}, f32[512,1536]{1,0:T(8,128)}, f32[1536,1536]{1,0:T(8...) custom-call(bf16[128,1536]{1,0:T(8,128)(2,1)} %get-tuple-element.44.du_in, bf16[128,1536]{1,0:T(8,128)(2,1)} %dy.1, ...), custom_call_target="tpu_custom_call" | custom-call | flops 14000000000 | bytes 40000000 | tf_op jit(solution)/shard_map/attn_bwd/pallas_call | solution.py:254
  121.3 4.5 %collective-permute-done.3 = f32[128,1536]{1,0:T(8,128)S(1)} collective-permute-done((f32[128,1536]{1,0:T(8,128)}, f32[128,1536]{1,0:T(8,128)S(1)}, u32[]{:S(2)}, u32[]{:S(2)}) %collective-permute-start.3) | collective-permute-done | bytes 786464 | tf_op jit(solution)/shard_map/ppermute | solution.py:567
  125.8 0.0 copy-done
  125.8 0.0 copy-done.1
  125.8 0.9 add_convert_fusion
Async XLA Ops:
  20.0 56.8 %collective-permute-start.2 = (bf16[128,1536]{1,0:T(8,128)(2,1)}, bf16[128,1536]{1,0:T(8,128)(2,1)}, u32[]{:S(2)}, u32[]{:S(2)}) collective-permute-start(bf16[128,1536]{1,0:T(8,128)(2,1)} %get-tuple-element.36.u0), channel_id=1, source_target_pairs={{0,3},{1,2},{2,1},{3,0},{4,7},{5,6},{6,5},{7,4}} | collective-permute-start | bytes 1179656 | tf_op jit(solution)/shard_map/ppermute | solution.py:567
  20.2 56.6 %collective-permute-start.1 = (bf16[128,1536]{1,0:T(8,128)(2,1)}, bf16[128,1536]{1,0:T(8,128)(2,1)}, u32[]{:S(2)}, u32[]{:S(2)}) collective-permute-start(bf16[128,1536]{1,0:T(8,128)(2,1)} %get-tuple-element.36.u0), channel_id=1, source_target_pairs={{0,2},{1,3},{2,0},{3,1},{4,6},{5,7},{6,4},{7,5}} | collective-permute-start | bytes 1179656 | tf_op jit(solution)/shard_map/ppermute | solution.py:567
  22.1 54.8 %collective-permute-start = (bf16[128,1536]{1,0:T(8,128)(2,1)}, bf16[128,1536]{1,0:T(8,128)(2,1)}, u32[]{:S(2)}, u32[]{:S(2)}) collective-permute-start(bf16[128,1536]{1,0:T(8,128)(2,1)} %get-tuple-element.36.u0), channel_id=1, source_target_pairs={{0,1},{1,0},{2,3},{3,2},{4,5},{5,4},{6,7},{7,6}} | collective-permute-start | bytes 1179656 | tf_op jit(solution)/shard_map/ppermute | solution.py:567
  106.0 19.8 %collective-permute-start.3 = (f32[128,1536]{1,0:T(8,128)}, f32[128,1536]{1,0:T(8,128)S(1)}, u32[]{:S(2)}, u32[]{:S(2)}) collective-permute-start(f32[128,1536]{1,0:T(8,128)} %get-tuple-element.43), channel_id=1, source_target_pairs={{0,2},{1,3},{2,0},{3,1},{4,6},{5,7},{6,4},{7,5}} | collective-permute-start | bytes 2359304 | tf_op jit(solution)/shard_map/ppermute | solution.py:567
  106.0 19.8 %copy-start = (f32[128,1536]{1,0:T(8,128)S(1)}, f32[128,1536]{1,0:T(8,128)}, u32[]{:S(2)}) copy-start(f32[128,1536]{1,0:T(8,128)} %get-tuple-element.42) | copy-start | bytes 2359300
  106.0 19.8 %copy-start.1 = (bf16[128,1536]{1,0:T(8,128)(2,1)S(1)}, bf16[128,1536]{1,0:T(8,128)(2,1)}, u32[]{:S(2)}) copy-start(bf16[128,1536]{1,0:T(8,128)(2,1)} %get-tuple-element.35) | copy-start | bytes 1179652

commit v6 on v5

--- a/solution.py
+++ b/solution.py
@@ -92,7 +92,8 @@
     half = heads * dim // 2
     moves = ((dy_h, mine.at[0:tokens]), (xa_h, xs.at[first]), (xb_h, xs.at[second]), (wk_h, wk), (wv_h, wv), (wq_h.at[0:half], wq.at[0:half]), (wq_h.at[half:], wq.at[half:]), (wo_h, wo))
     copies = [pltpu.make_async_copy(s, d, sems.at[i]) for i, (s, d) in enumerate(moves)]
-    start_all(copies[0:1] + tiny + copies[1:])
+    start_all(copies[0:1] + tiny + copies[1:3])
+    start_all(copies[3:], 1)
     outs = []
 
     def flush(src, dst):
@@ -309,9 +310,9 @@
     return lax.broadcasted_iota(jnp.int32, (4 * capacity, slot_row.shape[1]), 0) == col_row
 
 
-def start_all(copies):
+def start_all(copies, priority=0):
     for c in copies:
-        c.start()
+        c.start(priority=priority)
 
 
 def wait_all(copies):
@@ -477,7 +478,8 @@
 
     @pl.when(e == 0)
     def _():
-        start_all(arrivals + ring_copies(pairs, wsem, 0, ring) + ring_copies(pairs, wsem, 1, ring) + local)
+        start_all(arrivals + local)
+        start_all(ring_copies(pairs, wsem, 0, ring) + ring_copies(pairs, wsem, 1, ring), 1)
         greet((near, far))
         swap3.start()
         acc[...] = jnp.zeros_like(acc)
@@ -494,7 +496,7 @@
 
     @pl.when(e + 2 < count)
     def _():
-        start_all(ring_copies(pairs, wsem, e + 2, ring))
+        start_all(ring_copies(pairs, wsem, e + 2, ring), 1)
 
     slot_row, gate_row = route_rows(info, 0, me * count + e)
     keep_routes(slots, gates, q, slot_row, gate_row)

time: 127 us -> 124 us (0.976)
  Pallas kernels: 118 us -> 115 us
    pallas_call x1, Pallas kernels: 19.4 us -> 17.1 us  [attn_fwd(): pl.pallas_call(functools.partial(attn_fwd_kernel, kv_heads, reps, dim), o...]
  transfers between devices with their start and end apart: 4 -> 4, of which waited for: 1 -> 1; matrix products, arithmetic and copies ran while one was open for 0% -> 0% of each run, Pallas kernels for 55% -> 57%
where the time goes in v6:
time: 124 us
  Pallas kernels  115 us (93%)
  waiting for transfers between devices  4.12 us (3%)
  starting transfers between devices  2.5 us (2%)
    pallas_call x1, Pallas kernels, expert_bwd(): pl.pallas_call(functools.partial(expert_bwd_kernel, cols // 4), grid=(cou...  54.8 us
    pallas_call x1, Pallas kernels, expert_fwd(): pl.pallas_call(functools.partial(expert_fwd_kernel, capacity), grid=(coun...  28.3 us
    pallas_call x1, Pallas kernels, attn_fwd(): pl.pallas_call(functools.partial(attn_fwd_kernel, kv_heads, reps, dim), o...  17.1 us
    pallas_call x1, Pallas kernels, attn_bwd(): pl.pallas_call(functools.partial(attn_bwd_kernel, kv_heads, reps, dim), o...  15.2 us
    ppermute x4, waiting for transfers between devices, hop(): return lax.ppermute(value, 'expert', [(i, i ^ bits) for i in range(group)])  4.12 us
    ppermute x4, starting transfers between devices, hop(): return lax.ppermute(value, 'expert', [(i, i ^ bits) for i in range(group)])  2.5 us
  transfers between devices with their start and end apart: 4, of which 1 were waited for; matrix products, arithmetic and copies ran while one was open for 0% of the time, Pallas kernels for 57%

profile of v6, /device:TPU:0, one launch (start us, length us, event | category | flops | bytes accessed | tf_op | source)
XLA Modules:
  0.0 123.6 jit_solution(737633792023409134)
XLA Ops:
  0.6 17.1 %attn_fwd.1 = (bf16[128,1536]{1,0:T(8,128)(2,1)}, bf16[128,1536]{1,0:T(8,128)(2,1)}, bf16[128,1536]{1,0:T(8,128)(2,1)}, bf16[128,1536]{1,0:T(8,128)(2,1)}, bf16[...) custom-call(bf16[128,1536]{1,0:T(8,128)(2,1)} %xa_h.1, bf16[128,1536]{1,0:T(8,128)(2,1)} %x_b.1, ...), custom_call_target="tpu_custom_call" | custom-call | flops 10000000000 | bytes 14000000 | tf_op jit(solution)/shard_map/attn_fwd/pallas_call | solution.py:166
  17.8 0.7 collective-permute-start.2
  18.4 1.4 %collective-permute-start.1 = (bf16[128,1536]{1,0:T(8,128)(2,1)}, bf16[128,1536]{1,0:T(8,128)(2,1)}, u32[]{:S(2)}, u32[]{:S(2)}) collective-permute-start(bf16[128,1536]{1,0:T(8,128)(2,1)} %get-tuple-element.36.u0), channel_id=1, source_target_pairs={{0,2},{1,3},{2,0},{3,1},{4,6},{5,7},{6,4},{7,5}} | collective-permute-start | bytes 1179656 | tf_op jit(solution)/shard_map/ppermute | solution.py:569
  19.8 0.0 collective-permute-start
  19.8 54.8 %expert_bwd.1 = (f32[10,1536,512]{2,1,0:T(8,128)}, f32[10,512,1536]{2,1,0:T(8,128)}, f32[10,1536,512]{2,1,0:T(8,128)}, f32[128,1536]{1,0:T(8,128)}, f32[128,1536...) custom-call(bf16[4,144,1536]{2,1,0:T(8,128)(2,1)} %get-tuple-element.37.loads, bf16[10,224,1536]{2,1,0:T(8,128)(2,1)} %u_h.1, ...), custom_call_target="tpu_custom_call" | custom-call | flops 49999998976 | bytes 150000000 | tf_op jit(solution)/shard_map/expert_bwd/pallas_call | solution.py:439
  74.5 0.0 collective-permute-done.2.u3
  74.5 0.0 collective-permute-done.1.u2
  74.6 0.0 collective-permute-done.u1
  74.6 28.3 %expert_fwd.1 = (bf16[128,1536]{1,0:T(8,128)(2,1)}, f32[128,1536]{1,0:T(8,128)}, f32[128,1536]{1,0:T(8,128)}) custom-call(bf16[128,1536]{1,0:T(8,128)(2,1)} %get-tuple-element.36.u0, bf16[128,1536]{1,0:T(8,128)(2,1)} %collective-permute-done.u1, bf16[128,1536]{1,0:T(8,128)(2,1)} %collective-permute-done.1.u2, bf16[128,1536]{1,0:T(8,128)(2,1)} %collective-permute-done.2.u3, ...), custom_call_target="tpu_custom_call" | custom-call | flops 16000000000 | bytes 50000000 | tf_op jit(solution)/shard_map/expert_fwd/pallas_call | solution.py:546
  102.9 0.5 collective-permute-start.3
  103.3 0.0 copy-start
  103.3 0.0 copy-start.1
  103.3 15.2 %attn_bwd.1 = (bf16[128,1536]{1,0:T(8,128)(2,1)}, f32[1536,1536]{1,0:T(8,128)}, f32[512,1536]{1,0:T(8,128)}, f32[512,1536]{1,0:T(8,128)}, f32[1536,1536]{1,0:T(8...) custom-call(bf16[128,1536]{1,0:T(8,128)(2,1)} %get-tuple-element.44.du_in, bf16[128,1536]{1,0:T(8,128)(2,1)} %dy.1, ...), custom_call_target="tpu_custom_call" | custom-call | flops 14000000000 | bytes 40000000 | tf_op jit(solution)/shard_map/attn_bwd/pallas_call | solution.py:255
  118.6 4.1 %collective-permute-done.3 = f32[128,1536]{1,0:T(8,128)S(1)} collective-permute-done((f32[128,1536]{1,0:T(8,128)}, f32[128,1536]{1,0:T(8,128)S(1)}, u32[]{:S(2)}, u32[]{:S(2)}) %collective-permute-start.3) | collective-permute-done | bytes 786464 | tf_op jit(solution)/shard_map/ppermute | solution.py:569
  122.7 0.0 copy-done
  122.7 0.0 copy-done.1
  122.7 0.9 add_convert_fusion
Async XLA Ops:
  17.8 56.8 %collective-permute-start.2 = (bf16[128,1536]{1,0:T(8,128)(2,1)}, bf16[128,1536]{1,0:T(8,128)(2,1)}, u32[]{:S(2)}, u32[]{:S(2)}) collective-permute-start(bf16[128,1536]{1,0:T(8,128)(2,1)} %get-tuple-element.36.u0), channel_id=1, source_target_pairs={{0,3},{1,2},{2,1},{3,0},{4,7},{5,6},{6,5},{7,4}} | collective-permute-start | bytes 1179656 | tf_op jit(solution)/shard_map/ppermute | solution.py:569
  18.4 56.1 %collective-permute-start.1 = (bf16[128,1536]{1,0:T(8,128)(2,1)}, bf16[128,1536]{1,0:T(8,128)(2,1)}, u32[]{:S(2)}, u32[]{:S(2)}) collective-permute-start(bf16[128,1536]{1,0:T(8,128)(2,1)} %get-tuple-element.36.u0), channel_id=1, source_target_pairs={{0,2},{1,3},{2,0},{3,1},{4,6},{5,7},{6,4},{7,5}} | collective-permute-start | bytes 1179656 | tf_op jit(solution)/shard_map/ppermute | solution.py:569
  19.8 54.8 %collective-permute-start = (bf16[128,1536]{1,0:T(8,128)(2,1)}, bf16[128,1536]{1,0:T(8,128)(2,1)}, u32[]{:S(2)}, u32[]{:S(2)}) collective-permute-start(bf16[128,1536]{1,0:T(8,128)(2,1)} %get-tuple-element.36.u0), channel_id=1, source_target_pairs={{0,1},{1,0},{2,3},{3,2},{4,5},{5,4},{6,7},{7,6}} | collective-permute-start | bytes 1179656 | tf_op jit(solution)/shard_map/ppermute | solution.py:569
  102.9 19.8 %collective-permute-start.3 = (f32[128,1536]{1,0:T(8,128)}, f32[128,1536]{1,0:T(8,128)S(1)}, u32[]{:S(2)}, u32[]{:S(2)}) collective-permute-start(f32[128,1536]{1,0:T(8,128)} %get-tuple-element.43), channel_id=1, source_target_pairs={{0,2},{1,3},{2,0},{3,1},{4,6},{5,7},{6,4},{7,5}} | collective-permute-start | bytes 2359304 | tf_op jit(solution)/shard_map/ppermute | solution.py:569
  103.3 19.3 %copy-start = (f32[128,1536]{1,0:T(8,128)S(1)}, f32[128,1536]{1,0:T(8,128)}, u32[]{:S(2)}) copy-start(f32[128,1536]{1,0:T(8,128)} %get-tuple-element.42) | copy-start | bytes 2359300
  103.3 19.3 %copy-start.1 = (bf16[128,1536]{1,0:T(8,128)(2,1)S(1)}, bf16[128,1536]{1,0:T(8,128)(2,1)}, u32[]{:S(2)}) copy-start(bf16[128,1536]{1,0:T(8,128)(2,1)} %get-tuple-element.35) | copy-start | bytes 1179652

commit v7 on v6

--- a/solution.py
+++ b/solution.py
@@ -184,19 +184,20 @@
     )(x_a, x_b, dy, *fields, n1, n2, wq, wk, wv, wo)
 
 
-def attn_bwd_kernel(kv_heads, reps, dim, du_in, dy, h_b, x_b, nb, qkv, ctx, n1, n2, wo_h, wq_h, wk_h, wv_h,
-                    dx, gq, gk, gv, go, gn1, gn2,
-                    wo, wq, wk, wv, oq, ok, ov, oo, dctx, dq, dk, dv, sems, osems):
+def attn_bwd_kernel(kv_heads, reps, dim, du_in, dy, h_b, x_b, nb, qkv, ctx, n1, n2, wo_h, wq_h, wk_h, wv_h, g1_in, g2_in, g3_in, u_h, hid_h, da1_h, da3_h, do_h,
+                    dx, gq, gk, gv, go, gn1, gn2, g1, g2, g3,
+                    wo, wq, wk, wv, oq, ok, ov, oo, dctx, dq, dk, dv, u, hid, da1, da3, d_out, o1, o2, o3, sems, osems, esems):
+    last = u_h.shape[0] - 1
+    extra = [pltpu.make_async_copy(s, d, esems.at[i]) for i, (s, d) in enumerate(((do_h, d_out), (hid_h, hid), (u_h.at[last], u), (da1_h, da1), (da3_h, da3)))]
+    start_all(extra)
     copies = [pltpu.make_async_copy(s, d, sems.at[i]) for i, (s, d) in enumerate(((wo_h, wo), (wq_h, wq), (wk_h, wk), (wv_h, wv)))]
-    for c in copies:
-        c.start()
+    start_all(copies, 1)
     tokens = x_b.shape[0]
     q_dim, kv_dim = kv_heads * reps * dim, kv_heads * dim
     du = du_in[...].astype(F32)
-    grad_h, g2 = rms_pull(h_b[...].astype(F32), row_of(n2), du)
-    gn2[...] = g2
+    grad_h, gain_2 = rms_pull(h_b[...].astype(F32), row_of(n2), du)
+    gn2[...] = gain_2
     dh = (dy[...].astype(F32) + grad_h).astype(BF)
-    copies[0].wait()
     outs = []
 
     def flush(src, dst):
@@ -204,6 +205,17 @@
         c.start()
         outs.append(c)
 
+    wait_all(extra)
+    for m in range(hid.shape[1] // 256):
+        part = slice(m * 256, (m + 1) * 256)
+        o2[part] = tn(hid[:, part], d_out[...])
+    flush(o2, g2.at[last])
+    for grad, cot, dst in ((o1, da1, g1), (o3, da3, g3)):
+        for m in range(u.shape[1] // 256):
+            part = slice(m * 256, (m + 1) * 256)
+            grad[part] = tn(u[:, part], cot[...])
+        flush(grad, dst.at[last])
+    copies[0].wait()
     step = q_dim // 4
     for i in range(4):
         dctx[i * step:(i + 1) * step] = nt(wo[i * step:(i + 1) * step], dh).astype(BF)
@@ -239,37 +251,41 @@
     for c in copies[1:]:
         c.wait()
     dn = (tn(dq[...], wq[...]) + tn(dk[...], wk[...]) + tn(dv[...], wv[...])).astype(BF).astype(F32)
-    grad_x, g1 = rms_pull(x_b[...].astype(F32), row_of(n1), dn)
-    gn1[...] = g1
+    grad_x, gain_1 = rms_pull(x_b[...].astype(F32), row_of(n1), dn)
+    gn1[...] = gain_1
     dx[...] = (dh.astype(F32) + grad_x).astype(BF)
     for c in outs:
         c.wait()
 
 
-def attn_bwd(du, dy, h_b, x_b, nb, qkv, ctx, n1, n2, wo, wq, wk, wv, kv_heads, reps, dim):
+def attn_bwd(du, dy, h_b, x_b, nb, qkv, ctx, n1, n2, wo, wq, wk, wv, grads, u, keeps, kv_heads, reps, dim):
     tokens, model = x_b.shape
     q_dim, kv_dim = kv_heads * reps * dim, kv_heads * dim
     vm = pl.BlockSpec(memory_space=pltpu.VMEM)
     hb = pl.BlockSpec(memory_space=pl.ANY)
-    n_out = 4 + kv_heads // 2 + 2
+    n_out = 4 + kv_heads // 2 + 2 + 3
+    cols, ff = keeps[0].shape
+    kept = pltpu.VMEM((cols, ff), BF)
     return pl.pallas_call(
         functools.partial(attn_bwd_kernel, kv_heads, reps, dim),
         out_shape=(
             jax.ShapeDtypeStruct((tokens, model), BF), jax.ShapeDtypeStruct((q_dim, model), F32), jax.ShapeDtypeStruct((kv_dim, model), F32),
             jax.ShapeDtypeStruct((kv_dim, model), F32), jax.ShapeDtypeStruct((q_dim, model), F32), jax.ShapeDtypeStruct((1, model), F32), jax.ShapeDtypeStruct((1, model), F32),
-        ),
-        in_specs=[vm] * 9 + [hb] * 4,
-        out_specs=(vm, hb, hb, hb, hb, vm, vm),
+        ) + tuple(jax.ShapeDtypeStruct(g.shape, F32) for g in grads),
+        in_specs=[vm] * 9 + [hb] * 12,
+        out_specs=(vm, hb, hb, hb, hb, vm, vm, hb, hb, hb),
+        input_output_aliases={13: 7, 14: 8, 15: 9},
         scratch_shapes=[
             pltpu.VMEM((q_dim, model), BF), pltpu.VMEM((q_dim, model), BF), pltpu.VMEM((kv_dim, model), BF), pltpu.VMEM((kv_dim, model), BF),
             pltpu.VMEM((q_dim, model), F32), pltpu.VMEM((kv_dim, model), F32), pltpu.VMEM((kv_dim, model), F32), pltpu.VMEM((q_dim, model), F32),
             pltpu.VMEM((q_dim, tokens), BF), pltpu.VMEM((q_dim, tokens), BF), pltpu.VMEM((kv_dim, tokens), BF), pltpu.VMEM((kv_dim, tokens), BF),
-            pltpu.SemaphoreType.DMA((4,)), pltpu.SemaphoreType.DMA((n_out,)),
+            pltpu.VMEM((cols, model), BF), kept, kept, kept, pltpu.VMEM((cols, model), BF), pltpu.VMEM((model, ff), F32), pltpu.VMEM((ff, model), F32), pltpu.VMEM((model, ff), F32),
+            pltpu.SemaphoreType.DMA((4,)), pltpu.SemaphoreType.DMA((n_out,)), pltpu.SemaphoreType.DMA((5,)),
         ],
         compiler_params=pltpu.CompilerParams(vmem_limit_bytes=60 * 1024 * 1024),
         cost_estimate=pl.CostEstimate(flops=14 * 10 ** 9, bytes_accessed=40 * 10 ** 6, transcendentals=0),
         name="attn_bwd",
-    )(du, dy, h_b, x_b, nb, qkv, ctx, n1, n2, wo, wq, wk, wv)
+    )(du, dy, h_b, x_b, nb, qkv, ctx, n1, n2, wo, wq, wk, wv, *grads, u, *keeps)
 
 
 def route_rows(info, base, expert):
@@ -347,8 +363,8 @@
 
 
 def expert_bwd_kernel(capacity, loads, u_h, w1_h, w2_h, w3_h,
-                      g1, g2, g3, p0, p1, p2, p3,
-                      rows, info, us, w1s, w2s, w3s, slots, gates, du_all, d_out, hid, da1, da3, o1, o2, o3, acc, rsem, wsem, sems, psem):
+                      g1, g2, g3, p0, p1, p2, p3, s_hid, s_da1, s_da3, s_do,
+                      rows, info, us, w1s, w2s, w3s, slots, gates, du_all, d_out, hid, da1, da3, o1, o2, o3, acc, rsem, wsem, sems, psem, ksem):
     e = pl.program_id(0)
     count = pl.num_programs(0)
     me = lax.axis_index('expert')
@@ -397,21 +413,32 @@
         da1[:, part] = (grad_hid * pre3 * sigma * (1.0 + pre1 * (1.0 - sigma))).astype(BF)
         da3[:, part] = (grad_hid * silu).astype(BF)
 
-    @pl.when(e >= 2)
+    keeps = [pltpu.make_async_copy(src, dst, ksem.at[i]) for i, (src, dst) in enumerate(((hid, s_hid), (da1, s_da1), (da3, s_da3), (d_out, s_do)))]
+
+    @pl.when((e >= 2) & (e < count - 1))
     def _():
         wait_all(flush(e - 2))
 
-    fresh = flush(e)
-    for m in range(ff // 256):
-        part = slice(m * 256, (m + 1) * 256)
-        o2[slot_e, part] = tn(hid[:, part], dov)
-    fresh[1].start()
-    for m in range(model // 256):
-        part = slice(m * 256, (m + 1) * 256)
-        o1[slot_e, part] = tn(u[:, part], da1[...])
-        o3[slot_e, part] = tn(u[:, part], da3[...])
-    fresh[0].start()
-    fresh[2].start()
+    @pl.when(e < count - 1)
+    def _():
+        fresh = flush(e)
+        for m in range(ff // 256):
+            part = slice(m * 256, (m + 1) * 256)
+            o2[slot_e, part] = tn(hid[:, part], d_out[...])
+        fresh[1].start()
+        for m in range(model // 256):
+            part = slice(m * 256, (m + 1) * 256)
+            o1[slot_e, part] = tn(u[:, part], da1[...])
+        fresh[0].start()
+        for m in range(model // 256):
+            part = slice(m * 256, (m + 1) * 256)
+            o3[slot_e, part] = tn(u[:, part], da3[...])
+        fresh[2].start()
+
+    @pl.when(e == count - 1)
+    def _():
+        start_all(keeps)
+
     for n in range(model // 256):
         part = slice(n * 256, (n + 1) * 256)
         stash(du_all, q, capacity, part, nt(da1[...], w1[part]) + nt(da3[...], w3[part]))
@@ -424,8 +451,9 @@
     def _():
         sends = [pltpu.make_async_copy(acc.at[pl.ds(pl.multiple_of(p * tokens, tokens), tokens)], ref, psem.at[r]) for r, (p, ref) in enumerate(zip(order, (p0, p1, p2, p3)))]
         start_all(sends)
+        wait_all(keeps)
+        wait_all(flush(e - 2))
         wait_all(flush(e - 1))
-        wait_all(flush(e))
         wait_all(sends)
 
 
@@ -435,13 +463,14 @@
     ff = w1.shape[2]
     ring = 3
     hb = pl.BlockSpec(memory_space=pl.ANY)
+    keep = jax.ShapeDtypeStruct((cols, ff), BF)
     part = jax.ShapeDtypeStruct((tokens, model), F32)
     return pl.pallas_call(
         functools.partial(expert_bwd_kernel, cols // 4),
         grid=(count,),
-        out_shape=(jax.ShapeDtypeStruct((count, model, ff), F32), jax.ShapeDtypeStruct((count, ff, model), F32), jax.ShapeDtypeStruct((count, model, ff), F32), part, part, part, part),
+        out_shape=(jax.ShapeDtypeStruct((count, model, ff), F32), jax.ShapeDtypeStruct((count, ff, model), F32), jax.ShapeDtypeStruct((count, model, ff), F32), part, part, part, part, keep, keep, keep, jax.ShapeDtypeStruct((cols, model), BF)),
         in_specs=[hb] * 5,
-        out_specs=(hb,) * 7,
+        out_specs=(hb,) * 11,
         scratch_shapes=[
             pltpu.VMEM((4 * tokens, model), BF), pltpu.VMEM((4, loads.shape[1] - tokens, 3 * tokens), BF),
             pltpu.VMEM((ring, cols, model), BF), pltpu.VMEM((ring, model, ff), BF), pltpu.VMEM((ring, ff, model), BF), pltpu.VMEM((ring, model, ff), BF),
@@ -449,7 +478,7 @@
             pltpu.VMEM((cols, model), BF), pltpu.VMEM((cols, ff), BF), pltpu.VMEM((cols, ff), BF), pltpu.VMEM((cols, ff), BF),
             pltpu.VMEM((2, model, ff), F32), pltpu.VMEM((2, ff, model), F32), pltpu.VMEM((2, model, ff), F32),
             pltpu.VMEM((4 * tokens, model), F32),
-            pltpu.SemaphoreType.DMA((8,)), pltpu.SemaphoreType.DMA((ring, 4)), pltpu.SemaphoreType.DMA((2, 3)), pltpu.SemaphoreType.DMA((4,)),
+            pltpu.SemaphoreType.DMA((8,)), pltpu.SemaphoreType.DMA((ring, 4)), pltpu.SemaphoreType.DMA((2, 3)), pltpu.SemaphoreType.DMA((4,)), pltpu.SemaphoreType.DMA((4,)),
         ],
         compiler_params=pltpu.CompilerParams(vmem_limit_bytes=VMEM_BYTES, dimension_semantics=("arbitrary",)),
         cost_estimate=pl.CostEstimate(flops=50 * 10 ** 9, bytes_accessed=150 * 10 ** 6, transcendentals=0),
@@ -577,10 +606,10 @@
         fields = [a.T for a in (eid_a, slot_a, gate_a, eid_b, slot_b, gate_b)]
         h_a, u_a, h_b, nb, qkv_b, ctx_b, loads = attn_fwd(x_a, x_b, dy_b, fields, norm_1, norm_2, wq_t, wk_t, wv_t, wo, kv_heads, reps, dim)
         us = (u_a, hop(u_a, 1), hop(u_a, 2), hop(u_a, 3))
-        g1, g2, g3, *sums = expert_bwd(loads, u_b, w_1, w_2, w_3, x_a.shape[0])
-        du, mine_a, out_a = expert_fwd(us, loads, sums, w_1, w_2, w_3, u_b.shape[1] // group)
+        g1, g2, g3, *rest = expert_bwd(loads, u_b, w_1, w_2, w_3, x_a.shape[0])
+        du, mine_a, out_a = expert_fwd(us, loads, rest[0:4], w_1, w_2, w_3, u_b.shape[1] // group)
         far_a = hop(out_a, 2)
-        dx_b, g_q, g_k, g_v, g_o, g_n1, g_n2 = attn_bwd(du, dy_b, h_b, x_b, nb, qkv_b, ctx_b, norm_1, norm_2, wo, wq_t, wk_t, wv_t, kv_heads, reps, dim)
+        dx_b, g_q, g_k, g_v, g_o, g_n1, g_n2, g1, g2, g3 = attn_bwd(du, dy_b, h_b, x_b, nb, qkv_b, ctx_b, norm_1, norm_2, wo, wq_t, wk_t, wv_t, (g1, g2, g3), u_b, rest[4:8], kv_heads, reps, dim)
         y_a = (h_a.astype(F32) + (mine_a + far_a)).astype(BF)
         g_q = g_q.reshape(heads, dim, model).transpose(2, 0, 1)
         g_k = g_k.reshape(kv_heads, dim, model).transpose(2, 0, 1)

time: 124 us -> 120 us (0.968)
  waiting for transfers between devices: 4.12 us -> 1.14 us
    pallas_call x1, Pallas kernels: 54.8 us -> 51.1 us  [expert_bwd(): pl.pallas_call(functools.partial(expert_bwd_kernel, cols // 4), grid=(cou...]
    ppermute x4, waiting for transfers between devices: 4.12 us -> 1.14 us  [hop(): return lax.ppermute(value, 'expert', [(i, i ^ bits) for i in range(group)])]
    pallas_call x1, Pallas kernels: 15.2 us -> 18.2 us  [attn_bwd(): pl.pallas_call(functools.partial(attn_bwd_kernel, kv_heads, reps, dim), o...]
  transfers between devices with their start and end apart: 4 -> 4, of which waited for: 1 -> 1; matrix products, arithmetic and copies ran while one was open for 0% -> 0% of each run, Pallas kernels for 57% -> 58%
where the time goes in v7:
time: 120 us
  Pallas kernels  115 us (96%)
  starting transfers between devices  2.51 us (2%)
    pallas_call x1, Pallas kernels, expert_bwd(): pl.pallas_call(functools.partial(expert_bwd_kernel, cols // 4), grid=(cou...  51.1 us
    pallas_call x1, Pallas kernels, expert_fwd(): pl.pallas_call(functools.partial(expert_fwd_kernel, capacity), grid=(coun...  28.3 us
    pallas_call x1, Pallas kernels, attn_bwd(): pl.pallas_call(functools.partial(attn_bwd_kernel, kv_heads, reps, dim), o...  18.2 us
    pallas_call x1, Pallas kernels, attn_fwd(): pl.pallas_call(functools.partial(attn_fwd_kernel, kv_heads, reps, dim), o...  17.1 us
    ppermute x4, starting transfers between devices, hop(): return lax.ppermute(value, 'expert', [(i, i ^ bits) for i in range(group)])  2.51 us
  transfers between devices with their start and end apart: 4, of which 1 were waited for; matrix products, arithmetic and copies ran while one was open for 0% of the time, Pallas kernels for 58%

profile of v7, /device:TPU:0, one launch (start us, length us, event | category | flops | bytes accessed | tf_op | source)
XLA Modules:
  0.0 119.9 jit_solution(10861412649676268737)
XLA Ops:
  0.6 17.1 %attn_fwd.1 = (bf16[128,1536]{1,0:T(8,128)(2,1)}, bf16[128,1536]{1,0:T(8,128)(2,1)}, bf16[128,1536]{1,0:T(8,128)(2,1)}, bf16[128,1536]{1,0:T(8,128)(2,1)}, bf16[...) custom-call(bf16[128,1536]{1,0:T(8,128)(2,1)} %xa_h.1, bf16[128,1536]{1,0:T(8,128)(2,1)} %x_b.1, ...), custom_call_target="tpu_custom_call" | custom-call | flops 10000000000 | bytes 14000000 | tf_op jit(solution)/shard_map/attn_fwd/pallas_call | solution.py:166
  17.8 0.7 collective-permute-start.2
  18.4 1.4 %collective-permute-start.1 = (bf16[128,1536]{1,0:T(8,128)(2,1)}, bf16[128,1536]{1,0:T(8,128)(2,1)}, u32[]{:S(2)}, u32[]{:S(2)}) collective-permute-start(bf16[128,1536]{1,0:T(8,128)(2,1)} %get-tuple-element.43.u0), channel_id=1, source_target_pairs={{0,2},{1,3},{2,0},{3,1},{4,6},{5,7},{6,4},{7,5}} | collective-permute-start | bytes 1179656 | tf_op jit(solution)/shard_map/ppermute | solution.py:598
  19.8 0.0 collective-permute-start
  19.8 51.1 %expert_bwd.1 = (f32[10,1536,512]{2,1,0:T(8,128)}, f32[10,512,1536]{2,1,0:T(8,128)}, f32[10,1536,512]{2,1,0:T(8,128)}, f32[128,1536]{1,0:T(8,128)}, f32[128,1536...) custom-call(bf16[4,144,1536]{2,1,0:T(8,128)(2,1)} %get-tuple-element, ...), custom_call_target="tpu_custom_call" | custom-call | flops 49999998976 | bytes 150000000 | tf_op jit(solution)/shard_map/expert_bwd/pallas_call | solution.py:468
  70.9 0.0 collective-permute-done.2.u3
  70.9 0.0 collective-permute-done.1.u2
  70.9 0.0 collective-permute-done.u1
  70.9 28.3 %expert_fwd.1 = (bf16[128,1536]{1,0:T(8,128)(2,1)}, f32[128,1536]{1,0:T(8,128)}, f32[128,1536]{1,0:T(8,128)}) custom-call(bf16[128,1536]{1,0:T(8,128)(2,1)} %get-tuple-element.43.u0, bf16[128,1536]{1,0:T(8,128)(2,1)} %collective-permute-done.u1, bf16[128,1536]{1,0:T(8,128)(2,1)} %collective-permute-done.1.u2, bf16[128,1536]{1,0:T(8,128)(2,1)} %collective-permute-done.2.u3, ...), custom_call_target="tpu_custom_call" | custom-call | flops 16000000000 | bytes 50000000 | tf_op jit(solution)/shard_map/expert_fwd/pallas_call | solution.py:575
  99.2 0.5 collective-permute-start.3
  99.7 0.0 copy-start
  99.7 0.0 copy-start.1
  99.7 18.2 %attn_bwd.1 = (bf16[128,1536]{1,0:T(8,128)(2,1)}, f32[1536,1536]{1,0:T(8,128)}, f32[512,1536]{1,0:T(8,128)}, f32[512,1536]{1,0:T(8,128)}, f32[1536,1536]{1,0:T(8...) custom-call(bf16[128,1536]{1,0:T(8,128)(2,1)} %get-tuple-element.51., ...), custom_call_target="tpu_custom_call", output_to_operand_aliasing={{7}: (13, {}), {8}: (14, {}), {9}: (15, {})} | custom-call | flops 14000000000 | bytes 40000000 | tf_op jit(solution)/shard_map/attn_bwd/pallas_call | solution.py:269
  117.9 1.1 collective-permute-done.3
  119.0 0.0 copy-done
  119.0 0.0 copy-done.1
  119.0 0.9 add_convert_fusion
Async XLA Ops:
  17.8 53.1 %collective-permute-start.2 = (bf16[128,1536]{1,0:T(8,128)(2,1)}, bf16[128,1536]{1,0:T(8,128)(2,1)}, u32[]{:S(2)}, u32[]{:S(2)}) collective-permute-start(bf16[128,1536]{1,0:T(8,128)(2,1)} %get-tuple-element.43.u0), channel_id=1, source_target_pairs={{0,3},{1,2},{2,1},{3,0},{4,7},{5,6},{6,5},{7,4}} | collective-permute-start | bytes 1179656 | tf_op jit(solution)/shard_map/ppermute | solution.py:598
  18.4 52.5 %collective-permute-start.1 = (bf16[128,1536]{1,0:T(8,128)(2,1)}, bf16[128,1536]{1,0:T(8,128)(2,1)}, u32[]{:S(2)}, u32[]{:S(2)}) collective-permute-start(bf16[128,1536]{1,0:T(8,128)(2,1)} %get-tuple-element.43.u0), channel_id=1, source_target_pairs={{0,2},{1,3},{2,0},{3,1},{4,6},{5,7},{6,4},{7,5}} | collective-permute-start | bytes 1179656 | tf_op jit(solution)/shard_map/ppermute | solution.py:598
  19.8 51.1 %collective-permute-start = (bf16[128,1536]{1,0:T(8,128)(2,1)}, bf16[128,1536]{1,0:T(8,128)(2,1)}, u32[]{:S(2)}, u32[]{:S(2)}) collective-permute-start(bf16[128,1536]{1,0:T(8,128)(2,1)} %get-tuple-element.43.u0), channel_id=1, source_target_pairs={{0,1},{1,0},{2,3},{3,2},{4,5},{5,4},{6,7},{7,6}} | collective-permute-start | bytes 1179656 | tf_op jit(solution)/shard_map/ppermute | solution.py:598
  99.2 19.8 %collective-permute-start.3 = (f32[128,1536]{1,0:T(8,128)}, f32[128,1536]{1,0:T(8,128)S(1)}, u32[]{:S(2)}, u32[]{:S(2)}) collective-permute-start(f32[128,1536]{1,0:T(8,128)} %get-tuple-element.50), channel_id=1, source_target_pairs={{0,2},{1,3},{2,0},{3,1},{4,6},{5,7},{6,4},{7,5}} | collective-permute-start | bytes 2359304 | tf_op jit(solution)/shard_map/ppermute | solution.py:598
  99.7 19.3 %copy-start = (f32[128,1536]{1,0:T(8,128)S(1)}, f32[128,1536]{1,0:T(8,128)}, u32[]{:S(2)}) copy-start(f32[128,1536]{1,0:T(8,128)} %get-tuple-element.49) | copy-start | bytes 2359300
  99.7 19.3 %copy-start.1 = (bf16[128,1536]{1,0:T(8,128)(2,1)S(1)}, bf16[128,1536]{1,0:T(8,128)(2,1)}, u32[]{:S(2)}) copy-start(bf16[128,1536]{1,0:T(8,128)(2,1)} %get-tuple-element.42) | copy-start | bytes 1179652

commit v8 on v7

--- a/solution.py
+++ b/solution.py
@@ -184,11 +184,11 @@
     )(x_a, x_b, dy, *fields, n1, n2, wq, wk, wv, wo)
 
 
-def attn_bwd_kernel(kv_heads, reps, dim, du_in, dy, h_b, x_b, nb, qkv, ctx, n1, n2, wo_h, wq_h, wk_h, wv_h, g1_in, g2_in, g3_in, u_h, hid_h, da1_h, da3_h, do_h,
+def attn_bwd_kernel(kv_heads, reps, dim, du_in, dy, h_b, x_b, nb, qkv, ctx, n1, n2, wo_h, wq_h, wk_h, wv_h, g1_in, g2_in, g3_in, u_h, hid_h, da1_h, da3_h, do_h, hid2_h, do2_h,
                     dx, gq, gk, gv, go, gn1, gn2, g1, g2, g3,
-                    wo, wq, wk, wv, oq, ok, ov, oo, dctx, dq, dk, dv, u, hid, da1, da3, d_out, o1, o2, o3, sems, osems, esems):
+                    wo, wq, wk, wv, oq, ok, ov, oo, dctx, dq, dk, dv, u, hid, da1, da3, d_out, hid2, d_out2, o1, o2, o3, o2b, sems, osems, esems):
     last = u_h.shape[0] - 1
-    extra = [pltpu.make_async_copy(s, d, esems.at[i]) for i, (s, d) in enumerate(((do_h, d_out), (hid_h, hid), (u_h.at[last], u), (da1_h, da1), (da3_h, da3)))]
+    extra = [pltpu.make_async_copy(s, d, esems.at[i]) for i, (s, d) in enumerate(((do_h, d_out), (hid_h, hid), (u_h.at[last], u), (da1_h, da1), (da3_h, da3), (hid2_h, hid2), (do2_h, d_out2)))]
     start_all(extra)
     copies = [pltpu.make_async_copy(s, d, sems.at[i]) for i, (s, d) in enumerate(((wo_h, wo), (wq_h, wq), (wk_h, wk), (wv_h, wv)))]
     start_all(copies, 1)
@@ -206,10 +206,11 @@
         outs.append(c)
 
     wait_all(extra)
-    for m in range(hid.shape[1] // 256):
-        part = slice(m * 256, (m + 1) * 256)
-        o2[part] = tn(hid[:, part], d_out[...])
-    flush(o2, g2.at[last])
+    for acts, cots, grad, which in ((hid, d_out, o2, last), (hid2, d_out2, o2b, last - 1)):
+        for m in range(hid.shape[1] // 256):
+            part = slice(m * 256, (m + 1) * 256)
+            grad[part] = tn(acts[:, part], cots[...])
+        flush(grad, g2.at[which])
     for grad, cot, dst in ((o1, da1, g1), (o3, da3, g3)):
         for m in range(u.shape[1] // 256):
             part = slice(m * 256, (m + 1) * 256)
@@ -263,7 +264,7 @@
     q_dim, kv_dim = kv_heads * reps * dim, kv_heads * dim
     vm = pl.BlockSpec(memory_space=pltpu.VMEM)
     hb = pl.BlockSpec(memory_space=pl.ANY)
-    n_out = 4 + kv_heads // 2 + 2 + 3
+    n_out = 4 + kv_heads // 2 + 2 + 4
     cols, ff = keeps[0].shape
     kept = pltpu.VMEM((cols, ff), BF)
     return pl.pallas_call(
@@ -272,15 +273,16 @@
             jax.ShapeDtypeStruct((tokens, model), BF), jax.ShapeDtypeStruct((q_dim, model), F32), jax.ShapeDtypeStruct((kv_dim, model), F32),
             jax.ShapeDtypeStruct((kv_dim, model), F32), jax.ShapeDtypeStruct((q_dim, model), F32), jax.ShapeDtypeStruct((1, model), F32), jax.ShapeDtypeStruct((1, model), F32),
         ) + tuple(jax.ShapeDtypeStruct(g.shape, F32) for g in grads),
-        in_specs=[vm] * 9 + [hb] * 12,
+        in_specs=[vm] * 9 + [hb] * 14,
         out_specs=(vm, hb, hb, hb, hb, vm, vm, hb, hb, hb),
         input_output_aliases={13: 7, 14: 8, 15: 9},
         scratch_shapes=[
             pltpu.VMEM((q_dim, model), BF), pltpu.VMEM((q_dim, model), BF), pltpu.VMEM((kv_dim, model), BF), pltpu.VMEM((kv_dim, model), BF),
             pltpu.VMEM((q_dim, model), F32), pltpu.VMEM((kv_dim, model), F32), pltpu.VMEM((kv_dim, model), F32), pltpu.VMEM((q_dim, model), F32),
             pltpu.VMEM((q_dim, tokens), BF), pltpu.VMEM((q_dim, tokens), BF), pltpu.VMEM((kv_dim, tokens), BF), pltpu.VMEM((kv_dim, tokens), BF),
-            pltpu.VMEM((cols, model), BF), kept, kept, kept, pltpu.VMEM((cols, model), BF), pltpu.VMEM((model, ff), F32), pltpu.VMEM((ff, model), F32), pltpu.VMEM((model, ff), F32),
-            pltpu.SemaphoreType.DMA((4,)), pltpu.SemaphoreType.DMA((n_out,)), pltpu.SemaphoreType.DMA((5,)),
+            pltpu.VMEM((cols, model), BF), kept, kept, kept, pltpu.VMEM((cols, model), BF), kept, pltpu.VMEM((cols, model), BF),
+            pltpu.VMEM((model, ff), F32), pltpu.VMEM((ff, model), F32), pltpu.VMEM((model, ff), F32), pltpu.VMEM((ff, model), F32),
+            pltpu.SemaphoreType.DMA((4,)), pltpu.SemaphoreType.DMA((n_out,)), pltpu.SemaphoreType.DMA((7,)),
         ],
         compiler_params=pltpu.CompilerParams(vmem_limit_bytes=60 * 1024 * 1024),
         cost_estimate=pl.CostEstimate(flops=14 * 10 ** 9, bytes_accessed=40 * 10 ** 6, transcendentals=0),
@@ -346,10 +348,10 @@
         outs[r, pl.ds(pl.multiple_of(q * BLOCK, BLOCK), capacity), lanes] = res[r * capacity:(r + 1) * capacity].astype(BF)
 
 
-def mix_into(acc, outs, slots, gates, q, weighted):
+def mix_into(acc, outs, slots, gates, q, weighted, order=(0, 1, 2, 3), after=lambda r: None):
     tokens = acc.shape[0] // outs.shape[0]
     depth = lax.broadcasted_iota(jnp.int32, (BLOCK, tokens), 0).astype(F32)
-    for r in range(outs.shape[0]):
+    for r in order:
         lanes = slice(r * tokens, (r + 1) * tokens)
         blocks = []
         for k in range(QUAD):
@@ -360,10 +362,11 @@
         for n in range(acc.shape[1] // 512):
             part = slice(n * 512, (n + 1) * 512)
             acc[lanes, part] += nn(pick, outs[r, :, part])
+        after(r)
 
 
 def expert_bwd_kernel(capacity, loads, u_h, w1_h, w2_h, w3_h,
-                      g1, g2, g3, p0, p1, p2, p3, s_hid, s_da1, s_da3, s_do,
+                      g1, g2, g3, p0, p1, p2, p3, s_hid, s_da1, s_da3, s_do, s_hid2, s_do2,
                       rows, info, us, w1s, w2s, w3s, slots, gates, du_all, d_out, hid, da1, da3, o1, o2, o3, acc, rsem, wsem, sems, psem, ksem):
     e = pl.program_id(0)
     count = pl.num_programs(0)
@@ -388,6 +391,12 @@
         start_all(ring_copies(pairs, wsem, e + 2, ring))
 
     slot_row, gate_row = route_rows(info, 1, me * count + e)
+    early = [pltpu.make_async_copy(src, dst, ksem.at[4 + i]) for i, (src, dst) in enumerate(((hid, s_hid2), (d_out, s_do2)))]
+
+    @pl.when(e == count - 1)
+    def _():
+        wait_all(early)
+
     q = lax.rem(e, QUAD)
     keep_routes(slots, gates, q, slot_row, gate_row)
     hot = hits(slot_row, tokens, capacity)
@@ -422,10 +431,18 @@
     @pl.when(e < count - 1)
     def _():
         fresh = flush(e)
-        for m in range(ff // 256):
-            part = slice(m * 256, (m + 1) * 256)
-            o2[slot_e, part] = tn(hid[:, part], d_out[...])
-        fresh[1].start()
+
+        @pl.when(e < count - 2)
+        def _():
+            for m in range(ff // 256):
+                part = slice(m * 256, (m + 1) * 256)
+                o2[slot_e, part] = tn(hid[:, part], d_out[...])
+            fresh[1].start()
+
+        @pl.when(e == count - 2)
+        def _():
+            start_all(early)
+
         for m in range(model // 256):
             part = slice(m * 256, (m + 1) * 256)
             o1[slot_e, part] = tn(u[:, part], da1[...])
@@ -453,7 +470,7 @@
         start_all(sends)
         wait_all(keeps)
         wait_all(flush(e - 2))
-        wait_all(flush(e - 1))
+        wait_all(flush(e - 1)[0:3:2])
         wait_all(sends)
 
 
@@ -463,14 +480,14 @@
     ff = w1.shape[2]
     ring = 3
     hb = pl.BlockSpec(memory_space=pl.ANY)
-    keep = jax.ShapeDtypeStruct((cols, ff), BF)
+    keep, keep_do = jax.ShapeDtypeStruct((cols, ff), BF), jax.ShapeDtypeStruct((cols, model), BF)
     part = jax.ShapeDtypeStruct((tokens, model), F32)
     return pl.pallas_call(
         functools.partial(expert_bwd_kernel, cols // 4),
         grid=(count,),
-        out_shape=(jax.ShapeDtypeStruct((count, model, ff), F32), jax.ShapeDtypeStruct((count, ff, model), F32), jax.ShapeDtypeStruct((count, model, ff), F32), part, part, part, part, keep, keep, keep, jax.ShapeDtypeStruct((cols, model), BF)),
+        out_shape=(jax.ShapeDtypeStruct((count, model, ff), F32), jax.ShapeDtypeStruct((count, ff, model), F32), jax.ShapeDtypeStruct((count, model, ff), F32), part, part, part, part, keep, keep, keep, keep_do, keep, keep_do),
         in_specs=[hb] * 5,
-        out_specs=(hb,) * 11,
+        out_specs=(hb,) * 13,
         scratch_shapes=[
             pltpu.VMEM((4 * tokens, model), BF), pltpu.VMEM((4, loads.shape[1] - tokens, 3 * tokens), BF),
             pltpu.VMEM((ring, cols, model), BF), pltpu.VMEM((ring, model, ff), BF), pltpu.VMEM((ring, ff, model), BF), pltpu.VMEM((ring, model, ff), BF),
@@ -478,7 +495,7 @@
             pltpu.VMEM((cols, model), BF), pltpu.VMEM((cols, ff), BF), pltpu.VMEM((cols, ff), BF), pltpu.VMEM((cols, ff), BF),
             pltpu.VMEM((2, model, ff), F32), pltpu.VMEM((2, ff, model), F32), pltpu.VMEM((2, model, ff), F32),
             pltpu.VMEM((4 * tokens, model), F32),
-            pltpu.SemaphoreType.DMA((8,)), pltpu.SemaphoreType.DMA((ring, 4)), pltpu.SemaphoreType.DMA((2, 3)), pltpu.SemaphoreType.DMA((4,)), pltpu.SemaphoreType.DMA((4,)),
+            pltpu.SemaphoreType.DMA((8,)), pltpu.SemaphoreType.DMA((ring, 4)), pltpu.SemaphoreType.DMA((2, 3)), pltpu.SemaphoreType.DMA((4,)), pltpu.SemaphoreType.DMA((6,)),
         ],
         compiler_params=pltpu.CompilerParams(vmem_limit_bytes=VMEM_BYTES, dimension_semantics=("arbitrary",)),
         cost_estimate=pl.CostEstimate(flops=50 * 10 ** 9, bytes_accessed=150 * 10 ** 6, transcendentals=0),
@@ -487,7 +504,7 @@
 
 
 def expert_fwd_kernel(capacity, u0, u1, u2, u3, loads, b0, b1, b2, b3, w1_h, w2_h, w3_h, du_o, mine_o, out_o,
-                      rows, info, w1s, w2s, w3s, slots, gates, out_all, acc, loc0, loc2, rx1, rx3, rxf, ra1, ra3, rsem, wsem, bsem, ssem, xsem):
+                      rows, info, w1s, w2s, w3s, slots, gates, out_all, acc, loc0, loc2, rx1, rx3, rxf, ra1, ra3, dus, rsem, wsem, bsem, ssem, xsem, osem):
     e = pl.program_id(0)
     count = pl.num_programs(0)
     me = lax.axis_index('expert')
@@ -544,25 +561,26 @@
         lanes = slice(n * 256, (n + 1) * 256)
         stash(out_all, q, capacity, lanes, nn(hidden, w2[:, lanes]))
 
-    @pl.when((q == QUAD - 1) | (e == count - 1))
+    @pl.when((q == QUAD - 1) & (e < count - 1))
     def _():
         mix_into(acc, out_all, slots, gates, q, True)
 
     @pl.when(e == count - 1)
     def _():
-        late3.start()
-        late1.start()
+        late = {3: late3, 1: late1}
+        mix_into(acc, out_all, slots, gates, q, True, (3, 1, 2, 0), lambda r: late[r].start() if r in late else None)
+        moves = [pltpu.make_async_copy(src, dst, osem.at[i]) for i, (src, dst) in enumerate(((dus, du_o), (loc2, out_o), (loc0, mine_o)))]
         swap1.wait()
         over.wait()
-        du_o[...] = ((loc0[...] + rx1[...]) + rxf[...]).astype(BF)
+        dus[...] = ((loc0[...] + rx1[...]) + rxf[...]).astype(BF)
+        moves[0].start()
         late3.wait()
-        out_o[...] = acc[part[2]] + ra3[...]
+        loc2[...] = acc[part[2]] + ra3[...]
+        moves[1].start()
         late1.wait()
-        mine_o[...] = acc[part[0]] + ra1[...]
-
-
-def whole(shape):
-    return pl.BlockSpec(shape, lambda e: (0,) * len(shape), pipeline_mode=pl.Buffered(1))
+        loc0[...] = acc[part[0]] + ra1[...]
+        moves[2].start()
+        wait_all(moves)
 
 
 def expert_fwd(us, loads, sums, w1, w2, w3, capacity):
@@ -577,13 +595,13 @@
         grid=(count,),
         out_shape=(jax.ShapeDtypeStruct((tokens, model), BF), part, part),
         in_specs=[hb] * 12,
-        out_specs=(whole((tokens, model)),) * 3,
+        out_specs=(hb,) * 3,
         scratch_shapes=[
             pltpu.VMEM((4 * tokens, model), BF), pltpu.VMEM((4, loads.shape[1] - tokens, 3 * tokens), BF),
             pltpu.VMEM((ring, model, ff), BF), pltpu.VMEM((ring, ff, model), BF), pltpu.VMEM((ring, model, ff), BF),
             pltpu.VMEM((8, 4 * tokens), F32), pltpu.VMEM((8, 4 * tokens), F32), pltpu.VMEM((4, QUAD * BLOCK, model), BF), pltpu.VMEM((4 * tokens, model), F32),
-            tile, tile, tile, tile, tile, tile, tile,
-            pltpu.SemaphoreType.DMA((8,)), pltpu.SemaphoreType.DMA((ring, 3)), pltpu.SemaphoreType.DMA((2,)), pltpu.SemaphoreType.DMA((5,)), pltpu.SemaphoreType.DMA((5,)),
+            tile, tile, tile, tile, tile, tile, tile, pltpu.VMEM((tokens, model), BF),
+            pltpu.SemaphoreType.DMA((8,)), pltpu.SemaphoreType.DMA((ring, 3)), pltpu.SemaphoreType.DMA((2,)), pltpu.SemaphoreType.DMA((5,)), pltpu.SemaphoreType.DMA((5,)), pltpu.SemaphoreType.DMA((3,)),
         ],
         compiler_params=pltpu.CompilerParams(vmem_limit_bytes=VMEM_BYTES, dimension_semantics=("arbitrary",), collective_id=1, has_side_effects=True),
         cost_estimate=pl.CostEstimate(flops=16 * 10 ** 9, bytes_accessed=50 * 10 ** 6, transcendentals=0),
@@ -609,7 +627,7 @@
         g1, g2, g3, *rest = expert_bwd(loads, u_b, w_1, w_2, w_3, x_a.shape[0])
         du, mine_a, out_a = expert_fwd(us, loads, rest[0:4], w_1, w_2, w_3, u_b.shape[1] // group)
         far_a = hop(out_a, 2)
-        dx_b, g_q, g_k, g_v, g_o, g_n1, g_n2, g1, g2, g3 = attn_bwd(du, dy_b, h_b, x_b, nb, qkv_b, ctx_b, norm_1, norm_2, wo, wq_t, wk_t, wv_t, (g1, g2, g3), u_b, rest[4:8], kv_heads, reps, dim)
+        dx_b, g_q, g_k, g_v, g_o, g_n1, g_n2, g1, g2, g3 = attn_bwd(du, dy_b, h_b, x_b, nb, qkv_b, ctx_b, norm_1, norm_2, wo, wq_t, wk_t, wv_t, (g1, g2, g3), u_b, rest[4:10], kv_heads, reps, dim)
         y_a = (h_a.astype(F32) + (mine_a + far_a)).astype(BF)
         g_q = g_q.reshape(heads, dim, model).transpose(2, 0, 1)
         g_k = g_k.reshape(kv_heads, dim, model).transpose(2, 0, 1)

time: 120 us -> 121 us (level)
    pallas_call x1, Pallas kernels: 51.1 us -> 52.4 us  [expert_bwd(): pl.pallas_call(functools.partial(expert_bwd_kernel, cols // 4), grid=(cou...]
    pallas_call x1, Pallas kernels: 18.2 us -> 19.4 us  [attn_bwd(): pl.pallas_call(functools.partial(attn_bwd_kernel, kv_heads, reps, dim), o...]
  transfers between devices with their start and end apart: 4 -> 4, of which waited for: 1 -> 0; matrix products, arithmetic and copies ran while one was open for 0% -> 0% of each run, Pallas kernels for 58% -> 60%
where the time goes in v8:
time: 121 us
  Pallas kernels  116 us (96%)
  starting transfers between devices  2.51 us (2%)
    pallas_call x1, Pallas kernels, expert_bwd(): pl.pallas_call(functools.partial(expert_bwd_kernel, cols // 4), grid=(cou...  52.4 us
    pallas_call x1, Pallas kernels, expert_fwd(): pl.pallas_call(functools.partial(expert_fwd_kernel, capacity), grid=(coun...  27.5 us
    pallas_call x1, Pallas kernels, attn_bwd(): pl.pallas_call(functools.partial(attn_bwd_kernel, kv_heads, reps, dim), o...  19.4 us
    pallas_call x1, Pallas kernels, attn_fwd(): pl.pallas_call(functools.partial(attn_fwd_kernel, kv_heads, reps, dim), o...  17.1 us
    ppermute x4, starting transfers between devices, hop(): return lax.ppermute(value, 'expert', [(i, i ^ bits) for i in range(group)])  2.51 us
  transfers between devices with their start and end apart: 4, of which 0 were waited for; matrix products, arithmetic and copies ran while one was open for 0% of the time, Pallas kernels for 60%

profile of v8, /device:TPU:0, one launch (start us, length us, event | category | flops | bytes accessed | tf_op | source)
XLA Modules:
  0.0 120.6 jit_solution(2058073378851456069)
XLA Ops:
  0.6 17.1 %attn_fwd.1 = (bf16[128,1536]{1,0:T(8,128)(2,1)}, bf16[128,1536]{1,0:T(8,128)(2,1)}, bf16[128,1536]{1,0:T(8,128)(2,1)}, bf16[128,1536]{1,0:T(8,128)(2,1)}, bf16[...) custom-call(bf16[128,1536]{1,0:T(8,128)(2,1)} %xa_h.1, bf16[128,1536]{1,0:T(8,128)(2,1)} %x_b.1, ...), custom_call_target="tpu_custom_call" | custom-call | flops 10000000000 | bytes 14000000 | tf_op jit(solution)/shard_map/attn_fwd/pallas_call | solution.py:166
  17.8 0.7 collective-permute-start.2
  18.4 1.4 %collective-permute-start.1 = (bf16[128,1536]{1,0:T(8,128)(2,1)}, bf16[128,1536]{1,0:T(8,128)(2,1)}, u32[]{:S(2)}, u32[]{:S(2)}) collective-permute-start(bf16[128,1536]{1,0:T(8,128)(2,1)} %get-tuple-element.45.u0), channel_id=1, source_target_pairs={{0,2},{1,3},{2,0},{3,1},{4,6},{5,7},{6,4},{7,5}} | collective-permute-start | bytes 1179656 | tf_op jit(solution)/shard_map/ppermute | solution.py:616
  19.8 0.0 collective-permute-start
  19.8 52.4 %expert_bwd.1 = (f32[10,1536,512]{2,1,0:T(8,128)}, f32[10,512,1536]{2,1,0:T(8,128)}, f32[10,1536,512]{2,1,0:T(8,128)}, f32[128,1536]{1,0:T(8,128)}, f32[128,1536...) custom-call(bf16[4,144,1536]{2,1,0:T(8,128)(2,1)} %get-tuple-element, ...), custom_call_target="tpu_custom_call" | custom-call | flops 49999998976 | bytes 150000000 | tf_op jit(solution)/shard_map/expert_bwd/pallas_call | solution.py:485
  72.2 0.0 collective-permute-done.2.u3
  72.2 0.0 collective-permute-done.1.u2
  72.2 0.0 collective-permute-done.u1
  72.2 27.5 %expert_fwd.1 = (bf16[128,1536]{1,0:T(8,128)(2,1)}, f32[128,1536]{1,0:T(8,128)}, f32[128,1536]{1,0:T(8,128)}) custom-call(bf16[128,1536]{1,0:T(8,128)(2,1)} %get-tuple-element.45.u0, bf16[128,1536]{1,0:T(8,128)(2,1)} %collective-permute-done.u1, bf16[128,1536]{1,0:T(8,128)(2,1)} %collective-permute-done.1.u2, bf16[128,1536]{1,0:T(8,128)(2,1)} %collective-permute-done.2.u3, ...), custom_call_target="tpu_custom_call" | custom-call | flops 16000000000 | bytes 50000000 | tf_op jit(solution)/shard_map/expert_fwd/pallas_call | solution.py:593
  99.7 0.5 collective-permute-start.3
  100.2 0.0 copy-start
  100.2 0.0 copy-start.1
  100.2 19.4 %attn_bwd.1 = (bf16[128,1536]{1,0:T(8,128)(2,1)}, f32[1536,1536]{1,0:T(8,128)}, f32[512,1536]{1,0:T(8,128)}, f32[512,1536]{1,0:T(8,128)}, f32[1536,1536]{1,0:T(8...) custom-call(bf16[128,1536]{1,0:T(8,128)(2,1)} %get-tuple-element.53., ...), custom_call_target="tpu_custom_call", output_to_operand_aliasing={{7}: (13, {}), {8}: (14, {}), {9}: (15, {})} | custom-call | flops 14000000000 | bytes 40000000 | tf_op jit(solution)/shard_map/attn_bwd/pallas_call | solution.py:270
  119.6 0.0 collective-permute-done.3
  119.7 0.0 copy-done
  119.7 0.0 copy-done.1
  119.7 0.9 add_convert_fusion
Async XLA Ops:
  17.8 54.4 %collective-permute-start.2 = (bf16[128,1536]{1,0:T(8,128)(2,1)}, bf16[128,1536]{1,0:T(8,128)(2,1)}, u32[]{:S(2)}, u32[]{:S(2)}) collective-permute-start(bf16[128,1536]{1,0:T(8,128)(2,1)} %get-tuple-element.45.u0), channel_id=1, source_target_pairs={{0,3},{1,2},{2,1},{3,0},{4,7},{5,6},{6,5},{7,4}} | collective-permute-start | bytes 1179656 | tf_op jit(solution)/shard_map/ppermute | solution.py:616
  18.4 53.7 %collective-permute-start.1 = (bf16[128,1536]{1,0:T(8,128)(2,1)}, bf16[128,1536]{1,0:T(8,128)(2,1)}, u32[]{:S(2)}, u32[]{:S(2)}) collective-permute-start(bf16[128,1536]{1,0:T(8,128)(2,1)} %get-tuple-element.45.u0), channel_id=1, source_target_pairs={{0,2},{1,3},{2,0},{3,1},{4,6},{5,7},{6,4},{7,5}} | collective-permute-start | bytes 1179656 | tf_op jit(solution)/shard_map/ppermute | solution.py:616
  19.8 52.4 %collective-permute-start = (bf16[128,1536]{1,0:T(8,128)(2,1)}, bf16[128,1536]{1,0:T(8,128)(2,1)}, u32[]{:S(2)}, u32[]{:S(2)}) collective-permute-start(bf16[128,1536]{1,0:T(8,128)(2,1)} %get-tuple-element.45.u0), channel_id=1, source_target_pairs={{0,1},{1,0},{2,3},{3,2},{4,5},{5,4},{6,7},{7,6}} | collective-permute-start | bytes 1179656 | tf_op jit(solution)/shard_map/ppermute | solution.py:616
  99.7 19.9 %collective-permute-start.3 = (f32[128,1536]{1,0:T(8,128)}, f32[128,1536]{1,0:T(8,128)S(1)}, u32[]{:S(2)}, u32[]{:S(2)}) collective-permute-start(f32[128,1536]{1,0:T(8,128)} %get-tuple-element.52), channel_id=1, source_target_pairs={{0,2},{1,3},{2,0},{3,1},{4,6},{5,7},{6,4},{7,5}} | collective-permute-start | bytes 2359304 | tf_op jit(solution)/shard_map/ppermute | solution.py:616
  100.2 19.5 %copy-start = (f32[128,1536]{1,0:T(8,128)S(1)}, f32[128,1536]{1,0:T(8,128)}, u32[]{:S(2)}) copy-start(f32[128,1536]{1,0:T(8,128)} %get-tuple-element.51) | copy-start | bytes 2359300
  100.2 19.5 %copy-start.1 = (bf16[128,1536]{1,0:T(8,128)(2,1)S(1)}, bf16[128,1536]{1,0:T(8,128)(2,1)}, u32[]{:S(2)}) copy-start(bf16[128,1536]{1,0:T(8,128)(2,1)} %get-tuple-element.44) | copy-start | bytes 1179652

commit v9 on v7

--- a/solution.py
+++ b/solution.py
@@ -346,10 +346,10 @@
         outs[r, pl.ds(pl.multiple_of(q * BLOCK, BLOCK), capacity), lanes] = res[r * capacity:(r + 1) * capacity].astype(BF)
 
 
-def mix_into(acc, outs, slots, gates, q, weighted):
+def mix_into(acc, outs, slots, gates, q, weighted, order, after=lambda r: r):
     tokens = acc.shape[0] // outs.shape[0]
     depth = lax.broadcasted_iota(jnp.int32, (BLOCK, tokens), 0).astype(F32)
-    for r in range(outs.shape[0]):
+    for r in order:
         lanes = slice(r * tokens, (r + 1) * tokens)
         blocks = []
         for k in range(QUAD):
@@ -360,6 +360,7 @@
         for n in range(acc.shape[1] // 512):
             part = slice(n * 512, (n + 1) * 512)
             acc[lanes, part] += nn(pick, outs[r, :, part])
+        after(r)
 
 
 def expert_bwd_kernel(capacity, loads, u_h, w1_h, w2_h, w3_h,
@@ -445,7 +446,7 @@
 
     @pl.when((q == QUAD - 1) | (e == count - 1))
     def _():
-        mix_into(acc, du_all, slots, gates, q, False)
+        mix_into(acc, du_all, slots, gates, q, False, range(QUAD))
 
     @pl.when(e == count - 1)
     def _():
@@ -487,7 +488,7 @@
 
 
 def expert_fwd_kernel(capacity, u0, u1, u2, u3, loads, b0, b1, b2, b3, w1_h, w2_h, w3_h, du_o, mine_o, out_o,
-                      rows, info, w1s, w2s, w3s, slots, gates, out_all, acc, loc0, loc2, rx1, rx3, rxf, ra1, ra3, rsem, wsem, bsem, ssem, xsem):
+                      rows, info, w1s, w2s, w3s, slots, gates, out_all, acc, loc0, loc2, rx1, rx3, rxf, ra1, ra3, dus, rsem, wsem, bsem, ssem, xsem, osem):
     e = pl.program_id(0)
     count = pl.num_programs(0)
     me = lax.axis_index('expert')
@@ -544,25 +545,28 @@
         lanes = slice(n * 256, (n + 1) * 256)
         stash(out_all, q, capacity, lanes, nn(hidden, w2[:, lanes]))
 
-    @pl.when((q == QUAD - 1) | (e == count - 1))
-    def _():
-        mix_into(acc, out_all, slots, gates, q, True)
-
-    @pl.when(e == count - 1)
-    def _():
-        late3.start()
-        late1.start()
+    final = e == count - 1
+
+    @pl.when((q == QUAD - 1) & jnp.logical_not(final))
+    def _():
+        mix_into(acc, out_all, slots, gates, q, True, range(QUAD))
+
+    @pl.when(final)
+    def _():
+        late = {3: late3, 1: late1}
+        mix_into(acc, out_all, slots, gates, q, True, (3, 1, 2, 0), lambda r: late[r].start() if r in late else r)
+        to_du, to_out, to_mine = [pltpu.make_async_copy(src, dst, osem.at[i]) for i, (src, dst) in enumerate(((dus, du_o), (loc2, out_o), (loc0, mine_o)))]
         swap1.wait()
         over.wait()
-        du_o[...] = ((loc0[...] + rx1[...]) + rxf[...]).astype(BF)
+        dus[...] = ((loc0[...] + rx1[...]) + rxf[...]).astype(BF)
+        to_du.start()
         late3.wait()
-        out_o[...] = acc[part[2]] + ra3[...]
+        loc2[...] = acc[part[2]] + ra3[...]
+        to_out.start()
         late1.wait()
-        mine_o[...] = acc[part[0]] + ra1[...]
-
-
-def whole(shape):
-    return pl.BlockSpec(shape, lambda e: (0,) * len(shape), pipeline_mode=pl.Buffered(1))
+        loc0[...] = acc[part[0]] + ra1[...]
+        to_mine.start()
+        wait_all((to_du, to_out, to_mine))
 
 
 def expert_fwd(us, loads, sums, w1, w2, w3, capacity):
@@ -577,13 +581,13 @@
         grid=(count,),
         out_shape=(jax.ShapeDtypeStruct((tokens, model), BF), part, part),
         in_specs=[hb] * 12,
-        out_specs=(whole((tokens, model)),) * 3,
+        out_specs=(hb,) * 3,
         scratch_shapes=[
             pltpu.VMEM((4 * tokens, model), BF), pltpu.VMEM((4, loads.shape[1] - tokens, 3 * tokens), BF),
             pltpu.VMEM((ring, model, ff), BF), pltpu.VMEM((ring, ff, model), BF), pltpu.VMEM((ring, model, ff), BF),
             pltpu.VMEM((8, 4 * tokens), F32), pltpu.VMEM((8, 4 * tokens), F32), pltpu.VMEM((4, QUAD * BLOCK, model), BF), pltpu.VMEM((4 * tokens, model), F32),
-            tile, tile, tile, tile, tile, tile, tile,
-            pltpu.SemaphoreType.DMA((8,)), pltpu.SemaphoreType.DMA((ring, 3)), pltpu.SemaphoreType.DMA((2,)), pltpu.SemaphoreType.DMA((5,)), pltpu.SemaphoreType.DMA((5,)),
+            tile, tile, tile, tile, tile, tile, tile, pltpu.VMEM((tokens, model), BF),
+            pltpu.SemaphoreType.DMA((8,)), pltpu.SemaphoreType.DMA((ring, 3)), pltpu.SemaphoreType.DMA((2,)), pltpu.SemaphoreType.DMA((5,)), pltpu.SemaphoreType.DMA((5,)), pltpu.SemaphoreType.DMA((3,)),
         ],
         compiler_params=pltpu.CompilerParams(vmem_limit_bytes=VMEM_BYTES, dimension_semantics=("arbitrary",), collective_id=1, has_side_effects=True),
         cost_estimate=pl.CostEstimate(flops=16 * 10 ** 9, bytes_accessed=50 * 10 ** 6, transcendentals=0),

time: 120 us -> 119 us (level)
  no operation moved by 1% of the time
where the time goes in v9:
time: 119 us
  Pallas kernels  114 us (96%)
  starting transfers between devices  2.51 us (2%)
    pallas_call x1, Pallas kernels, expert_bwd(): pl.pallas_call(functools.partial(expert_bwd_kernel, cols // 4), grid=(cou...  51.1 us
    pallas_call x1, Pallas kernels, expert_fwd(): pl.pallas_call(functools.partial(expert_fwd_kernel, capacity), grid=(coun...  27.5 us
    pallas_call x1, Pallas kernels, attn_bwd(): pl.pallas_call(functools.partial(attn_bwd_kernel, kv_heads, reps, dim), o...  18.2 us
    pallas_call x1, Pallas kernels, attn_fwd(): pl.pallas_call(functools.partial(attn_fwd_kernel, kv_heads, reps, dim), o...  17.1 us
    ppermute x4, starting transfers between devices, hop(): return lax.ppermute(value, 'expert', [(i, i ^ bits) for i in range(group)])  2.51 us
  transfers between devices with their start and end apart: 4, of which 1 were waited for; matrix products, arithmetic and copies ran while one was open for 0% of the time, Pallas kernels for 58%

profile of v9, /device:TPU:0, one launch (start us, length us, event | category | flops | bytes accessed | tf_op | source)
XLA Modules:
  0.0 119.1 jit_solution(14718055748048121379)
XLA Ops:
  0.6 17.1 %attn_fwd.1 = (bf16[128,1536]{1,0:T(8,128)(2,1)}, bf16[128,1536]{1,0:T(8,128)(2,1)}, bf16[128,1536]{1,0:T(8,128)(2,1)}, bf16[128,1536]{1,0:T(8,128)(2,1)}, bf16[...) custom-call(bf16[128,1536]{1,0:T(8,128)(2,1)} %xa_h.1, bf16[128,1536]{1,0:T(8,128)(2,1)} %x_b.1, ...), custom_call_target="tpu_custom_call" | custom-call | flops 10000000000 | bytes 14000000 | tf_op jit(solution)/shard_map/attn_fwd/pallas_call | solution.py:166
  17.8 0.7 collective-permute-start.2
  18.4 1.4 %collective-permute-start.1 = (bf16[128,1536]{1,0:T(8,128)(2,1)}, bf16[128,1536]{1,0:T(8,128)(2,1)}, u32[]{:S(2)}, u32[]{:S(2)}) collective-permute-start(bf16[128,1536]{1,0:T(8,128)(2,1)} %get-tuple-element.43.u0), channel_id=1, source_target_pairs={{0,2},{1,3},{2,0},{3,1},{4,6},{5,7},{6,4},{7,5}} | collective-permute-start | bytes 1179656 | tf_op jit(solution)/shard_map/ppermute | solution.py:602
  19.8 0.0 collective-permute-start
  19.8 51.1 %expert_bwd.1 = (f32[10,1536,512]{2,1,0:T(8,128)}, f32[10,512,1536]{2,1,0:T(8,128)}, f32[10,1536,512]{2,1,0:T(8,128)}, f32[128,1536]{1,0:T(8,128)}, f32[128,1536...) custom-call(bf16[4,144,1536]{2,1,0:T(8,128)(2,1)} %get-tuple-element, ...), custom_call_target="tpu_custom_call" | custom-call | flops 49999998976 | bytes 150000000 | tf_op jit(solution)/shard_map/expert_bwd/pallas_call | solution.py:469
  70.9 0.0 collective-permute-done.2.u3
  70.9 0.0 collective-permute-done.1.u2
  70.9 0.0 collective-permute-done.u1
  70.9 27.5 %expert_fwd.1 = (bf16[128,1536]{1,0:T(8,128)(2,1)}, f32[128,1536]{1,0:T(8,128)}, f32[128,1536]{1,0:T(8,128)}) custom-call(bf16[128,1536]{1,0:T(8,128)(2,1)} %get-tuple-element.43.u0, bf16[128,1536]{1,0:T(8,128)(2,1)} %collective-permute-done.u1, bf16[128,1536]{1,0:T(8,128)(2,1)} %collective-permute-done.1.u2, bf16[128,1536]{1,0:T(8,128)(2,1)} %collective-permute-done.2.u3, ...), custom_call_target="tpu_custom_call" | custom-call | flops 16000000000 | bytes 50000000 | tf_op jit(solution)/shard_map/expert_fwd/pallas_call | solution.py:579
  98.5 0.5 collective-permute-start.3
  98.9 0.0 copy-start
  98.9 0.0 copy-start.1
  98.9 18.2 %attn_bwd.1 = (bf16[128,1536]{1,0:T(8,128)(2,1)}, f32[1536,1536]{1,0:T(8,128)}, f32[512,1536]{1,0:T(8,128)}, f32[512,1536]{1,0:T(8,128)}, f32[1536,1536]{1,0:T(8...) custom-call(bf16[128,1536]{1,0:T(8,128)(2,1)} %get-tuple-element.51., ...), custom_call_target="tpu_custom_call", output_to_operand_aliasing={{7}: (13, {}), {8}: (14, {}), {9}: (15, {})} | custom-call | flops 14000000000 | bytes 40000000 | tf_op jit(solution)/shard_map/attn_bwd/pallas_call | solution.py:269
  117.1 1.1 collective-permute-done.3
  118.3 0.0 copy-done
  118.3 0.0 copy-done.1
  118.3 0.9 add_convert_fusion
Async XLA Ops:
  17.8 53.1 %collective-permute-start.2 = (bf16[128,1536]{1,0:T(8,128)(2,1)}, bf16[128,1536]{1,0:T(8,128)(2,1)}, u32[]{:S(2)}, u32[]{:S(2)}) collective-permute-start(bf16[128,1536]{1,0:T(8,128)(2,1)} %get-tuple-element.43.u0), channel_id=1, source_target_pairs={{0,3},{1,2},{2,1},{3,0},{4,7},{5,6},{6,5},{7,4}} | collective-permute-start | bytes 1179656 | tf_op jit(solution)/shard_map/ppermute | solution.py:602
  18.4 52.5 %collective-permute-start.1 = (bf16[128,1536]{1,0:T(8,128)(2,1)}, bf16[128,1536]{1,0:T(8,128)(2,1)}, u32[]{:S(2)}, u32[]{:S(2)}) collective-permute-start(bf16[128,1536]{1,0:T(8,128)(2,1)} %get-tuple-element.43.u0), channel_id=1, source_target_pairs={{0,2},{1,3},{2,0},{3,1},{4,6},{5,7},{6,4},{7,5}} | collective-permute-start | bytes 1179656 | tf_op jit(solution)/shard_map/ppermute | solution.py:602
  19.8 51.1 %collective-permute-start = (bf16[128,1536]{1,0:T(8,128)(2,1)}, bf16[128,1536]{1,0:T(8,128)(2,1)}, u32[]{:S(2)}, u32[]{:S(2)}) collective-permute-start(bf16[128,1536]{1,0:T(8,128)(2,1)} %get-tuple-element.43.u0), channel_id=1, source_target_pairs={{0,1},{1,0},{2,3},{3,2},{4,5},{5,4},{6,7},{7,6}} | collective-permute-start | bytes 1179656 | tf_op jit(solution)/shard_map/ppermute | solution.py:602
  98.5 19.8 %collective-permute-start.3 = (f32[128,1536]{1,0:T(8,128)}, f32[128,1536]{1,0:T(8,128)S(1)}, u32[]{:S(2)}, u32[]{:S(2)}) collective-permute-start(f32[128,1536]{1,0:T(8,128)} %get-tuple-element.50), channel_id=1, source_target_pairs={{0,2},{1,3},{2,0},{3,1},{4,6},{5,7},{6,4},{7,5}} | collective-permute-start | bytes 2359304 | tf_op jit(solution)/shard_map/ppermute | solution.py:602
  98.9 19.3 %copy-start = (f32[128,1536]{1,0:T(8,128)S(1)}, f32[128,1536]{1,0:T(8,128)}, u32[]{:S(2)}) copy-start(f32[128,1536]{1,0:T(8,128)} %get-tuple-element.49) | copy-start | bytes 2359300
  98.9 19.3 %copy-start.1 = (bf16[128,1536]{1,0:T(8,128)(2,1)S(1)}, bf16[128,1536]{1,0:T(8,128)(2,1)}, u32[]{:S(2)}) copy-start(bf16[128,1536]{1,0:T(8,128)(2,1)} %get-tuple-element.42) | copy-start | bytes 1179652
